TPU v7x, 32 devices: a whole 2x2x4 slice. The times are simulated.
32 devices in a mesh: gx: 4 (over x, core), gy: 2 (over y), gz: 4 (over z).
Axes of the slice: x: 2, y: 2, z: 4, core: 2. Of those that a mesh axis runs over, the one named last changes fastest.
Arguments:
- magnetization: float32 [3, 64, 64, 512], P(None, 'gx', 'gy', 'gz'), may hold values from -1 to 1, as said below
- kernel: float32 [6, 64, 512, 64], P(None, ('gx', 'gz'), 'gy'), may hold values from -3 to 3, as said below
- applied: float32 [3], replicated, may hold values from -4 to 4
Outputs:
- predicted: float32 [3, 64, 64, 512], P(None, 'gx', 'gy', 'gz')
- torque: float32 [3, 64, 64, 512], P(None, 'gx', 'gy', 'gz')
Inputs may be any that keep to these rules, and one draw needn't show every extreme that they name: `magnetization`: each cell's three components form a vector of unit length. The tensor is even in wavenumber: kernel[c, ky, kz, kx] equals kernel[c, (64 - ky) mod 64, (512 - kz) mod 512, (64 - kx) mod 64].
All inputs are finite; a program needn't handle non-finite values.
Results may differ from a plain program's by a relative error of at most 0.00011.
Values sent between devices are 32-bit elements; how exact they have to be, the bound alone decides.
No kernel may reach another device: no remote copies, remote signals or barrier semaphores. Data moves between devices by JAX's collectives and lax.ppermute only.
A program may use at most 128 MiB of HBM per device.

v0:
```python
import math

import jax
import jax.numpy as jnp
import numpy as np
from jax import lax
from jax.experimental import pallas as pl
from jax.experimental.pallas import tpu as pltpu
from jax.sharding import PartitionSpec as P

exchange_coeff = 1.0
damping = 0.3
time_step = 0.2
highest = lax.Precision.HIGHEST
LANES = 128
SUBS = 8
SLOTS = 8


def phase_table(row_index, col_index, length):
    product = row_index[:, None] * col_index[None, :] % length
    angles = product.astype(jnp.float32) * (2.0 * math.pi / length)
    return (jnp.cos(angles), jnp.sin(angles))


def forward_mix(real_part, imag_part, cosine_table, sine_table, pattern):
    real_out = jnp.einsum(pattern, real_part, cosine_table, precision=highest) + jnp.einsum(
        pattern, imag_part, sine_table, precision=highest
    )
    imag_out = jnp.einsum(pattern, imag_part, cosine_table, precision=highest) - jnp.einsum(
        pattern, real_part, sine_table, precision=highest
    )
    return (real_out, imag_out)


def inverse_mix(real_part, imag_part, cosine_table, sine_table, pattern):
    real_out = jnp.einsum(pattern, real_part, cosine_table, precision=highest) - jnp.einsum(
        pattern, imag_part, sine_table, precision=highest
    )
    imag_out = jnp.einsum(pattern, imag_part, cosine_table, precision=highest) + jnp.einsum(
        pattern, real_part, sine_table, precision=highest
    )
    return (real_out, imag_out)


def apply_tensor(kernel, spectrum):
    return jnp.stack(
        [
            kernel[0] * spectrum[0] + kernel[3] * spectrum[1] + kernel[4] * spectrum[2],
            kernel[3] * spectrum[0] + kernel[1] * spectrum[1] + kernel[5] * spectrum[2],
            kernel[4] * spectrum[0] + kernel[5] * spectrum[1] + kernel[2] * spectrum[2],
        ]
    )


def cross_product(first_vec, second_vec):
    return jnp.stack(
        [
            first_vec[1] * second_vec[2] - first_vec[2] * second_vec[1],
            first_vec[2] * second_vec[0] - first_vec[0] * second_vec[2],
            first_vec[0] * second_vec[1] - first_vec[1] * second_vec[0],
        ]
    )


def general_shards(magnetization, kernel, applied):
    count_gx = lax.axis_size("gx")
    count_gy = lax.axis_size("gy")
    count_gz = lax.axis_size("gz")
    local_x = magnetization.shape[1]
    local_y = magnetization.shape[2]
    local_z = magnetization.shape[3]
    full_x = local_x * count_gx
    full_y = local_y * count_gy
    full_z = local_z * count_gz
    part_x = local_x // count_gz
    part_y = full_y // (count_gx * count_gz)
    part_z = full_z // count_gy
    outside = applied[:, None, None, None]
    z_index = jnp.arange(full_z, dtype=jnp.int32)
    weights = jnp.ones((full_z,), jnp.float32)
    planes = z_index.shape[0] // count_gy
    wave_count = z_index.shape[0]
    zlines = lax.all_to_all(magnetization, "gz", split_axis=1, concat_axis=3, tiled=True)
    cos_zf, sin_zf = phase_table(z_index, z_index, full_z)
    cos_zb, sin_zb = phase_table(z_index, z_index, full_z)
    cos_zb = cos_zb * weights[:, None]
    sin_zb = sin_zb * weights[:, None]
    lines_shape = (3, part_x, local_y, full_z)
    wave_shape = (3, part_x, local_y, wave_count)
    z_rows = zlines.reshape(-1, full_z)
    spec_real = jnp.dot(z_rows, cos_zf, precision=highest).reshape(wave_shape)
    spec_imag = -jnp.dot(z_rows, sin_zf, precision=highest).reshape(wave_shape)
    spec_real, spec_imag = (
        lax.all_to_all(spec_real, "gy", split_axis=3, concat_axis=2, tiled=True),
        lax.all_to_all(spec_imag, "gy", split_axis=3, concat_axis=2, tiled=True),
    )
    y_index = jnp.arange(full_y, dtype=jnp.int32)
    cos_y, sin_y = phase_table(y_index, y_index, full_y)
    spec_real, spec_imag = forward_mix(spec_real, spec_imag, cos_y, sin_y, "cxyz,yk->ckxz")
    x_index = jnp.arange(full_x, dtype=jnp.int32)
    cos_xn, sin_xn = phase_table(x_index, x_index, full_x)
    spec_real, spec_imag = (
        lax.all_to_all(spec_real, ("gx", "gz"), split_axis=1, concat_axis=2, tiled=True),
        lax.all_to_all(spec_imag, ("gx", "gz"), split_axis=1, concat_axis=2, tiled=True),
    )
    cos_x, sin_x = (cos_xn, sin_xn)
    spec_real, spec_imag = forward_mix(spec_real, spec_imag, cos_x, sin_x, "cyxz,xk->cyzk")
    inverse_count = 1.0 / (full_x * full_y * full_z)
    out_real = -inverse_count * apply_tensor(kernel, spec_real)
    out_imag = -inverse_count * apply_tensor(kernel, spec_imag)
    wave_y = (lax.axis_index("gx") * count_gz + lax.axis_index("gz")) * part_y + jnp.arange(
        part_y, dtype=jnp.int32
    )
    wave_z = lax.axis_index("gy") * part_z + jnp.arange(planes, dtype=jnp.int32)
    eigenvalue = (
        lattice_eigen(wave_y, full_y)[:, None, None]
        + lattice_eigen(wave_z, full_z)[None, :, None]
        + lattice_eigen(x_index, full_x)[None, None, :]
    )
    factor = inverse_count * exchange_coeff * eigenvalue
    out_real = out_real + factor * spec_real
    out_imag = out_imag + factor * spec_imag
    back_real, back_imag = inverse_mix(out_real, out_imag, cos_xn, sin_xn, "cyzk,kx->cyxz")
    back_real, back_imag = (
        lax.all_to_all(back_real, ("gx", "gz"), split_axis=2, concat_axis=1, tiled=True),
        lax.all_to_all(back_imag, ("gx", "gz"), split_axis=2, concat_axis=1, tiled=True),
    )
    cos_yb, sin_yb = (cos_y, sin_y)
    back_real, back_imag = inverse_mix(back_real, back_imag, cos_yb, sin_yb, "cyxz,yn->cxnz")
    back_real, back_imag = (
        lax.all_to_all(back_real, "gy", split_axis=2, concat_axis=3, tiled=True),
        lax.all_to_all(back_imag, "gy", split_axis=2, concat_axis=3, tiled=True),
    )
    real_rows = back_real.reshape(-1, wave_count)
    imag_rows = back_imag.reshape(-1, wave_count)
    field_lines = (
        jnp.dot(real_rows, cos_zb, precision=highest)
        - jnp.dot(imag_rows, sin_zb, precision=highest)
    ).reshape(lines_shape)
    field_block = lax.all_to_all(field_lines, "gz", split_axis=3, concat_axis=1, tiled=True)
    total_field = field_block + outside
    precess = cross_product(magnetization, total_field)
    double_twist = cross_product(magnetization, precess)
    torque = -(precess + damping * double_twist) / (1.0 + damping * damping)
    stepped = magnetization + time_step * torque
    length = jnp.sqrt(jnp.sum(stepped * stepped, axis=0))
    return (stepped / length, torque)


def cmul_const(value, angle):
    re, im = value
    quarter = angle / (math.pi / 2)
    if abs(quarter - round(quarter)) < 1e-9:
        turn = round(quarter) % 4
        if turn == 0:
            return (re, im)
        if turn == 1:
            return (-im, re)
        if turn == 2:
            return (-re, -im)
        return (im, -re)
    c, s = math.cos(angle), math.sin(angle)
    if abs(abs(c) - abs(s)) < 1e-9:
        h = abs(c)
        sc, ss = math.copysign(1, c), math.copysign(1, s)
        first = re if sc > 0 else -re
        out_re = (first - im) if ss > 0 else (first + im)
        second = im if sc > 0 else -im
        out_im = (second + re) if ss > 0 else (second - re)
        return (h * out_re, h * out_im)
    return (c * re - s * im, c * im + s * re)


def cadd(a, b):
    return (a[0] + b[0], a[1] + b[1])


def csub(a, b):
    return (a[0] - b[0], a[1] - b[1])


def conj(a):
    return (a[0], -a[1])


def complex_fft(values, sign):
    n = len(values)
    if n == 1:
        return values
    even = complex_fft(values[0::2], sign)
    odd = complex_fft(values[1::2], sign)
    odd = [cmul_const(v, sign * 2 * math.pi * k / n) for k, v in enumerate(odd)]
    return [cadd(e, o) for e, o in zip(even, odd)] + [csub(e, o) for e, o in zip(even, odd)]


def real_fft(values):
    n = len(values)
    if n == 2:
        return [values[0] + values[1], values[0] - values[1]]
    even = real_fft(values[0::2])
    odd = real_fft(values[1::2])
    quarter = n // 4
    out = [None] * (n // 2 + 1)
    out[0] = even[0] + odd[0]
    out[n // 2] = even[0] - odd[0]
    for k in range(1, quarter):
        turned = cmul_const(odd[k], -2 * math.pi * k / n)
        out[k] = cadd(even[k], turned)
        out[n // 2 - k] = conj(csub(even[k], turned))
    out[quarter] = (even[quarter], -odd[quarter])
    return out


def real_ifft(values):
    n = 2 * (len(values) - 1)
    if n == 2:
        return [values[0] + values[1], values[0] - values[1]]
    quarter = n // 4
    even = [None] * (quarter + 1)
    odd = [None] * (quarter + 1)
    even[0] = values[0] + values[n // 2]
    odd[0] = values[0] - values[n // 2]
    for k in range(1, quarter):
        mirror = conj(values[n // 2 - k])
        even[k] = cadd(values[k], mirror)
        odd[k] = cmul_const(csub(values[k], mirror), 2 * math.pi * k / n)
    mid = values[quarter]
    even[quarter] = 2.0 * mid[0]
    odd[quarter] = -2.0 * mid[1]
    even = real_ifft(even)
    odd = real_ifft(odd)
    out = [None] * n
    out[0::2] = even
    out[1::2] = odd
    return out


def mm(a, b, dims):
    return lax.dot_general(
        a, b, (dims, ((), ())), precision=highest, preferred_element_type=jnp.float32
    )


class Plan:
    def __init__(self, cx, cy, cz, shape):
        comps, lx, ly, lz = shape
        self.comps, self.lx, self.ly, self.lz = comps, lx, ly, lz
        self.cx, self.cy, self.cz = cx, cy, cz
        self.nx, self.ny, self.nz = lx * cx, ly * cy, lz * cz
        self.planes = cx * cy
        self.groups = cx * cz
        self.devices = cx * cy * cz

    def fits(self):
        if self.devices % 1 or self.lz % self.planes:
            return False
        self.zc = self.lz // self.planes
        self.xl = LANES // self.ly if LANES % self.ly == 0 else 0
        return (
            self.comps == 3
            and self.xl == 4
            and self.cy == 2
            and self.nx == 16 * self.xl
            and self.lx % self.xl == 0
            and self.ly == 2 * self.groups
            and self.zc * SLOTS == LANES
            and self.lz == LANES
            and self.nz % self.zc == 0
        )


def slot_kx(plan, kx2, slot):
    if slot:
        return slot + 16 * kx2
    return (0, 16, 8, 24)[kx2]


def xy_tables(plan):
    lane = np.arange(LANES)
    xl, yl = lane // plan.ly, lane % plan.ly
    half = plan.ny // 2
    fwd = np.zeros((2, 256, 512))
    back = np.zeros((2, 256, 512))
    for r in range(2):
        for k2h in range(2):
            for g in range(plan.groups):
                for ri in range(2):
                    for k2l in range(2):
                        for ql in range(2):
                            block = ri if r == 0 else 1 - ri
                            f = (k2h * plan.groups + g) * 8 + block * 4 + k2l * 2 + ql
                            kx2 = 2 * k2h + k2l
                            ky = 2 * (2 * g + ql) + r
                            ph = 2 * math.pi * (xl * kx2 / 4 + yl * ky / plan.ny)
                            c, s = np.cos(ph), np.sin(ph)
                            if ri == 0:
                                fwd[r, f, 0:128], fwd[r, f, 128:256] = c, s
                                back[r, f, 0:128], back[r, f, 128:256] = c, s
                            else:
                                fwd[r, f, 0:128], fwd[r, f, 128:256] = -s, c
                                back[r, f, 0:128], back[r, f, 128:256] = -s, c
                            kx = slot_kx(plan, kx2, 0)
                            if kx2 == 0:
                                edge = ky in (0, half)
                                if edge:
                                    kx = 0 if ri == 0 else 32
                                else:
                                    kx = 0 if ky < half else 32
                            ph = 2 * math.pi * (xl * kx / plan.nx + yl * ky / plan.ny)
                            c, s = np.cos(ph), np.sin(ph)
                            at = 256 if kx % 16 == 0 else 384
                            if kx2 == 0 and edge:
                                fwd[r, f, at : at + 128] = c
                                back[r, f, at : at + 128] = c
                            else:
                                fwd[r, f, at : at + 128] = c if ri == 0 else -s
                                back[r, f, at : at + 128] = 2 * (c if ri == 0 else -s)
    return fwd.astype(np.float32), back.astype(np.float32)


def x_twiddles(plan):
    xl = np.arange(LANES) // plan.ly
    ph = 2 * math.pi * np.arange(SLOTS)[:, None] * xl[None, :] / plan.nx
    return np.stack([np.cos(ph), np.sin(ph)]).astype(np.float32)


def z_tables(plan):
    zc, nz = plan.zc, plan.nz
    lane = np.arange(LANES) % zc
    ph = 2 * math.pi * np.arange(plan.devices)[:, None] * lane[None, :] / nz
    twiddle = np.stack([np.cos(ph), np.sin(ph)]).astype(np.float32)
    small = 2 * math.pi * np.arange(zc)[:, None] * np.arange(zc)[None, :] / zc
    c = np.kron(np.eye(SLOTS), np.cos(small))
    s = np.kron(np.eye(SLOTS), np.sin(small))
    fwd = np.block([[c, -s], [s, c]]).astype(np.float32)
    back = np.block([[c, s], [-s, c]]).astype(np.float32)
    return twiddle, fwd, back


def pack_kernel(m_ref, out_ref):
    for t in range(m_ref.shape[0]):
        out_ref[:, LANES * t : LANES * (t + 1)] = m_ref[t].T


def xy_forward_kernel(plan, lines_ref, table_ref, tw_ref, out_ref, g_ref):
    zc = plan.zc
    per = plan.lx // plan.xl
    sub = lax.broadcasted_iota(jnp.int32, (SUBS, LANES), 0)
    low = sub < 4
    zero = jnp.zeros((zc, 256), jnp.float32)
    for r in range(2):
        g_ref[r, 0:zc, 0:256] = zero
        for k in range(1, SLOTS):
            g_ref[r, zc * k : zc * (k + 1), 256:512] = zero
    for c in range(plan.comps):
        parts = [[], []]
        for gx in range(plan.cx):
            for xh in range(per):
                at = c * (plan.lx * plan.ly) + xh * LANES
                first = lines_ref[gx * 2, :, at : at + LANES]
                second = lines_ref[gx * 2 + 1, :, at : at + LANES]
                parts[0].append(first + second)
                parts[1].append(first - second)
        outs = []
        for r in range(2):
            spec = real_fft(parts[r])
            g_ref[r, 0:zc, 256:384] = spec[0]
            g_ref[r, 0:zc, 384:512] = spec[8]
            for k in range(1, SLOTS):
                re, im = spec[k]
                tc = tw_ref[0, k : k + 1, :]
                ts = tw_ref[1, k : k + 1, :]
                g_ref[r, zc * k : zc * (k + 1), 0:128] = re * tc + im * ts
                g_ref[r, zc * k : zc * (k + 1), 128:256] = im * tc - re * ts
            outs.append(mm(table_ref[r], g_ref[r], ((1,), (1,))))
        for k2h in range(2):
            for g in range(plan.groups):
                f = (k2h * plan.groups + g) * SUBS
                one = outs[0][f : f + SUBS]
                two = outs[1][f : f + SUBS]
                gx, gz = g // plan.cz, g % plan.cz
                dest = gz * plan.planes + gx * plan.cy + k2h
                out_ref[dest, 2 * c] = jnp.where(low, one, two)
                out_ref[dest, 2 * c + 1] = pltpu.roll(jnp.where(low, two, one), 4, 0)


def xy_inverse_kernel(plan, spec_ref, table_ref, tw_ref, out_ref, h_ref):
    zc = plan.zc
    per = plan.lx // plan.xl
    sub = lax.broadcasted_iota(jnp.int32, (SUBS, LANES), 0)
    low = sub < 4
    for c in range(plan.comps):
        for k2h in range(2):
            for g in range(plan.groups):
                f = (k2h * plan.groups + g) * SUBS
                gx, gz = g // plan.cz, g % plan.cz
                src = gz * plan.planes + gx * plan.cy + k2h
                re = spec_ref[src, 2 * c]
                im = pltpu.roll(spec_ref[src, 2 * c + 1], 4, 0)
                h_ref[0, f : f + SUBS, :] = jnp.where(low, re, im)
                h_ref[1, f : f + SUBS, :] = jnp.where(low, im, re)
        pieces = [mm(h_ref[r].T, table_ref[r], ((1,), (0,))) for r in range(2)]
        fields = []
        for r in range(2):
            u = pieces[r]
            values = [u[0:zc, 256:384]]
            for k in range(1, SLOTS):
                re = u[zc * k : zc * (k + 1), 0:128]
                im = u[zc * k : zc * (k + 1), 128:256]
                tc = tw_ref[0, k : k + 1, :]
                ts = tw_ref[1, k : k + 1, :]
                values.append((re * tc - im * ts, im * tc + re * ts))
            values.append(u[0:zc, 384:512])
            fields.append(real_ifft(values))
        for gx in range(plan.cx):
            for xh in range(per):
                at = c * (plan.lx * plan.ly) + xh * LANES
                one = fields[0][gx * per + xh]
                two = fields[1][gx * per + xh]
                out_ref[gx * 2, :, at : at + LANES] = one + two
                out_ref[gx * 2 + 1, :, at : at + LANES] = one - two


def z_kernel(plan, in_ref, k_ref, kx_ref, mask_ref, tw_ref, fwd_ref, back_ref, out_ref, s_ref):
    n = plan.devices
    mask = mask_ref[...]
    keep = 1.0 - mask

    def to_spectrum(values, at):
        values = complex_fft(values, -1)
        for k in range(n):
            re, im = values[k]
            tc = tw_ref[0, k : k + 1, :]
            ts = tw_ref[1, k : k + 1, :]
            s_ref[at, SUBS * k : SUBS * (k + 1), 0:128] = re * tc + im * ts
            s_ref[at, SUBS * k : SUBS * (k + 1), 128:256] = im * tc - re * ts
        s_ref[at] = mm(s_ref[at], fwd_ref[...], ((1,), (0,)))

    def from_spectrum(at):
        s_ref[at] = mm(s_ref[at], back_ref[...], ((1,), (0,)))
        values = []
        for k in range(n):
            re = s_ref[at, SUBS * k : SUBS * (k + 1), 0:128]
            im = s_ref[at, SUBS * k : SUBS * (k + 1), 128:256]
            tc = tw_ref[0, k : k + 1, :]
            ts = tw_ref[1, k : k + 1, :]
            values.append((re * tc - im * ts, im * tc + re * ts))
        return complex_fft(values, 1)

    for c in range(plan.comps):
        to_spectrum([(in_ref[s, 2 * c], in_ref[s, 2 * c + 1] * keep) for s in range(n)], c)
    extra = []
    zeros = jnp.zeros((SUBS, LANES), jnp.float32)
    for s in range(n):
        e = in_ref[s, 1] * mask
        e = e + pltpu.roll(in_ref[s, 3] * mask, 1, 0)
        e = e + pltpu.roll(in_ref[s, 5] * mask, 2, 0)
        extra.append((e + pltpu.roll(e, 3, 0), zeros))
    to_spectrum(extra, 3)
    for k in range(n):
        rows = slice(SUBS * k, SUBS * (k + 1))
        t = [k_ref[i, k] for i in range(6)]
        d = [kx_ref[i, k] for i in range(3)]
        for half in range(2):
            lanes = slice(128 * half, 128 * (half + 1))
            a, b, g = (s_ref[c, rows, lanes] for c in range(3))
            s_ref[0, rows, lanes] = t[0] * a + t[3] * b + t[4] * g
            s_ref[1, rows, lanes] = t[3] * a + t[1] * b + t[5] * g
            s_ref[2, rows, lanes] = t[4] * a + t[5] * b + t[2] * g
            e = s_ref[3, rows, lanes]
            s_ref[3, rows, lanes] = (
                d[0] * e + d[1] * pltpu.roll(e, 7, 0) + d[2] * pltpu.roll(e, 6, 0)
            )
    extra = from_spectrum(3)
    for c in range(plan.comps):
        values = from_spectrum(c)
        for s in range(n):
            e = extra[s][0]
            if c:
                e = pltpu.roll(e, SUBS - c, 0)
            out_ref[s, 2 * c] = values[s][0]
            out_ref[s, 2 * c + 1] = values[s][1] * keep + e * mask


def finish_kernel(plan, field_ref, m_ref, applied_ref, pred_ref, torque_ref):
    tiles = plan.lx * plan.ly // LANES
    for t in range(tiles):
        h, m = [], []
        for c in range(3):
            at = (c * tiles + t) * LANES
            h.append(field_ref[:, at : at + LANES].T + applied_ref[c])
            m.append(m_ref[c * tiles + t])
        a = [m[1] * h[2] - m[2] * h[1], m[2] * h[0] - m[0] * h[2], m[0] * h[1] - m[1] * h[0]]
        b = [m[1] * a[2] - m[2] * a[1], m[2] * a[0] - m[0] * a[2], m[0] * a[1] - m[1] * a[0]]
        scale = -1.0 / (1.0 + damping * damping)
        torque = [(a[c] + damping * b[c]) * scale for c in range(3)]
        step = [m[c] + time_step * torque[c] for c in range(3)]
        total = step[0] * step[0] + step[1] * step[1] + step[2] * step[2]
        inverse = 1.0 / jnp.sqrt(total)
        for c in range(3):
            torque_ref[c * tiles + t] = torque[c]
            pred_ref[c * tiles + t] = step[c] * inverse


def lattice_eigen(wave_index, length):
    return 2.0 * jnp.cos(wave_index.astype(jnp.float32) * (2.0 * math.pi / length)) - 2.0


def field_tensor(plan, kernel):
    gx, gy, gz = (lax.axis_index(a) for a in ("gx", "gy", "gz"))
    group = gx * plan.cz + gz
    kzs = kernel.shape[2]
    kt = jnp.swapaxes(kernel, 2, 3)
    ky = 4 * group + jnp.arange(4)
    packed = jnp.where((ky <= plan.ny // 2)[None, :, None, None], kt[:, :, 0:1], kt[:, :, 32:33])
    cols = [
        jnp.concatenate([packed, kt[:, :, 1:8]], 2),
        jnp.concatenate([kt[:, :, 16:24]], 2),
        jnp.concatenate([kt[:, :, 8:9], kt[:, :, 33:40]], 2),
        jnp.concatenate([kt[:, :, 24:25], kt[:, :, 49:56]], 2),
    ]
    send = jnp.stack([jnp.stack(cols[0:2], 2), jnp.stack(cols[2:4], 2)])
    edge = jnp.stack([kt[:, 0, 32]] * 2)
    rows = send.reshape(2, 6 * 4 * 2 * 8, kzs)
    rows = jnp.concatenate([rows, edge], 1)
    got = lax.all_to_all(rows, "gy", split_axis=0, concat_axis=0, tiled=True)
    main = got[:, : 6 * 4 * 2 * 8].reshape(2, 6, 2, 2, 2, 8, kzs // 32, 32)
    main = jnp.transpose(main, (1, 7, 3, 4, 2, 5, 0, 6)).reshape(6, 32, 8, 128)
    edge = got[:, 6 * 4 * 2 * 8 :].reshape(2, 6, kzs // 32, 32)
    edge = jnp.transpose(edge, (1, 3, 0, 2)).reshape(6, 32, plan.zc)
    kz = jnp.arange(plan.nz).reshape(plan.zc, 32).T
    table = np.array([[slot_kx(plan, k2, s) for s in range(SLOTS)] for k2 in range(4)])
    kx = jnp.asarray(table.reshape(2, 2, SLOTS), jnp.int32)[gy]
    kyq = (4 * group + 2 * jnp.arange(2)[None, :] + jnp.arange(2)[:, None])
    kx_full = jnp.broadcast_to(kx[None, :, None, :], (2, 2, 2, SLOTS))
    swap = (gy == 0) & (kyq > plan.ny // 2)
    is_packed = (jnp.arange(2)[None, :, None, None] == 0) & (jnp.arange(SLOTS) == 0)
    kx_full = jnp.where(is_packed & swap[:, None, :, None], 32, kx_full)
    ex = lattice_eigen(kx_full, plan.nx)
    ey = lattice_eigen(kyq, plan.ny)
    ez = lattice_eigen(kz, plan.nz)
    plane = (ex + ey[:, None, :, None]).reshape(8, SLOTS)
    eig = plane[None, :, :, None] + ez[:, None, None, :]
    eig = eig.reshape(32, 8, 128)
    scale = 1.0 / (plan.nx * plan.ny * plan.nz)
    diag = jnp.asarray([1, 1, 1, 0, 0, 0], jnp.float32)[:, None, None, None]
    tensor = scale * (exchange_coeff * diag * eig[None] - main)
    edge_eig = lattice_eigen(jnp.asarray(32), plan.nx) + lattice_eigen(4 * group, plan.ny) + ez
    edge = scale * (exchange_coeff * diag[:, :, :, 0] * edge_eig[None] - edge)
    order = np.array([[0, 1, 2], [3, 5, 4], [4, 3, 5]])
    edge = edge[order]
    edge = jnp.transpose(edge, (0, 2, 1, 3))
    edge = jnp.pad(edge, ((0, 0), (0, 0), (0, 5), (0, LANES - plan.zc)))
    special = (gy == 0) & ((group == 0) | (group == plan.groups // 2))
    spot = (jnp.arange(8)[:, None] == 0) & (jnp.arange(LANES)[None, :] < plan.zc)
    mask = jnp.where(special & spot, 1.0, 0.0).astype(jnp.float32)
    return tensor, edge, mask


def call(body, outs, scratch=(), name=None, smem=()):
    def run(*args):
        specs = [
            pl.BlockSpec(memory_space=pltpu.SMEM if i in smem else pltpu.VMEM)
            for i in range(len(args))
        ]
        return pl.pallas_call(
            body,
            out_shape=outs,
            in_specs=specs,
            out_specs=jax.tree.map(lambda _: pl.BlockSpec(memory_space=pltpu.VMEM), outs),
            scratch_shapes=list(scratch),
            name=name,
            compiler_params=pltpu.CompilerParams(vmem_limit_bytes=56 * 2**20),
        )(*args)

    return run


def fast_shards(plan, magnetization, kernel, applied):
    f32 = jnp.float32
    sds = jax.ShapeDtypeStruct
    n, zc = plan.devices, plan.zc
    width = 3 * plan.lx * plan.ly
    tiles = width // LANES
    fwd, back = xy_tables(plan)
    tw = x_twiddles(plan)
    ztw, zf, zb = z_tables(plan)
    m_tiles = magnetization.reshape(tiles, LANES, LANES)
    tensor, edge, mask = field_tensor(plan, kernel)
    packed = call(pack_kernel, sds((plan.lz, width), f32), name="pack")(m_tiles)
    lines = lax.all_to_all(
        packed.reshape(plan.planes, zc, width), ("gx", "gy"), split_axis=0, concat_axis=0, tiled=True
    )
    spec = call(
        lambda *a: xy_forward_kernel(plan, *a),
        sds((n, 6, SUBS, LANES), f32),
        [pltpu.VMEM((2, 128, 512), f32)],
        name="xy_forward",
    )(lines, fwd, tw)
    spec = lax.all_to_all(spec, ("gz", "gx", "gy"), split_axis=0, concat_axis=0, tiled=True)
    spec = call(
        lambda *a: z_kernel(plan, *a),
        sds((n, 6, SUBS, LANES), f32),
        [pltpu.VMEM((4, n * SUBS, 256), f32)],
        name="z_step",
    )(spec, tensor, edge, mask, ztw, zf, zb)
    spec = lax.all_to_all(spec, ("gz", "gx", "gy"), split_axis=0, concat_axis=0, tiled=True)
    field = call(
        lambda *a: xy_inverse_kernel(plan, *a),
        sds((plan.planes, zc, width), f32),
        [pltpu.VMEM((2, 256, 128), f32)],
        name="xy_inverse",
    )(spec, back, tw)
    field = lax.all_to_all(field, ("gx", "gy"), split_axis=0, concat_axis=0, tiled=True)
    pred, torque = call(
        lambda *a: finish_kernel(plan, *a),
        (sds(m_tiles.shape, f32), sds(m_tiles.shape, f32)),
        name="finish",
        smem=(2,),
    )(field.reshape(plan.lz, width), m_tiles, applied)
    return pred.reshape(magnetization.shape), torque.reshape(magnetization.shape)


def solution(mesh):
    sizes = mesh.shape

    def shards(magnetization, kernel, applied):
        plan = Plan(sizes["gx"], sizes["gy"], sizes["gz"], magnetization.shape)
        if plan.fits():
            return fast_shards(plan, magnetization, kernel, applied)
        return general_shards(magnetization, kernel, applied)

    return jax.shard_map(
        shards,
        mesh=mesh,
        in_specs=(P(None, "gx", "gy", "gz"), P(None, ("gx", "gz"), "gy", None), P()),
        out_specs=(P(None, "gx", "gy", "gz"), P(None, "gx", "gy", "gz")),
        check_vma=False,
    )
```

profile of v0, /device:TPU:0, one launch (start us, length us, event | category | flops | bytes accessed | tf_op | source)
XLA Modules:
  0.0 113.1 jit_solution(3807365472168518348)
XLA Ops:
  0.6 2.3 %pack.1 = f32[128,1536]{1,0:T(8,128)} custom-call(f32[12,128,128]{2,1,0:T(8,128)} %bitcast.42), custom_call_target="tpu_custom_call" | custom-call | tf_op jit(solution)/shard_map/pack/pallas_call | solution.py:567
  2.9 5.2 %all-to-all-start = ((f32[8,16,1536]{2,1,0:T(8,128)}), f32[8,16,1536]{2,1,0:T(8,128)S(1)}, u32[]{:S(2)}, u32[]{:S(2)}) async-start(f32[8,16,1536]{2,1,0:T(8,128)} %bitcast.44), calls=%async_computation | async-start | bytes 1572864 | tf_op jit(solution)/shard_map/all_to_all | solution.py:592
  8.1 2.4 %copy.25 = f32[6,4,256,64]{2,0,3,1:T(8,128)S(1)} copy(f32[6,4,256,64]{2,3,1,0:T(8,128)} %param.14) | data formatting | bytes 3145728 | tf_op args[1]
  10.5 0.9 fusion.1
  11.4 0.1 slice_select_fusion
  11.5 1.0 maximum_bitcast_fusion.2
  12.4 1.1 maximum_bitcast_fusion
  13.6 0.1 pad_maximum_fusion.1
  13.6 0.1 copy.19
  13.7 0.1 pad_maximum_fusion
  13.8 0.0 copy-start.4
  13.8 0.9 copy.18
  14.7 0.1 and.84
  14.9 0.1 add.143
  14.9 2.0 %maximum_maximum_fusion = f32[2,390,256]{2,1,0:T(8,128)} fusion(f32[1,6,256]{2,1,0:T(8,128)S(1)} %slice_bitcast_fusion.1, f32[1,384,256]{2,1,0:T(8,128)S(1)} %bitcast.46, f32[1,384,256]{2,1,0:T(8,128)} %bitcast.47), kind=kLoop, calls=%fused_computation.2 | loop fusion | flops 599040 | bytes 1591296 | tf_op jit(solution)/shard_map/concatenate | solution.py:526
  16.9 2.9 %all-to-all-done.a_0_ = f32[8,16,1536]{2,1,0:T(8,128)S(1)} async-done(((f32[8,16,1536]{2,1,0:T(8,128)}), f32[8,16,1536]{2,1,0:T(8,128)S(1)}, u32[]{:S(2)}, u32[]{:S(2)}) %all-to-all-start) | async-done | bytes 786464 | tf_op jit(solution)/shard_map/all_to_all | solution.py:592
  19.8 3.5 %all-to-all-start.2 = ((f32[2,390,256]{2,1,0:T(8,128)}), f32[2,390,256]{2,1,0:T(8,128)S(1)}, u32[]{:S(2)}, u32[]{:S(2)}) async-start(f32[2,390,256]{2,1,0:T(8,128)} %maximum_maximum_fusion), calls=%async_computation.2 | async-start | bytes 1605632 | tf_op jit(solution)/shard_map/all_to_all | solution.py:527
  23.4 0.1 broadcast_and_fusion
  23.5 0.0 copy-done.4
  23.5 0.0 copy-done.1
  23.5 0.0 copy-start.3
  23.5 5.1 %xy_forward.1 = f32[32,6,8,128]{3,2,1,0:T(8,128)} custom-call(f32[8,16,1536]{2,1,0:T(8,128)} %copy-done.1, f32[2,256,512]{2,1,0:T(8,128)} %constant.84.clone.a_1_, f32[2,8,128]{2,1,0:T(8,128)} %constant.85.clone.a_2_), custom_call_target="tpu_custom_call" | custom-call | tf_op jit(solution)/shard_map/xy_forward/pallas_call | solution.py:567
  28.7 6.1 %all-to-all-done.2 = f32[2,390,256]{2,1,0:T(8,128)S(1)} async-done(((f32[2,390,256]{2,1,0:T(8,128)}), f32[2,390,256]{2,1,0:T(8,128)S(1)}, u32[]{:S(2)}, u32[]{:S(2)}) %all-to-all-start.2) | async-done | bytes 798752 | tf_op jit(solution)/shard_map/all_to_all | solution.py:527
  34.8 4.9 %all-to-all-start.1 = ((f32[32,6,8,128]{3,2,1,0:T(8,128)}), f32[32,6,8,128]{3,2,1,0:T(8,128)}, u32[]{:S(2)}, u32[]{:S(2)}) async-start(f32[32,6,8,128]{3,2,1,0:T(8,128)} %xy_forward.1), calls=%async_computation.1 | async-start | bytes 1572864 | tf_op jit(solution)/shard_map/all_to_all | solution.py:601
  39.7 0.1 add_add_fusion
  39.8 0.1 add.146
  39.9 0.1 add.147
  40.0 0.1 multiply_add_fusion
  40.1 0.1 copy.16
  40.3 0.1 broadcast_add_fusion.1
  40.4 0.7 and_select_fusion.a_3_
  41.1 0.9 slice.55
  42.0 1.8 %reshape.230 = f32[2,6,2,2,2,8,8,32]{7,6,5,4,3,2,1,0:T(8,128)S(1)} reshape(f32[2,384,256]{2,1,0:T(8,128)} %slice.55) | data formatting | bytes 1572864 | tf_op jit(solution)/shard_map/reshape | solution.py:528
  43.8 1.9 %copy.20 = f32[6,32,2,2,2,8,2,8]{1,7,6,5,4,3,2,0:T(8,128)} copy(f32[6,32,2,2,2,8,2,8]{1,7,5,3,2,4,0,6:T(8,128)S(1)} %bitcast.36) | data formatting | bytes 1572864 | tf_op jit(solution)/shard_map/transpose | solution.py:529
  45.7 2.4 %copy.21 = f32[6,32,8,128]{3,2,1,0:T(8,128)S(1)} copy(f32[6,32,8,128]{1,3,2,0:T(8,128)} %bitcast.37) | data formatting | bytes 1572864 | tf_op jit(solution)/shard_map/reshape | solution.py:529
  48.1 0.0 slice-done
  48.2 0.1 reshape.232
  48.2 0.1 fusion
  48.3 0.6 gather_fusion
  48.9 0.1 copy.23
  49.0 0.8 pad.4.a_2_
  49.8 1.0 subtract_multiply_fusion.a_1_
  50.8 9.5 %all-to-all-done.1.a_0_ = f32[32,6,8,128]{3,2,1,0:T(8,128)} async-done(((f32[32,6,8,128]{3,2,1,0:T(8,128)}), f32[32,6,8,128]{3,2,1,0:T(8,128)}, u32[]{:S(2)}, u32[]{:S(2)}) %all-to-all-start.1) | async-done | bytes 786464 | tf_op jit(solution)/shard_map/all_to_all | solution.py:601
  60.3 5.5 %z_step.1 = f32[32,6,8,128]{3,2,1,0:T(8,128)} custom-call(f32[32,6,8,128]{3,2,1,0:T(8,128)} %all-to-all-done.1.a_0_, f32[6,32,8,128]{3,2,1,0:T(8,128)} %subtract_multiply_fusion.a_1_, f32[3,32,8,128]{3,2,1,0:T(8,128)} %pad.4.a_2_, f32[8,128]{1,0:T(8,128)} %and_select_fusion.a_3_, f32[2,32,128]{2,1,0:T(8,128)} %constant.86.clone.a_4_, ...), custom_call_target="tpu_custom_call" | custom-call | tf_op jit(solution)/shard_map/z_step/pallas_call | solution.py:567
  65.8 24.3 %all_to_all.25.a_0_ = f32[32,6,8,128]{3,2,1,0:T(8,128)} all-to-all(f32[32,6,8,128]{3,2,1,0:T(8,128)} %z_step.1), channel_id=1, replica_groups=mesh['gx'=4,'gy'=2,'gz'=4] {'gz','gx','gy'}, dimensions={0} | all-to-all | bytes 1572864 | tf_op jit(solution)/shard_map/all_to_all | solution.py:608
  90.1 4.2 %xy_inverse.1 = f32[8,16,1536]{2,1,0:T(8,128)} custom-call(f32[32,6,8,128]{3,2,1,0:T(8,128)} %all_to_all.25.a_0_, f32[2,256,512]{2,1,0:T(8,128)} %constant.89.clone.a_1_, f32[2,8,128]{2,1,0:T(8,128)} %constant.85.clone.a_2_), custom_call_target="tpu_custom_call" | custom-call | tf_op jit(solution)/shard_map/xy_inverse/pallas_call | solution.py:567
  94.2 15.8 %all_to_all.26 = f32[8,16,1536]{2,1,0:T(8,128)} all-to-all(f32[8,16,1536]{2,1,0:T(8,128)} %xy_inverse.1), channel_id=1, replica_groups=mesh['gx'=4,'gy'=2,'gz'=4] {'gx','gy'}, dimensions={0} | all-to-all | bytes 1572864 | tf_op jit(solution)/shard_map/all_to_all | solution.py:615
  110.1 3.1 %finish.1 = (f32[12,128,128]{2,1,0:T(8,128)}, f32[12,128,128]{2,1,0:T(8,128)}) custom-call(f32[128,1536]{1,0:T(8,128)} %bitcast.45, f32[12,128,128]{2,1,0:T(8,128)} %bitcast.43, f32[3]{0:T(128)} %a_2_.3), custom_call_target="tpu_custom_call" | custom-call | tf_op jit(solution)/shard_map/finish/pallas_call | solution.py:567
  (26 shorter events, 0.2 us)
Async XLA Ops:
  2.9 16.9 %all-to-all-start = ((f32[8,16,1536]{2,1,0:T(8,128)}), f32[8,16,1536]{2,1,0:T(8,128)S(1)}, u32[]{:S(2)}, u32[]{:S(2)}) async-start(f32[8,16,1536]{2,1,0:T(8,128)} %bitcast.44), calls=%async_computation | async-start | bytes 1572864 | tf_op jit(solution)/shard_map/all_to_all | solution.py:592
  13.8 9.7 %copy-start.4 = (s32[2,2,8]{2,1,0:T(2,128)S(1)}, s32[2,2,8]{2,1,0:T(2,128)}, u32[]{:S(2)}) copy-start(s32[2,2,8]{2,1,0:T(2,128)} %constant.80.clone) | copy-start | bytes 388
  19.8 3.7 %copy-start.1 = (f32[8,16,1536]{2,1,0:T(8,128)}, f32[8,16,1536]{2,1,0:T(8,128)S(1)}, u32[]{:S(2)}) copy-start(f32[8,16,1536]{2,1,0:T(8,128)S(1)} %all-to-all-done.a_0_) | copy-start | bytes 2359300
  19.8 15.0 %all-to-all-start.2 = ((f32[2,390,256]{2,1,0:T(8,128)}), f32[2,390,256]{2,1,0:T(8,128)S(1)}, u32[]{:S(2)}, u32[]{:S(2)}) async-start(f32[2,390,256]{2,1,0:T(8,128)} %maximum_maximum_fusion), calls=%async_computation.2 | async-start | bytes 1605632 | tf_op jit(solution)/shard_map/all_to_all | solution.py:527
  23.5 16.8 %copy-start.3 = (s32[9]{0:T(128)S(1)}, s32[9]{0:T(128)}, u32[]{:S(2)}) copy-start(s32[9]{0:T(128)} %constant.94) | copy-start | bytes 112
  34.8 6.3 %copy-start = (f32[2,390,256]{2,1,0:T(8,128)}, f32[2,390,256]{2,1,0:T(8,128)S(1)}, u32[]{:S(2)}) copy-start(f32[2,390,256]{2,1,0:T(8,128)S(1)} %all-to-all-done.2) | copy-start | bytes 2396164
  34.8 25.5 %all-to-all-start.1 = ((f32[32,6,8,128]{3,2,1,0:T(8,128)}), f32[32,6,8,128]{3,2,1,0:T(8,128)}, u32[]{:S(2)}, u32[]{:S(2)}) async-start(f32[32,6,8,128]{3,2,1,0:T(8,128)} %xy_forward.1), calls=%async_computation.1 | async-start | bytes 1572864 | tf_op jit(solution)/shard_map/all_to_all | solution.py:601
  45.7 2.4 %slice-start = ((f32[2,390,256]{2,1,0:T(8,128)}), f32[2,6,256]{2,1,0:T(8,128)S(1)}, s32[]{:S(2)}) async-start(f32[2,390,256]{2,1,0:T(8,128)} %copy-done), calls=%async_computation.5 | async-start | bytes 32768 | tf_op jit(solution)/shard_map/slice | solution.py:530
  45.7 2.5 %copy-start.2 = (f32[6]{0:T(128)S(1)}, f32[6]{0:T(128)}, u32[]{:S(2)}) copy-start(f32[6]{0:T(128)} %constant.81.clone) | copy-start | bytes 76
where the time goes:
time: 114 us; the launch traced here: 113 us
  blocking collectives  40.1 us (35%)
  Pallas kernels  20.1 us (18%)
  waiting for transfers between devices  18.5 us (16%)
  starting transfers between devices  13.7 us (12%)
  local copies, waits for them, and re-layouts  13.3 us (12%)
  other arithmetic  6.4 us (6%)
    all_to_all x1, blocking collectives, fast_shards(): lax.all_to_all(spec, ('gz', 'gx', 'gy'), split_axis=0, concat_axis=0, til...  24.3 us
    pallas_call x5, Pallas kernels, run(): pl.pallas_call(body, out_shape=outs, in_specs=specs, out_specs=jax.tree.m...  20.1 us
    all_to_all x1, blocking collectives, fast_shards(): lax.all_to_all(field, ('gx', 'gy'), split_axis=0, concat_axis=0, tiled=True)  15.8 us
    all_to_all x1, waiting for transfers between devices, fast_shards(): lax.all_to_all(spec, ('gz', 'gx', 'gy'), split_axis=0, concat_axis=0, til...  9.45 us
    all_to_all x1, waiting for transfers between devices, field_tensor(): got = lax.all_to_all(rows, 'gy', split_axis=0, concat_axis=0, tiled=True)  6.12 us
    all_to_all x1, starting transfers between devices, fast_shards(): lax.all_to_all(packed.reshape(plan.planes, zc, width), ('gx', 'gy'), spli...  5.2 us
    all_to_all x1, starting transfers between devices, fast_shards(): lax.all_to_all(spec, ('gz', 'gx', 'gy'), split_axis=0, concat_axis=0, til...  4.92 us
    all_to_all x1, starting transfers between devices, field_tensor(): got = lax.all_to_all(rows, 'gy', split_axis=0, concat_axis=0, tiled=True)  3.54 us
  transfers between devices with their start and end apart: 3, of which 3 were waited for; matrix products, arithmetic and copies ran while one was open for 17% of the time, Pallas kernels for 5%

commit v1 on v0

--- a/solution.py
+++ b/solution.py
@@ -236,10 +236,19 @@
     return out
 
 
+def split(value):
+    high = value.astype(jnp.bfloat16)
+    return high, (value - high.astype(jnp.float32)).astype(jnp.bfloat16)
+
+
+def split_table(table, axis):
+    high = table.astype(jnp.bfloat16)
+    low = (table - high.astype(np.float32)).astype(jnp.bfloat16)
+    return np.concatenate([high, low, high], axis)
+
+
 def mm(a, b, dims):
-    return lax.dot_general(
-        a, b, (dims, ((), ())), precision=highest, preferred_element_type=jnp.float32
-    )
+    return lax.dot_general(a, b, (dims, ((), ())), preferred_element_type=jnp.float32)
 
 
 class Plan:
@@ -343,16 +352,23 @@
         out_ref[:, LANES * t : LANES * (t + 1)] = m_ref[t].T
 
 
-def xy_forward_kernel(plan, lines_ref, table_ref, tw_ref, out_ref, g_ref):
+def xy_forward_kernel(plan, lines_ref, table_ref, edge_ref, tw_ref, out_ref, g_ref, e_ref):
     zc = plan.zc
     per = plan.lx // plan.xl
-    sub = lax.broadcasted_iota(jnp.int32, (SUBS, LANES), 0)
-    low = sub < 4
-    zero = jnp.zeros((zc, 256), jnp.float32)
+    low = lax.broadcasted_iota(jnp.int32, (SUBS, LANES), 0) < 4
+    first_slot = lax.broadcasted_iota(jnp.int32, (SUBS, LANES), 1) < zc
+    blank = jnp.zeros((zc, LANES), jnp.bfloat16)
     for r in range(2):
-        g_ref[r, 0:zc, 0:256] = zero
-        for k in range(1, SLOTS):
-            g_ref[r, zc * k : zc * (k + 1), 256:512] = zero
+        for k in range(plan.comps, SLOTS):
+            for q in range(4):
+                e_ref[r, zc * k : zc * (k + 1), LANES * q : LANES * (q + 1)] = blank
+
+    def keep(ref, at, rows, parts):
+        for q, part in enumerate(parts):
+            hi, lo = split(part)
+            ref[(*at, rows, slice(LANES * q, LANES * (q + 1)))] = hi
+            ref[(*at, rows, slice(LANES * (q + 2), LANES * (q + 3)))] = lo
+
     for c in range(plan.comps):
         parts = [[], []]
         for gx in range(plan.cx):
@@ -362,34 +378,43 @@
                 second = lines_ref[gx * 2 + 1, :, at : at + LANES]
                 parts[0].append(first + second)
                 parts[1].append(first - second)
-        outs = []
         for r in range(2):
             spec = real_fft(parts[r])
-            g_ref[r, 0:zc, 256:384] = spec[0]
-            g_ref[r, 0:zc, 384:512] = spec[8]
+            keep(e_ref, (r,), slice(zc * c, zc * (c + 1)), (spec[0], spec[8]))
             for k in range(1, SLOTS):
                 re, im = spec[k]
                 tc = tw_ref[0, k : k + 1, :]
                 ts = tw_ref[1, k : k + 1, :]
-                g_ref[r, zc * k : zc * (k + 1), 0:128] = re * tc + im * ts
-                g_ref[r, zc * k : zc * (k + 1), 128:256] = im * tc - re * ts
-            outs.append(mm(table_ref[r], g_ref[r], ((1,), (1,))))
+                rows = slice(zc * k, zc * (k + 1))
+                keep(g_ref, (r, c), rows, (re * tc + im * ts, im * tc - re * ts))
+            g_ref[r, c, 0:zc, :] = jnp.zeros((zc, 512), jnp.bfloat16)
+
+    def widen(value):
+        return jnp.concatenate([value[:, 0:256], value[:, 0:256], value[:, 256:512]], 1)
+
+    edges = [mm(edge_ref[r], widen(e_ref[r]), ((1,), (1,))) for r in range(2)]
+    for c in range(plan.comps):
+        outs = [mm(table_ref[r], widen(g_ref[r, c]), ((1,), (1,))) for r in range(2)]
         for k2h in range(2):
             for g in range(plan.groups):
                 f = (k2h * plan.groups + g) * SUBS
-                one = outs[0][f : f + SUBS]
-                two = outs[1][f : f + SUBS]
+                both = []
+                for r in range(2):
+                    edge = edges[r][f : f + SUBS]
+                    if c:
+                        edge = pltpu.roll(edge, LANES - zc * c, 1)
+                    both.append(jnp.where(first_slot, edge, outs[r][f : f + SUBS]))
+                one, two = both
                 gx, gz = g // plan.cz, g % plan.cz
                 dest = gz * plan.planes + gx * plan.cy + k2h
                 out_ref[dest, 2 * c] = jnp.where(low, one, two)
                 out_ref[dest, 2 * c + 1] = pltpu.roll(jnp.where(low, two, one), 4, 0)
 
 
-def xy_inverse_kernel(plan, spec_ref, table_ref, tw_ref, out_ref, h_ref):
+def xy_inverse_kernel(plan, spec_ref, table_ref, edge_ref, tw_ref, out_ref, h_ref, t_ref, u_ref):
     zc = plan.zc
     per = plan.lx // plan.xl
-    sub = lax.broadcasted_iota(jnp.int32, (SUBS, LANES), 0)
-    low = sub < 4
+    low = lax.broadcasted_iota(jnp.int32, (SUBS, LANES), 0) < 4
     for c in range(plan.comps):
         for k2h in range(2):
             for g in range(plan.groups):
@@ -398,20 +423,36 @@
                 src = gz * plan.planes + gx * plan.cy + k2h
                 re = spec_ref[src, 2 * c]
                 im = pltpu.roll(spec_ref[src, 2 * c + 1], 4, 0)
-                h_ref[0, f : f + SUBS, :] = jnp.where(low, re, im)
-                h_ref[1, f : f + SUBS, :] = jnp.where(low, im, re)
-        pieces = [mm(h_ref[r].T, table_ref[r], ((1,), (0,))) for r in range(2)]
+                h_ref[c, 0, f : f + SUBS, :] = jnp.where(low, re, im)
+                h_ref[c, 1, f : f + SUBS, :] = jnp.where(low, im, re)
+        for r in range(2):
+            hi, lo = split(h_ref[c, r].T)
+            t_ref[r, LANES * c : LANES * (c + 1), 0:256] = hi
+            t_ref[r, LANES * c : LANES * (c + 1), 256:512] = lo
+
+    def widen(value):
+        return jnp.concatenate([value[:, 0:256], value[:, 0:256], value[:, 256:512]], 1)
+
+    edges = []
+    for r in range(2):
+        u_ref[r] = mm(widen(t_ref[r]), table_ref[r], ((1,), (0,)))
+        rows = jnp.concatenate(
+            [t_ref[r, LANES * c : LANES * c + zc, :] for c in range(plan.comps)], 0
+        )
+        edges.append(mm(widen(rows), edge_ref[r], ((1,), (0,))))
+    for c in range(plan.comps):
         fields = []
         for r in range(2):
-            u = pieces[r]
-            values = [u[0:zc, 256:384]]
+            edge = edges[r][zc * c : zc * (c + 1)]
+            values = [edge[:, 0:128]]
             for k in range(1, SLOTS):
-                re = u[zc * k : zc * (k + 1), 0:128]
-                im = u[zc * k : zc * (k + 1), 128:256]
+                rows = slice(LANES * c + zc * k, LANES * c + zc * (k + 1))
+                re = u_ref[r, rows, 0:128]
+                im = u_ref[r, rows, 128:256]
                 tc = tw_ref[0, k : k + 1, :]
                 ts = tw_ref[1, k : k + 1, :]
                 values.append((re * tc - im * ts, im * tc + re * ts))
-            values.append(u[0:zc, 384:512])
+            values.append(edge[:, 128:256])
             fields.append(real_ifft(values))
         for gx in range(plan.cx):
             for xh in range(per):
@@ -422,61 +463,75 @@
                 out_ref[gx * 2 + 1, :, at : at + LANES] = one - two
 
 
-def z_kernel(plan, in_ref, k_ref, kx_ref, mask_ref, tw_ref, fwd_ref, back_ref, out_ref, s_ref):
+def z_kernel(plan, in_ref, k_ref, kx_ref, mask_ref, tw_ref, fwd_ref, back_ref, out_ref, s_ref, b_ref):
     n = plan.devices
+    half = n // 2 + 1
     mask = mask_ref[...]
     keep = 1.0 - mask
 
+    def transform(at, count, table):
+        hi, lo = split(s_ref[at, 0 : SUBS * count, :])
+        wide = jnp.concatenate([hi, hi, lo], 1)
+        s_ref[at, 0 : SUBS * count, :] = mm(wide, table[...], ((1,), (0,)))
+
     def to_spectrum(values, at):
-        values = complex_fft(values, -1)
-        for k in range(n):
-            re, im = values[k]
+        for k, (re, im) in enumerate(values):
             tc = tw_ref[0, k : k + 1, :]
             ts = tw_ref[1, k : k + 1, :]
             s_ref[at, SUBS * k : SUBS * (k + 1), 0:128] = re * tc + im * ts
             s_ref[at, SUBS * k : SUBS * (k + 1), 128:256] = im * tc - re * ts
-        s_ref[at] = mm(s_ref[at], fwd_ref[...], ((1,), (0,)))
-
-    def from_spectrum(at):
-        s_ref[at] = mm(s_ref[at], back_ref[...], ((1,), (0,)))
+        transform(at, len(values), fwd_ref)
+
+    def from_spectrum(at, count):
+        transform(at, count, back_ref)
         values = []
-        for k in range(n):
+        for k in range(count):
             re = s_ref[at, SUBS * k : SUBS * (k + 1), 0:128]
             im = s_ref[at, SUBS * k : SUBS * (k + 1), 128:256]
             tc = tw_ref[0, k : k + 1, :]
             ts = tw_ref[1, k : k + 1, :]
             values.append((re * tc - im * ts, im * tc + re * ts))
-        return complex_fft(values, 1)
-
-    for c in range(plan.comps):
-        to_spectrum([(in_ref[s, 2 * c], in_ref[s, 2 * c + 1] * keep) for s in range(n)], c)
+        return values
+
     extra = []
-    zeros = jnp.zeros((SUBS, LANES), jnp.float32)
     for s in range(n):
         e = in_ref[s, 1] * mask
         e = e + pltpu.roll(in_ref[s, 3] * mask, 1, 0)
         e = e + pltpu.roll(in_ref[s, 5] * mask, 2, 0)
-        extra.append((e + pltpu.roll(e, 3, 0), zeros))
+        extra.append(e + pltpu.roll(e, 3, 0))
+    extra = real_fft(extra)
+    zero = jnp.zeros((SUBS, LANES), jnp.float32)
+    extra[0] = (extra[0], zero)
+    extra[-1] = (extra[-1], zero)
     to_spectrum(extra, 3)
+    for c in range(plan.comps):
+        values = [(in_ref[s, 2 * c], in_ref[s, 2 * c + 1] * keep) for s in range(n)]
+        to_spectrum(complex_fft(values, -1), c)
     for k in range(n):
         rows = slice(SUBS * k, SUBS * (k + 1))
         t = [k_ref[i, k] for i in range(6)]
-        d = [kx_ref[i, k] for i in range(3)]
-        for half in range(2):
-            lanes = slice(128 * half, 128 * (half + 1))
+        for part in range(2):
+            lanes = slice(LANES * part, LANES * (part + 1))
             a, b, g = (s_ref[c, rows, lanes] for c in range(3))
             s_ref[0, rows, lanes] = t[0] * a + t[3] * b + t[4] * g
             s_ref[1, rows, lanes] = t[3] * a + t[1] * b + t[5] * g
             s_ref[2, rows, lanes] = t[4] * a + t[5] * b + t[2] * g
-            e = s_ref[3, rows, lanes]
-            s_ref[3, rows, lanes] = (
-                d[0] * e + d[1] * pltpu.roll(e, 7, 0) + d[2] * pltpu.roll(e, 6, 0)
-            )
-    extra = from_spectrum(3)
+            if k < half:
+                d = [kx_ref[i, k] for i in range(3)]
+                e = s_ref[3, rows, lanes]
+                s_ref[3, rows, lanes] = (
+                    d[0] * e + d[1] * pltpu.roll(e, 7, 0) + d[2] * pltpu.roll(e, 6, 0)
+                )
+    extra = from_spectrum(3, half)
+    extra[0] = extra[0][0]
+    extra[-1] = extra[-1][0]
+    extra = real_ifft(extra)
+    for s in range(n):
+        b_ref[s] = extra[s]
     for c in range(plan.comps):
-        values = from_spectrum(c)
+        values = complex_fft(from_spectrum(c, n), 1)
         for s in range(n):
-            e = extra[s][0]
+            e = b_ref[s]
             if c:
                 e = pltpu.roll(e, SUBS - c, 0)
             out_ref[s, 2 * c] = values[s][0]
@@ -497,7 +552,7 @@
         torque = [(a[c] + damping * b[c]) * scale for c in range(3)]
         step = [m[c] + time_step * torque[c] for c in range(3)]
         total = step[0] * step[0] + step[1] * step[1] + step[2] * step[2]
-        inverse = 1.0 / jnp.sqrt(total)
+        inverse = lax.rsqrt(total)
         for c in range(3):
             torque_ref[c * tiles + t] = torque[c]
             pred_ref[c * tiles + t] = step[c] * inverse
@@ -507,8 +562,8 @@
     return 2.0 * jnp.cos(wave_index.astype(jnp.float32) * (2.0 * math.pi / length)) - 2.0
 
 
-def field_tensor(plan, kernel):
-    gx, gy, gz = (lax.axis_index(a) for a in ("gx", "gy", "gz"))
+def tensor_rows(plan, kernel):
+    gx, gz = (lax.axis_index(a) for a in ("gx", "gz"))
     group = gx * plan.cz + gz
     kzs = kernel.shape[2]
     kt = jnp.swapaxes(kernel, 2, 3)
@@ -523,8 +578,17 @@
     send = jnp.stack([jnp.stack(cols[0:2], 2), jnp.stack(cols[2:4], 2)])
     edge = jnp.stack([kt[:, 0, 32]] * 2)
     rows = send.reshape(2, 6 * 4 * 2 * 8, kzs)
-    rows = jnp.concatenate([rows, edge], 1)
-    got = lax.all_to_all(rows, "gy", split_axis=0, concat_axis=0, tiled=True)
+    return jnp.concatenate([rows, edge], 1)
+
+
+def field_tensor(plan, rows):
+    gx, gy, gz = (lax.axis_index(a) for a in ("gx", "gy", "gz"))
+    group = gx * plan.cz + gz
+    kzs = rows.shape[2]
+    own = lax.dynamic_index_in_dim(rows, gy, 0)
+    other = lax.dynamic_index_in_dim(rows, 1 - gy, 0)
+    other = lax.ppermute(other, "gy", [(0, 1), (1, 0)])
+    got = jnp.where(gy == 0, jnp.concatenate([own, other]), jnp.concatenate([other, own]))
     main = got[:, : 6 * 4 * 2 * 8].reshape(2, 6, 2, 2, 2, 8, kzs // 32, 32)
     main = jnp.transpose(main, (1, 7, 3, 4, 2, 5, 0, 6)).reshape(6, 32, 8, 128)
     edge = got[:, 6 * 4 * 2 * 8 :].reshape(2, 6, kzs // 32, 32)
@@ -584,34 +648,42 @@
     width = 3 * plan.lx * plan.ly
     tiles = width // LANES
     fwd, back = xy_tables(plan)
+    fwd = [split_table(t, 2) for t in (fwd[:, :, 0:256], fwd[:, :, 256:512])]
+    back = [split_table(t, 1) for t in (back[:, :, 0:256], back[:, :, 256:512])]
     tw = x_twiddles(plan)
     ztw, zf, zb = z_tables(plan)
+    zf, zb = split_table(zf, 0), split_table(zb, 0)
     m_tiles = magnetization.reshape(tiles, LANES, LANES)
-    tensor, edge, mask = field_tensor(plan, kernel)
     packed = call(pack_kernel, sds((plan.lz, width), f32), name="pack")(m_tiles)
+    packed, kernel = lax.optimization_barrier((packed, kernel))
+    tensor, edge, mask = field_tensor(plan, tensor_rows(plan, kernel))
     lines = lax.all_to_all(
         packed.reshape(plan.planes, zc, width), ("gx", "gy"), split_axis=0, concat_axis=0, tiled=True
     )
     spec = call(
         lambda *a: xy_forward_kernel(plan, *a),
         sds((n, 6, SUBS, LANES), f32),
-        [pltpu.VMEM((2, 128, 512), f32)],
+        [pltpu.VMEM((2, 3, LANES, 512), jnp.bfloat16), pltpu.VMEM((2, LANES, 512), jnp.bfloat16)],
         name="xy_forward",
-    )(lines, fwd, tw)
+    )(lines, *fwd, tw)
     spec = lax.all_to_all(spec, ("gz", "gx", "gy"), split_axis=0, concat_axis=0, tiled=True)
     spec = call(
         lambda *a: z_kernel(plan, *a),
         sds((n, 6, SUBS, LANES), f32),
-        [pltpu.VMEM((4, n * SUBS, 256), f32)],
+        [pltpu.VMEM((4, n * SUBS, 256), f32), pltpu.VMEM((n, SUBS, LANES), f32)],
         name="z_step",
     )(spec, tensor, edge, mask, ztw, zf, zb)
     spec = lax.all_to_all(spec, ("gz", "gx", "gy"), split_axis=0, concat_axis=0, tiled=True)
     field = call(
         lambda *a: xy_inverse_kernel(plan, *a),
         sds((plan.planes, zc, width), f32),
-        [pltpu.VMEM((2, 256, 128), f32)],
+        [
+            pltpu.VMEM((3, 2, 256, LANES), f32),
+            pltpu.VMEM((2, 3 * LANES, 512), jnp.bfloat16),
+            pltpu.VMEM((2, 3 * LANES, 256), f32),
+        ],
         name="xy_inverse",
-    )(spec, back, tw)
+    )(spec, *back, tw)
     field = lax.all_to_all(field, ("gx", "gy"), split_axis=0, concat_axis=0, tiled=True)
     pred, torque = call(
         lambda *a: finish_kernel(plan, *a),

time: 114 us -> 101 us (0.89)
  waiting for transfers between devices: 18.5 us -> 13.7 us
  Pallas kernels: 20.1 us -> 16.3 us
  other arithmetic: 6.4 us -> 3.61 us
  starting transfers between devices: 13.7 us -> 12.3 us
    all_to_all x1 -> x0, waiting for transfers between devices: 6.12 us -> none  [field_tensor(): got = lax.all_to_all(rows, 'gy', split_axis=0, concat_axis=0, tiled=True)]
    pallas_call x5, Pallas kernels: 20.1 us -> 16.3 us  [run(): pl.pallas_call(body, out_shape=outs, in_specs=specs, out_specs=jax.tree.m...]
    all_to_all x1 -> x0, starting transfers between devices: 3.54 us -> none  [field_tensor(): got = lax.all_to_all(rows, 'gy', split_axis=0, concat_axis=0, tiled=True)]
    optimization_barrier x0 -> x1, local copies, waits for them, and re-layouts: none -> 2.35 us  [fast_shards(): packed, kernel = lax.optimization_barrier((packed, kernel))]
    ppermute x0 -> x1, starting transfers between devices: none -> 2.09 us  [field_tensor(): other = lax.ppermute(other, 'gy', [(0, 1), (1, 0)])]
    concatenate x1, other arithmetic: 1.96 us -> 0.06 us  [tensor_rows(): return jnp.concatenate([rows, edge], 1)]
    unnamed x11 -> x8, local copies, waits for them, and re-layouts: 2.38 us -> 0.91 us
  transfers between devices with their start and end apart: 3 -> 3, of which waited for: 3 -> 2; matrix products, arithmetic and copies ran while one was open for 17% -> 16% of each run, Pallas kernels for 5% -> 4%
where the time goes in v1:
time: 101 us; the launch traced here: 100 us
  blocking collectives  40.1 us (40%)
  Pallas kernels  16.3 us (16%)
  waiting for transfers between devices  13.7 us (14%)
  local copies, waits for them, and re-layouts  13.5 us (13%)
  starting transfers between devices  12.3 us (12%)
  other arithmetic  3.61 us (4%)
    all_to_all x1, blocking collectives, fast_shards(): lax.all_to_all(spec, ('gz', 'gx', 'gy'), split_axis=0, concat_axis=0, til...  24.3 us
    pallas_call x5, Pallas kernels, run(): pl.pallas_call(body, out_shape=outs, in_specs=specs, out_specs=jax.tree.m...  16.3 us
    all_to_all x1, blocking collectives, fast_shards(): lax.all_to_all(field, ('gx', 'gy'), split_axis=0, concat_axis=0, tiled=True)  15.8 us
    all_to_all x1, waiting for transfers between devices, fast_shards(): lax.all_to_all(spec, ('gz', 'gx', 'gy'), split_axis=0, concat_axis=0, til...  9.86 us
    all_to_all x1, starting transfers between devices, fast_shards(): lax.all_to_all(packed.reshape(plan.planes, zc, width), ('gx', 'gy'), spli...  5.2 us
    all_to_all x1, starting transfers between devices, fast_shards(): lax.all_to_all(spec, ('gz', 'gx', 'gy'), split_axis=0, concat_axis=0, til...  4.98 us
    all_to_all x1, waiting for transfers between devices, fast_shards(): lax.all_to_all(packed.reshape(plan.planes, zc, width), ('gx', 'gy'), spli...  3.84 us
    reshape x1, local copies, waits for them, and re-layouts, field_tensor(): main = jnp.transpose(main, (1, 7, 3, 4, 2, 5, 0, 6)).reshape(6, 32, 8, 128)  2.36 us
  transfers between devices with their start and end apart: 3, of which 2 were waited for; matrix products, arithmetic and copies ran while one was open for 16% of the time, Pallas kernels for 4%

profile of v1, /device:TPU:0, one launch (start us, length us, event | category | flops | bytes accessed | tf_op | source)
XLA Modules:
  0.0 100.4 jit_solution(11136176613160775865)
XLA Ops:
  0.6 2.3 %pack.1 = f32[128,1536]{1,0:T(8,128)} custom-call(f32[12,128,128]{2,1,0:T(8,128)} %bitcast.42), custom_call_target="tpu_custom_call" | custom-call | tf_op jit(solution)/shard_map/pack/pallas_call | solution.py:631
  2.9 5.2 %all-to-all-start = ((f32[8,16,1536]{2,1,0:T(8,128)}), f32[8,16,1536]{2,1,0:T(8,128)S(1)}, u32[]{:S(2)}, u32[]{:S(2)}) async-start(f32[8,16,1536]{2,1,0:T(8,128)} %bitcast.44), calls=%async_computation | async-start | bytes 1572864 | tf_op jit(solution)/shard_map/all_to_all | solution.py:660
  8.1 2.4 %copy.27 = f32[6,4,256,64]{2,0,3,1:T(8,128)S(1)} copy(f32[6,4,256,64]{2,3,1,0:T(8,128)} %param.16) | data formatting | bytes 3145728 | tf_op jit(solution)/shard_map/optimization_barrier | solution.py:658
  10.5 0.8 fusion.1
  11.3 0.1 slice_select_fusion
  11.4 1.1 %maximum_bitcast_fusion = (f32[6,4,1,8,256]{4,0,3,1,2:T(8,128)S(1)}, f32[6,4,1,8,256]{4,0,3,1,2:T(8,128)S(1)}) fusion(f32[6,4,7,256]{3,0,2,1:T(8,128)} %get-tuple-element.13, f32[6,4,1,256]{3,0,2,1:T(8,128)S(1)} %get-tuple-element.10, f32[6,4,7,256]{3,0,2,1:T(8,128)} %get-tuple-element.15, f32[6,4,1,256]{3,0,2,1:T(8,128)S(1)} %get-tuple-element.12), kind=kLoop, calls=%fused_computation.8 | loop fusion | flops 98304 | bytes 786432 | tf_op jit(solution)/shard_map/stack | solution.py:578
  12.5 0.1 pad_maximum_fusion
  12.6 0.1 copy.20
  12.8 0.1 pad_maximum_fusion.1
  12.8 0.0 copy-start.3
  12.8 0.1 copy.21
  13.0 0.1 maximum_maximum_fusion
  13.0 0.1 constant_dynamic-slice_fusion.1
  13.1 2.1 %collective-permute-start = (f32[1,390,256]{2,1,0:T(8,128)S(1)}, f32[1,390,256]{2,1,0:T(8,128)S(1)}, u32[]{:S(2)}, u32[]{:S(2)}) collective-permute-start(f32[1,390,256]{2,1,0:T(8,128)S(1)} %get-tuple-element.17), channel_id=1, source_target_pairs={{0,4},{4,0},{1,5},{5,1},{2,6},{6,2},{3,7},{7,3},{8,12},{12,8},{9,1... | collective-permute-start | bytes 1198088 | tf_op jit(solution)/shard_map/ppermute | solution.py:590
  15.4 0.1 and.84
  15.5 0.1 add.150
  15.6 0.1 broadcast_and_fusion
  15.7 0.1 add_add_fusion
  15.8 0.1 add.153
  15.9 0.1 add.154
  16.0 3.8 %all-to-all-done.a_0_ = f32[8,16,1536]{2,1,0:T(8,128)S(1)} async-done(((f32[8,16,1536]{2,1,0:T(8,128)}), f32[8,16,1536]{2,1,0:T(8,128)S(1)}, u32[]{:S(2)}, u32[]{:S(2)}) %all-to-all-start) | async-done | bytes 786464 | tf_op jit(solution)/shard_map/all_to_all | solution.py:660
  19.8 0.9 copy-done
  20.7 3.6 %xy_forward.1 = f32[32,6,8,128]{3,2,1,0:T(8,128)} custom-call(f32[8,16,1536]{2,1,0:T(8,128)} %copy-done, bf16[2,256,768]{2,1,0:T(8,128)(2,1)} %constant.98.clone.a_1_, bf16[2,256,768]{2,1,0:T(8,128)(2,1)} %constant.99.clone.a_2_, f32[2,8,128]{2,1,0:T(8,128)} %constant.100.clone.a_3_), custom_call_target="tpu_custom_call" | custom-call | tf_op jit(solution)/shard_map/xy_forward/pallas_call | solution.py:631
  24.3 5.0 %all-to-all-start.1 = ((f32[32,6,8,128]{3,2,1,0:T(8,128)}), f32[32,6,8,128]{3,2,1,0:T(8,128)}, u32[]{:S(2)}, u32[]{:S(2)}) async-start(f32[32,6,8,128]{3,2,1,0:T(8,128)} %xy_forward.1), calls=%async_computation.1 | async-start | bytes 1572864 | tf_op jit(solution)/shard_map/all_to_all | solution.py:669
  29.3 0.0 copy-start.1
  29.3 0.1 multiply_add_fusion
  29.4 0.1 copy.18
  29.5 0.0 copy-done.2
  29.5 0.1 broadcast_add_fusion.1
  29.6 0.7 and_select_fusion.a_3_
  30.3 0.0 collective-permute-done
  30.3 0.1 maximum_select_fusion
  30.3 0.9 slice.55
  31.3 0.1 reshape.232
  31.4 0.1 fusion
  31.5 0.6 gather_fusion
  32.0 0.1 copy.25
  32.1 1.8 %reshape.230 = f32[2,6,2,2,2,8,8,32]{7,6,5,4,3,2,1,0:T(8,128)S(1)} reshape(f32[2,384,256]{2,1,0:T(8,128)} %slice.55) | data formatting | bytes 1572864 | tf_op jit(solution)/shard_map/reshape | solution.py:592
  34.0 1.9 %copy.22 = f32[6,32,2,2,2,8,2,8]{1,7,6,5,4,3,2,0:T(8,128)} copy(f32[6,32,2,2,2,8,2,8]{1,7,5,3,2,4,0,6:T(8,128)S(1)} %bitcast.36) | data formatting | bytes 1572864 | tf_op jit(solution)/shard_map/transpose | solution.py:593
  35.9 2.4 %copy.23 = f32[6,32,8,128]{3,2,1,0:T(8,128)S(1)} copy(f32[6,32,8,128]{1,3,2,0:T(8,128)} %bitcast.37) | data formatting | bytes 1572864 | tf_op jit(solution)/shard_map/reshape | solution.py:593
  38.2 0.8 pad.4.a_2_
  39.0 1.0 %subtract_multiply_fusion.a_1_ = f32[6,32,8,128]{3,2,1,0:T(8,128)} fusion(f32[6,32,8,128]{3,2,1,0:T(8,128)S(1)} %copy.23, f32[32,8,128]{2,1,0:T(8,128)S(1)} %broadcast_add_fusion, f32[6]{0:T(128)S(1)} %copy-done.1), kind=kLoop, calls=%fused_computation.4 | loop fusion | flops 589824 | bytes 1703960 | tf_op jit(solution)/shard_map/mul | solution.py:612
  40.1 9.9 %all-to-all-done.1.a_0_ = f32[32,6,8,128]{3,2,1,0:T(8,128)} async-done(((f32[32,6,8,128]{3,2,1,0:T(8,128)}), f32[32,6,8,128]{3,2,1,0:T(8,128)}, u32[]{:S(2)}, u32[]{:S(2)}) %all-to-all-start.1) | async-done | bytes 786464 | tf_op jit(solution)/shard_map/all_to_all | solution.py:669
  49.9 4.1 %z_step.1 = f32[32,6,8,128]{3,2,1,0:T(8,128)} custom-call(f32[32,6,8,128]{3,2,1,0:T(8,128)} %all-to-all-done.1.a_0_, f32[6,32,8,128]{3,2,1,0:T(8,128)} %subtract_multiply_fusion.a_1_, f32[3,32,8,128]{3,2,1,0:T(8,128)} %pad.4.a_2_, f32[8,128]{1,0:T(8,128)} %and_select_fusion.a_3_, f32[2,32,128]{2,1,0:T(8,128)} %constant.101.clone.a_4_, ...), custom_call_target="tpu_custom_call" | custom-call | tf_op jit(solution)/shard_map/z_step/pallas_call | solution.py:631
  54.0 24.3 %all_to_all.20.a_0_ = f32[32,6,8,128]{3,2,1,0:T(8,128)} all-to-all(f32[32,6,8,128]{3,2,1,0:T(8,128)} %z_step.1), channel_id=1, replica_groups=mesh['gx'=4,'gy'=2,'gz'=4] {'gz','gx','gy'}, dimensions={0} | all-to-all | bytes 1572864 | tf_op jit(solution)/shard_map/all_to_all | solution.py:676
  78.4 3.2 %xy_inverse.1 = f32[8,16,1536]{2,1,0:T(8,128)} custom-call(f32[32,6,8,128]{3,2,1,0:T(8,128)} %all_to_all.20.a_0_, bf16[2,768,256]{2,1,0:T(8,128)(2,1)} %constant.104.clone.a_1_, bf16[2,768,256]{2,1,0:T(8,128)(2,1)} %constant.105.clone.a_2_, f32[2,8,128]{2,1,0:T(8,128)} %constant.100.clone.a_3_), custom_call_target="tpu_custom_call" | custom-call | tf_op jit(solution)/shard_map/xy_inverse/pallas_call | solution.py:631
  81.6 15.8 %all_to_all.21 = f32[8,16,1536]{2,1,0:T(8,128)} all-to-all(f32[8,16,1536]{2,1,0:T(8,128)} %xy_inverse.1), channel_id=1, replica_groups=mesh['gx'=4,'gy'=2,'gz'=4] {'gx','gy'}, dimensions={0} | all-to-all | bytes 1572864 | tf_op jit(solution)/shard_map/all_to_all | solution.py:687
  97.4 3.0 %finish.1 = (f32[12,128,128]{2,1,0:T(8,128)}, f32[12,128,128]{2,1,0:T(8,128)}) custom-call(f32[128,1536]{1,0:T(8,128)} %bitcast.45, f32[12,128,128]{2,1,0:T(8,128)} %bitcast.43, f32[3]{0:T(128)} %a_2_.3), custom_call_target="tpu_custom_call" | custom-call | tf_op jit(solution)/shard_map/finish/pallas_call | solution.py:631
  (25 shorter events, 0.2 us)
Async XLA Ops:
  2.9 16.9 %all-to-all-start = ((f32[8,16,1536]{2,1,0:T(8,128)}), f32[8,16,1536]{2,1,0:T(8,128)S(1)}, u32[]{:S(2)}, u32[]{:S(2)}) async-start(f32[8,16,1536]{2,1,0:T(8,128)} %bitcast.44), calls=%async_computation | async-start | bytes 1572864 | tf_op jit(solution)/shard_map/all_to_all | solution.py:660
  12.8 2.9 %copy-start.3 = (s32[2,2,8]{2,1,0:T(2,128)S(1)}, s32[2,2,8]{2,1,0:T(2,128)}, u32[]{:S(2)}) copy-start(s32[2,2,8]{2,1,0:T(2,128)} %constant.94.clone) | copy-start | bytes 388
  13.1 17.1 %collective-permute-start = (f32[1,390,256]{2,1,0:T(8,128)S(1)}, f32[1,390,256]{2,1,0:T(8,128)S(1)}, u32[]{:S(2)}, u32[]{:S(2)}) collective-permute-start(f32[1,390,256]{2,1,0:T(8,128)S(1)} %get-tuple-element.17), channel_id=1, source_target_pairs={{0,4},{4,0},{1,5},{5,1},{2,6},{6,2},{3,7},{7,3},{8,12},{12,8},{9,1... | collective-permute-start | bytes 1198088 | tf_op jit(solution)/shard_map/ppermute | solution.py:590
  16.0 13.5 %copy-start.2 = (s32[9]{0:T(128)S(1)}, s32[9]{0:T(128)}, u32[]{:S(2)}) copy-start(s32[9]{0:T(128)} %constant.110) | copy-start | bytes 112
  19.8 0.9 copy-start
  24.3 25.6 %all-to-all-start.1 = ((f32[32,6,8,128]{3,2,1,0:T(8,128)}), f32[32,6,8,128]{3,2,1,0:T(8,128)}, u32[]{:S(2)}, u32[]{:S(2)}) async-start(f32[32,6,8,128]{3,2,1,0:T(8,128)} %xy_forward.1), calls=%async_computation.1 | async-start | bytes 1572864 | tf_op jit(solution)/shard_map/all_to_all | solution.py:669
  29.3 2.0 %copy-start.1 = (f32[6]{0:T(128)S(1)}, f32[6]{0:T(128)}, u32[]{:S(2)}) copy-start(f32[6]{0:T(128)} %constant.95.clone) | copy-start | bytes 76

commit v2 on v1

--- a/solution.py
+++ b/solution.py
@@ -7,6 +7,7 @@
 from jax.experimental import pallas as pl
 from jax.experimental.pallas import tpu as pltpu
 from jax.sharding import PartitionSpec as P
+
 
 exchange_coeff = 1.0
 damping = 0.3
@@ -279,7 +280,7 @@
         )
 
 
-def slot_kx(plan, kx2, slot):
+def slot_kx(kx2, slot):
     if slot:
         return slot + 16 * kx2
     return (0, 16, 8, 24)[kx2]
@@ -309,7 +310,7 @@
                             else:
                                 fwd[r, f, 0:128], fwd[r, f, 128:256] = -s, c
                                 back[r, f, 0:128], back[r, f, 128:256] = -s, c
-                            kx = slot_kx(plan, kx2, 0)
+                            kx = slot_kx(kx2, 0)
                             if kx2 == 0:
                                 edge = ky in (0, half)
                                 if edge:
@@ -347,12 +348,41 @@
     return twiddle, fwd, back
 
 
-def pack_kernel(m_ref, out_ref):
-    for t in range(m_ref.shape[0]):
-        out_ref[:, LANES * t : LANES * (t + 1)] = m_ref[t].T
-
-
-def xy_forward_kernel(plan, lines_ref, table_ref, edge_ref, tw_ref, out_ref, g_ref, e_ref):
+def fetch(source, target, sem):
+    copy = pltpu.make_async_copy(source, target, sem)
+    copy.start()
+    return copy
+
+
+def plane_index():
+    return lax.axis_index("gx") * lax.axis_size("gy") + lax.axis_index("gy")
+
+
+def pack_kernel(plan, m_ref, *rest):
+    outs, (m_buf, buf, sem_in) = rest[: plan.planes], rest[plan.planes :]
+    me = plane_index()
+    per = plan.lx * plan.ly // LANES
+    width = per * LANES
+    loads = [
+        fetch(m_ref.at[pl.ds(c * per, per)], m_buf.at[pl.ds(c * per, per)], sem_in.at[c])
+        for c in range(plan.comps)
+    ]
+    for c in range(plan.comps):
+        loads[c].wait()
+        for t in range(c * per, (c + 1) * per):
+            buf[:, LANES * t : LANES * (t + 1)] = m_buf[t].T
+        for o in range(plan.planes):
+            rows = pl.ds(plan.zc * (me ^ o), plan.zc)
+            cols = slice(width * c, width * (c + 1))
+            outs[o][:, cols] = buf[rows, cols]
+
+
+def xy_forward_kernel(plan, *refs):
+    chunks, refs = refs[: plan.planes], refs[plan.planes :]
+    table_ref, edge_ref, tw_ref, out_ref, lines_ref, g_ref, e_ref = refs
+    me = plane_index()
+    for o in range(plan.planes):
+        lines_ref[me ^ o] = chunks[o][...]
     zc = plan.zc
     per = plan.lx // plan.xl
     low = lax.broadcasted_iota(jnp.int32, (SUBS, LANES), 0) < 4
@@ -411,7 +441,9 @@
                 out_ref[dest, 2 * c + 1] = pltpu.roll(jnp.where(low, two, one), 4, 0)
 
 
-def xy_inverse_kernel(plan, spec_ref, table_ref, edge_ref, tw_ref, out_ref, h_ref, t_ref, u_ref):
+def xy_inverse_kernel(plan, spec_ref, table_ref, edge_ref, tw_ref, *refs):
+    outs, (h_ref, t_ref, u_ref, out_ref) = refs[: plan.planes], refs[plan.planes :]
+    me = plane_index()
     zc = plan.zc
     per = plan.lx // plan.xl
     low = lax.broadcasted_iota(jnp.int32, (SUBS, LANES), 0) < 4
@@ -461,9 +493,13 @@
                 two = fields[1][gx * per + xh]
                 out_ref[gx * 2, :, at : at + LANES] = one + two
                 out_ref[gx * 2 + 1, :, at : at + LANES] = one - two
-
-
-def z_kernel(plan, in_ref, k_ref, kx_ref, mask_ref, tw_ref, fwd_ref, back_ref, out_ref, s_ref, b_ref):
+    for o in range(plan.planes):
+        outs[o][...] = out_ref[me ^ o]
+
+
+def z_kernel(
+    plan, in_ref, k_ref, kx_ref, mask_ref, tw_ref, fwd_ref, back_ref, out_ref, s_ref, b_ref
+):
     n = plan.devices
     half = n // 2 + 1
     mask = mask_ref[...]
@@ -493,6 +529,9 @@
             values.append((re * tc - im * ts, im * tc + re * ts))
         return values
 
+    for c in range(plan.comps):
+        values = [(in_ref[s, 2 * c], in_ref[s, 2 * c + 1] * keep) for s in range(n)]
+        to_spectrum(complex_fft(values, -1), c)
     extra = []
     for s in range(n):
         e = in_ref[s, 1] * mask
@@ -504,9 +543,6 @@
     extra[0] = (extra[0], zero)
     extra[-1] = (extra[-1], zero)
     to_spectrum(extra, 3)
-    for c in range(plan.comps):
-        values = [(in_ref[s, 2 * c], in_ref[s, 2 * c + 1] * keep) for s in range(n)]
-        to_spectrum(complex_fft(values, -1), c)
     for k in range(n):
         rows = slice(SUBS * k, SUBS * (k + 1))
         t = [k_ref[i, k] for i in range(6)]
@@ -538,63 +574,94 @@
             out_ref[s, 2 * c + 1] = values[s][1] * keep + e * mask
 
 
-def finish_kernel(plan, field_ref, m_ref, applied_ref, pred_ref, torque_ref):
+def finish_kernel(plan, *refs):
+    chunks, refs = refs[: plan.planes], refs[plan.planes :]
+    m_ref, applied_ref, pred_hbm, torque_hbm, *refs = refs
+    field_ref, pred_ref, torque_ref, sem_out = refs
+    me = plane_index()
     tiles = plan.lx * plan.ly // LANES
+    for o in range(plan.planes):
+        field_ref[pl.ds(plan.zc * (me ^ o), plan.zc), :] = chunks[o][...]
+    stores = []
+    scale = -1.0 / (1.0 + damping * damping)
     for t in range(tiles):
         h, m = [], []
         for c in range(3):
             at = (c * tiles + t) * LANES
             h.append(field_ref[:, at : at + LANES].T + applied_ref[c])
-            m.append(m_ref[c * tiles + t])
+            m.append(m_ref[c, t])
         a = [m[1] * h[2] - m[2] * h[1], m[2] * h[0] - m[0] * h[2], m[0] * h[1] - m[1] * h[0]]
         b = [m[1] * a[2] - m[2] * a[1], m[2] * a[0] - m[0] * a[2], m[0] * a[1] - m[1] * a[0]]
-        scale = -1.0 / (1.0 + damping * damping)
         torque = [(a[c] + damping * b[c]) * scale for c in range(3)]
         step = [m[c] + time_step * torque[c] for c in range(3)]
         total = step[0] * step[0] + step[1] * step[1] + step[2] * step[2]
         inverse = lax.rsqrt(total)
         for c in range(3):
-            torque_ref[c * tiles + t] = torque[c]
-            pred_ref[c * tiles + t] = step[c] * inverse
+            torque_ref[c, t] = torque[c]
+            pred_ref[c, t] = step[c] * inverse
+        stores.append(fetch(torque_ref.at[:, t], torque_hbm.at[:, t], sem_out.at[0, t]))
+        stores.append(fetch(pred_ref.at[:, t], pred_hbm.at[:, t], sem_out.at[1, t]))
+    for store in stores:
+        store.wait()
 
 
 def lattice_eigen(wave_index, length):
     return 2.0 * jnp.cos(wave_index.astype(jnp.float32) * (2.0 * math.pi / length)) - 2.0
 
 
-def tensor_rows(plan, kernel):
-    gx, gz = (lax.axis_index(a) for a in ("gx", "gz"))
-    group = gx * plan.cz + gz
-    kzs = kernel.shape[2]
+def tensor_pick_kernel(plan, k_hbm, own_ref, give_ref, k_ref, sem):
+    parts = 6
+    loads = [fetch(k_hbm.at[i], k_ref.at[i], sem.at[i]) for i in range(parts)]
+    group = lax.axis_index("gx") * plan.cz + lax.axis_index("gz")
+    low = lax.axis_index("gy") == 0
+    sub = lax.broadcasted_iota(jnp.int32, (SUBS, k_ref.shape[3]), 0)
+    top = sub == 0
+    edge = jnp.zeros(sub.shape, jnp.float32)
+    tile = lambda i, j, t: k_ref[i, j, SUBS * t : SUBS * (t + 1), :]
+    for i in range(parts):
+        loads[i].wait()
+        edge = jnp.where(sub == i, pltpu.roll(tile(i, 0, 4), i, 0), edge)
+        for j in range(4):
+            far = 4 * group + j > plan.ny // 2
+            values = [
+                jnp.where(top & far, tile(i, j, 4), tile(i, j, 0)),
+                tile(i, j, 2),
+                jnp.where(top, tile(i, j, 1), tile(i, j, 4)),
+                jnp.where(top, tile(i, j, 3), tile(i, j, 6)),
+            ]
+            for k2l in range(2):
+                row = ((i * 4 + j) * 2 + k2l) * SUBS
+                own_ref[row : row + SUBS, :] = jnp.where(low, values[k2l], values[2 + k2l])
+                give_ref[row : row + SUBS, :] = jnp.where(low, values[2 + k2l], values[k2l])
+    row = parts * 4 * 2 * SUBS
+    own_ref[row : row + SUBS, :] = edge
+    give_ref[row : row + SUBS, :] = edge
+
+
+def tensor_pick(plan, kernel):
+    rows = pltpu.VMEM((6 * 4 * 2 * SUBS + SUBS, kernel.shape[2]), jnp.float32)
     kt = jnp.swapaxes(kernel, 2, 3)
-    ky = 4 * group + jnp.arange(4)
-    packed = jnp.where((ky <= plan.ny // 2)[None, :, None, None], kt[:, :, 0:1], kt[:, :, 32:33])
-    cols = [
-        jnp.concatenate([packed, kt[:, :, 1:8]], 2),
-        jnp.concatenate([kt[:, :, 16:24]], 2),
-        jnp.concatenate([kt[:, :, 8:9], kt[:, :, 33:40]], 2),
-        jnp.concatenate([kt[:, :, 24:25], kt[:, :, 49:56]], 2),
-    ]
-    send = jnp.stack([jnp.stack(cols[0:2], 2), jnp.stack(cols[2:4], 2)])
-    edge = jnp.stack([kt[:, 0, 32]] * 2)
-    rows = send.reshape(2, 6 * 4 * 2 * 8, kzs)
-    return jnp.concatenate([rows, edge], 1)
-
-
-def field_tensor(plan, rows):
+    return call(
+        lambda *a: tensor_pick_kernel(plan, *a),
+        "h",
+        (rows, rows),
+        [pltpu.VMEM(kt.shape, jnp.float32), pltpu.SemaphoreType.DMA((6,))],
+    )(kt)
+
+
+def field_tensor(plan, own, other):
     gx, gy, gz = (lax.axis_index(a) for a in ("gx", "gy", "gz"))
     group = gx * plan.cz + gz
-    kzs = rows.shape[2]
-    own = lax.dynamic_index_in_dim(rows, gy, 0)
-    other = lax.dynamic_index_in_dim(rows, 1 - gy, 0)
+    kzs = own.shape[1]
     other = lax.ppermute(other, "gy", [(0, 1), (1, 0)])
+    own, other = own[None], other[None]
     got = jnp.where(gy == 0, jnp.concatenate([own, other]), jnp.concatenate([other, own]))
     main = got[:, : 6 * 4 * 2 * 8].reshape(2, 6, 2, 2, 2, 8, kzs // 32, 32)
     main = jnp.transpose(main, (1, 7, 3, 4, 2, 5, 0, 6)).reshape(6, 32, 8, 128)
-    edge = got[:, 6 * 4 * 2 * 8 :].reshape(2, 6, kzs // 32, 32)
+    edge = got[:, 6 * 4 * 2 * 8 : 6 * 4 * 2 * 8 + 6].reshape(2, 6, kzs // 32, 32)
     edge = jnp.transpose(edge, (1, 3, 0, 2)).reshape(6, 32, plan.zc)
     kz = jnp.arange(plan.nz).reshape(plan.zc, 32).T
-    table = np.array([[slot_kx(plan, k2, s) for s in range(SLOTS)] for k2 in range(4)])
+    table = np.array([[slot_kx(k2, s) for s in range(SLOTS)] for k2 in range(4)])
     kx = jnp.asarray(table.reshape(2, 2, SLOTS), jnp.int32)[gy]
     kyq = (4 * group + 2 * jnp.arange(2)[None, :] + jnp.arange(2)[:, None])
     kx_full = jnp.broadcast_to(kx[None, :, None, :], (2, 2, 2, SLOTS))
@@ -622,29 +689,52 @@
     return tensor, edge, mask
 
 
-def call(body, outs, scratch=(), name=None, smem=()):
+def call(body, places, outs, scratch):
+    spaces = {"h": pltpu.HBM, "v": pltpu.VMEM, "s": pltpu.SMEM}
+
+    def space_of(out):
+        return pltpu.VMEM if isinstance(out, pl.MemoryRef) else pl.ANY
+
+    step = pl.pallas_call(
+        body,
+        out_shape=outs,
+        in_specs=[pl.BlockSpec(memory_space=spaces[p]) for p in places],
+        out_specs=jax.tree.map(lambda o: pl.BlockSpec(memory_space=space_of(o)), outs),
+        scratch_shapes=scratch,
+        compiler_params=pltpu.CompilerParams(vmem_limit_bytes=8 * 2**20),
+    )
+
     def run(*args):
-        specs = [
-            pl.BlockSpec(memory_space=pltpu.SMEM if i in smem else pltpu.VMEM)
-            for i in range(len(args))
-        ]
-        return pl.pallas_call(
-            body,
-            out_shape=outs,
-            in_specs=specs,
-            out_specs=jax.tree.map(lambda _: pl.BlockSpec(memory_space=pltpu.VMEM), outs),
-            scratch_shapes=list(scratch),
-            name=name,
-            compiler_params=pltpu.CompilerParams(vmem_limit_bytes=56 * 2**20),
-        )(*args)
+        return step(
+            *(
+                x if p == "s" else pltpu.with_memory_space_constraint(x, spaces[p])
+                for p, x in zip(places, args)
+            )
+        )
 
     return run
 
 
+SEND_ORDER = (7, 4, 1, 5, 6, 3, 2)
+
+
+def plane_swap(plan, chunks):
+    members = range(plan.planes)
+    out = list(chunks)
+    for o in SEND_ORDER:
+        out[o] = lax.ppermute(chunks[o], ("gx", "gy"), [(k, k ^ o) for k in members])
+    return out
+
+
+def on_chip(like, *tables):
+    there = like > -jnp.inf
+    return [jnp.where(there, t, jnp.zeros((), t.dtype)) for t in tables]
+
+
 def fast_shards(plan, magnetization, kernel, applied):
-    f32 = jnp.float32
-    sds = jax.ShapeDtypeStruct
-    n, zc = plan.devices, plan.zc
+    f32, bf16 = jnp.float32, jnp.bfloat16
+    sds, vmem, dma = jax.ShapeDtypeStruct, pltpu.VMEM, pltpu.SemaphoreType.DMA
+    n, zc, planes = plan.devices, plan.zc, plan.planes
     width = 3 * plan.lx * plan.ly
     tiles = width // LANES
     fwd, back = xy_tables(plan)
@@ -653,44 +743,67 @@
     tw = x_twiddles(plan)
     ztw, zf, zb = z_tables(plan)
     zf, zb = split_table(zf, 0), split_table(zb, 0)
+    chunk = vmem((zc, width), f32)
+    spectrum = (n, 6, SUBS, LANES)
     m_tiles = magnetization.reshape(tiles, LANES, LANES)
-    packed = call(pack_kernel, sds((plan.lz, width), f32), name="pack")(m_tiles)
-    packed, kernel = lax.optimization_barrier((packed, kernel))
-    tensor, edge, mask = field_tensor(plan, tensor_rows(plan, kernel))
-    lines = lax.all_to_all(
-        packed.reshape(plan.planes, zc, width), ("gx", "gy"), split_axis=0, concat_axis=0, tiled=True
-    )
+    packed = call(
+        lambda *a: pack_kernel(plan, *a),
+        "h",
+        [chunk] * planes,
+        [vmem((tiles, LANES, LANES), f32), vmem((plan.lz, width), f32), dma((3,))],
+    )(m_tiles)
+    first, kernel = lax.optimization_barrier((packed[0], kernel))
+    packed = [first, *packed[1:]]
+    own, other = tensor_pick(plan, kernel)
+    *fwd, x_tw = on_chip(own[0, 0], *fwd, tw)
+    tensor, edge, mask = field_tensor(plan, own, other)
+    ztw, zf, zb = on_chip(tensor[0, 0, 0, 0], ztw, zf, zb)
+    lines = plane_swap(plan, packed)
     spec = call(
         lambda *a: xy_forward_kernel(plan, *a),
-        sds((n, 6, SUBS, LANES), f32),
-        [pltpu.VMEM((2, 3, LANES, 512), jnp.bfloat16), pltpu.VMEM((2, LANES, 512), jnp.bfloat16)],
-        name="xy_forward",
-    )(lines, *fwd, tw)
+        "v" * planes + "vvv",
+        vmem(spectrum, f32),
+        [
+            vmem((planes, zc, width), f32),
+            vmem((2, 3, LANES, 512), bf16),
+            vmem((2, LANES, 512), bf16),
+        ],
+    )(*lines, *fwd, x_tw)
     spec = lax.all_to_all(spec, ("gz", "gx", "gy"), split_axis=0, concat_axis=0, tiled=True)
     spec = call(
         lambda *a: z_kernel(plan, *a),
-        sds((n, 6, SUBS, LANES), f32),
-        [pltpu.VMEM((4, n * SUBS, 256), f32), pltpu.VMEM((n, SUBS, LANES), f32)],
-        name="z_step",
+        "vvvvvvv",
+        vmem(spectrum, f32),
+        [
+            vmem((4, n * SUBS, 256), f32),
+            vmem((n, SUBS, LANES), f32),
+        ],
     )(spec, tensor, edge, mask, ztw, zf, zb)
     spec = lax.all_to_all(spec, ("gz", "gx", "gy"), split_axis=0, concat_axis=0, tiled=True)
     field = call(
         lambda *a: xy_inverse_kernel(plan, *a),
-        sds((plan.planes, zc, width), f32),
+        "vvvv",
+        [chunk] * planes,
         [
-            pltpu.VMEM((3, 2, 256, LANES), f32),
-            pltpu.VMEM((2, 3 * LANES, 512), jnp.bfloat16),
-            pltpu.VMEM((2, 3 * LANES, 256), f32),
+            vmem((3, 2, 256, LANES), f32),
+            vmem((2, 3 * LANES, 512), bf16),
+            vmem((2, 3 * LANES, 256), f32),
+            vmem((planes, zc, width), f32),
         ],
-        name="xy_inverse",
     )(spec, *back, tw)
-    field = lax.all_to_all(field, ("gx", "gy"), split_axis=0, concat_axis=0, tiled=True)
+    field = plane_swap(plan, field)
+    cells = (3, tiles // 3, LANES, LANES)
     pred, torque = call(
         lambda *a: finish_kernel(plan, *a),
-        (sds(m_tiles.shape, f32), sds(m_tiles.shape, f32)),
-        name="finish",
-        smem=(2,),
-    )(field.reshape(plan.lz, width), m_tiles, applied)
+        "v" * planes + "vs",
+        (sds(cells, f32), sds(cells, f32)),
+        [
+            vmem((plan.lz, width), f32),
+            vmem(cells, f32),
+            vmem(cells, f32),
+            dma((2, tiles // 3)),
+        ],
+    )(*field, magnetization.reshape(cells), applied)
     return pred.reshape(magnetization.shape), torque.reshape(magnetization.shape)
 
 

time: 101 us -> 93.7 us (0.928)
  blocking collectives: 40.1 us -> 24 us
  starting transfers between devices: 12.3 us -> 24.4 us
  Pallas kernels: 16.3 us -> 9.36 us
  waiting for transfers between devices: 13.7 us -> 16.2 us
  between operations: 0.96 us -> 2.25 us
    all_to_all x1 -> x0, blocking collectives: 15.8 us -> none  [fast_shards(): lax.all_to_all(field, ('gx', 'gy'), split_axis=0, concat_axis=0, tiled=True)]
    ppermute x0 -> x14, starting transfers between devices: none -> 15.5 us  [plane_swap(): lax.ppermute(chunks[o], ('gx', 'gy'), [(k, k ^ o) for k in members])]
    ppermute x0 -> x14, waiting for transfers between devices: none -> 8.57 us  [plane_swap(): lax.ppermute(chunks[o], ('gx', 'gy'), [(k, k ^ o) for k in members])]
    pallas_call x5 -> x6, Pallas kernels: 16.3 us -> 9.36 us  [run(): step(*(x if p == 's' else pltpu.with_memory_space_constraint(x, spaces[p]...]
    all_to_all x1 -> x0, starting transfers between devices: 5.2 us -> none  [fast_shards(): lax.all_to_all(packed.reshape(plan.planes, zc, width), ('gx', 'gy'), spli...]
    reshape x1 -> x2, local copies, waits for them, and re-layouts: 1.8 us -> 6.22 us  [field_tensor(): main = got[:, :6 * 4 * 2 * 8].reshape(2, 6, 2, 2, 2, 8, kzs // 32, 32)]
    all_to_all x1 -> x0, waiting for transfers between devices: 3.84 us -> none  [fast_shards(): lax.all_to_all(packed.reshape(plan.planes, zc, width), ('gx', 'gy'), spli...]
    select_n x1 -> x4, other arithmetic: 0.08 us -> 3.81 us  [on_chip(): return [jnp.where(there, t, jnp.zeros((), t.dtype)) for t in tables]]
  transfers between devices with their start and end apart: 3 -> 16, of which waited for: 2 -> 8; matrix products, arithmetic and copies ran while one was open for 16% -> 17% of each run, Pallas kernels for 4% -> 4%
where the time goes in v2:
time: 93.7 us; the launch traced here: 93.3 us
  starting transfers between devices  24.4 us (26%)
  blocking collectives  24 us (26%)
  waiting for transfers between devices  16.2 us (17%)
  local copies, waits for them, and re-layouts  12.5 us (13%)
  Pallas kernels  9.36 us (10%)
  other arithmetic  4.56 us (5%)
  between operations  2.25 us (2%)
    all_to_all x1, blocking collectives, fast_shards(): lax.all_to_all(spec, ('gz', 'gx', 'gy'), split_axis=0, concat_axis=0, til...  24 us
    ppermute x14, starting transfers between devices, plane_swap(): lax.ppermute(chunks[o], ('gx', 'gy'), [(k, k ^ o) for k in members])  15.5 us
    pallas_call x6, Pallas kernels, run(): step(*(x if p == 's' else pltpu.with_memory_space_constraint(x, spaces[p]...  9.36 us
    ppermute x14, waiting for transfers between devices, plane_swap(): lax.ppermute(chunks[o], ('gx', 'gy'), [(k, k ^ o) for k in members])  8.57 us
    all_to_all x1, waiting for transfers between devices, fast_shards(): lax.all_to_all(spec, ('gz', 'gx', 'gy'), split_axis=0, concat_axis=0, til...  7.57 us
    all_to_all x1, starting transfers between devices, fast_shards(): lax.all_to_all(spec, ('gz', 'gx', 'gy'), split_axis=0, concat_axis=0, til...  6.95 us
    reshape x2, local copies, waits for them, and re-layouts, field_tensor(): main = got[:, :6 * 4 * 2 * 8].reshape(2, 6, 2, 2, 2, 8, kzs // 32, 32)  6.22 us
    select_n x4, other arithmetic, on_chip(): return [jnp.where(there, t, jnp.zeros((), t.dtype)) for t in tables]  3.81 us
  transfers between devices with their start and end apart: 16, of which 8 were waited for; matrix products, arithmetic and copies ran while one was open for 17% of the time, Pallas kernels for 4%

profile of v2, /device:TPU:0, one launch (start us, length us, event | category | flops | bytes accessed | tf_op | source)
XLA Modules:
  0.0 93.3 jit_solution(14947481342892012655)
XLA Ops:
  0.7 1.5 %shard_map.158 = (f32[16,1536]{1,0:T(8,128)S(1)}, f32[16,1536]{1,0:T(8,128)S(1)}, f32[16,1536]{1,0:T(8,128)S(1)}, f32[16,1536]{1,0:T(8,128)S(1)}, f32[16,1536]{1...) custom-call(f32[12,128,128]{2,1,0:T(8,128)} %bitcast.26), custom_call_target="tpu_custom_call" | custom-call | tf_op jit(solution)/shard_map/pallas_call | solution.py:708
  2.2 3.1 %collective-permute-start = (f32[16,1536]{1,0:T(8,128)S(1)}, f32[16,1536]{1,0:T(8,128)S(1)}, u32[]{:S(2)}, u32[]{:S(2)}) collective-permute-start(f32[16,1536]{1,0:T(8,128)S(1)} %get-tuple-element.26), channel_id=1, source_target_pairs={{0,4},{4,0},{8,12},{12,8},{16,20},{20,16},{24,28},{28,24},{1,5},{5... | collective-permute-start | bytes 294920 | tf_op jit(solution)/shard_map/ppermute | solution.py:725
  5.2 0.2 collective-permute-start.2
  5.4 1.9 %collective-permute-start.3 = (f32[16,1536]{1,0:T(8,128)S(1)}, f32[16,1536]{1,0:T(8,128)S(1)}, u32[]{:S(2)}, u32[]{:S(2)}) collective-permute-start(f32[16,1536]{1,0:T(8,128)S(1)} %get-tuple-element.29), channel_id=1, source_target_pairs={{0,16},{4,20},{8,24},{12,28},{16,0},{20,4},{24,8},{28,12},{1,17},{... | collective-permute-start | bytes 294920 | tf_op jit(solution)/shard_map/ppermute | solution.py:725
  7.3 1.5 %collective-permute-start.4 = (f32[16,1536]{1,0:T(8,128)S(1)}, f32[16,1536]{1,0:T(8,128)S(1)}, u32[]{:S(2)}, u32[]{:S(2)}) collective-permute-start(f32[16,1536]{1,0:T(8,128)S(1)} %get-tuple-element.30), channel_id=1, source_target_pairs={{0,20},{4,16},{8,28},{12,24},{16,4},{20,0},{24,12},{28,8},{1,21},{... | collective-permute-start | bytes 294920 | tf_op jit(solution)/shard_map/ppermute | solution.py:725
  9.1 0.1 and.84
  9.2 0.1 add.133
  9.4 0.7 dynamic-slice_bitcast_fusion
  10.1 0.1 add_add_fusion
  10.3 0.1 add.137
  10.5 1.4 %shard_map.159 = (f32[392,256]{1,0:T(8,128)S(1)}, f32[392,256]{1,0:T(8,128)S(1)}) custom-call(f32[6,4,64,256]{3,2,1,0:T(8,128)} %bitcast.30), custom_call_target="tpu_custom_call" | custom-call | tf_op jit(solution)/shard_map/pallas_call | solution.py:708
  11.9 0.5 slice.12
  13.1 0.7 broadcast_select_fusion.5.a_10_
  13.8 1.2 %broadcast_select_fusion = (bf16[2,256,768]{2,1,0:T(8,128)(2,1)S(1)}, bf16[2,256,768]{2,1,0:T(8,128)(2,1)S(1)}) fusion(bf16[2,256,768]{2,1,0:T(8,128)(2,1)S(1)} %copy-done.6, pred[]{:T(512)} %bitcast.2, bf16[2,256,768]{2,1,0:T(8,128)(2,1)} %constant.90.clone), kind=kLoop, calls=%fused_computation.3 | loop fusion | flops 786432 | bytes 3145729 | tf_op jit(solution)/shard_map/jit(_where)/select_n | solution.py:731
  15.1 0.6 collective-permute-start.5
  15.7 0.7 collective-permute-start.6
  16.4 1.9 %collective-permute-start.7 = (f32[392,256]{1,0:T(8,128)S(1)}, f32[392,256]{1,0:T(8,128)S(1)}, u32[]{:S(2)}, u32[]{:S(2)}) collective-permute-start(f32[392,256]{1,0:T(8,128)S(1)} %get-tuple-element.35), channel_id=1, source_target_pairs={{0,4},{4,0},{1,5},{5,1},{2,6},{6,2},{3,7},{7,3},{8,12},{12,8},{9,1... | collective-permute-start | bytes 1204232 | tf_op jit(solution)/shard_map/ppermute | solution.py:656
  18.3 1.8 %collective-permute-done.5.a_6_ = f32[16,1536]{1,0:T(8,128)S(1)} collective-permute-done((f32[16,1536]{1,0:T(8,128)S(1)}, f32[16,1536]{1,0:T(8,128)S(1)}, u32[]{:S(2)}, u32[]{:S(2)}) %collective-permute-start.5) | collective-permute-done | bytes 98336 | tf_op jit(solution)/shard_map/ppermute | solution.py:725
  20.2 0.7 collective-permute-done.6.a_7_
  20.9 2.1 %shard_map.160 = f32[32,6,8,128]{3,2,1,0:T(8,128)} custom-call(f32[16,1536]{1,0:T(8,128)S(1)} %get-tuple-element.25.a_0_, f32[16,1536]{1,0:T(8,128)S(1)} %collective-permute-done.a_1_, f32[16,1536]{1,0:T(8,128)S(1)} %collective-permute-done.1.a_2_, f32[16,1536]{1,0:T(8,128)S(1)} %collective-permute-done.2.a_3_, f32[16,1536]{1,0:T(8,128)S(1)} %collective-permute-done.3.a_4_, ...), custom_call_target="tpu_custom_call" | custom-call | tf_op jit(solution)/shard_map/pallas_call | solution.py:708
  23.0 7.0 %all-to-all-start = ((f32[32,6,8,128]{3,2,1,0:T(8,128)}), f32[32,6,8,128]{3,2,1,0:T(8,128)S(1)}, u32[]{:S(2)}, u32[]{:S(2)}) async-start(f32[32,6,8,128]{3,2,1,0:T(8,128)} %shard_map.160), calls=%async_computation | async-start | bytes 1572864 | tf_op jit(solution)/shard_map/all_to_all | solution.py:772
  30.0 0.1 and_select_fusion.a_3_
  30.3 0.1 reshape.220
  30.4 0.6 gather_fusion
  31.0 0.1 copy.22
  31.1 2.4 %reshape.218 = f32[2,6,2,2,2,8,8,32]{7,6,5,4,3,2,1,0:T(8,128)} reshape(f32[2,384,256]{2,1,0:T(8,128)S(1)} %slice.18) | data formatting | bytes 1572864 | tf_op jit(solution)/shard_map/reshape | solution.py:659
  33.5 3.9 %copy.19 = f32[2,6,2,2,2,8,8,32]{7,6,0,5,2,4,3,1:T(8,128)} copy(f32[2,6,2,2,2,8,8,32]{7,6,5,4,3,2,1,0:T(8,128)} %reshape.218) | data formatting | bytes 1572864 | tf_op jit(solution)/shard_map/reshape | solution.py:659
  37.4 2.4 %copy.20 = f32[6,32,8,128]{3,2,1,0:T(8,128)S(1)} copy(f32[6,32,8,128]{1,3,2,0:T(8,128)} %bitcast.29) | data formatting | bytes 1572864 | tf_op jit(solution)/shard_map/reshape | solution.py:660
  39.7 0.1 subtract_multiply_fusion.a_1_
  39.9 0.5 slice.20
  41.1 0.6 broadcast_select_fusion.4.a_4_
  41.7 1.2 %broadcast_select_fusion.2 = (bf16[768,256]{1,0:T(8,128)(2,1)S(1)}, bf16[768,256]{1,0:T(8,128)(2,1)S(1)}) fusion(bf16[768,256]{1,0:T(8,128)(2,1)} %constant.99.clone, pred[]{:T(512)} %bitcast.14, bf16[768,256]{1,0:T(8,128)(2,1)} %constant.98.clone), kind=kLoop, calls=%fused_computation.5 | loop fusion | flops 393216 | bytes 1572865 | tf_op jit(solution)/shard_map/jit(_where)/select_n | solution.py:731
  43.0 7.6 %all-to-all-done.a_0_ = f32[32,6,8,128]{3,2,1,0:T(8,128)S(1)} async-done(((f32[32,6,8,128]{3,2,1,0:T(8,128)}), f32[32,6,8,128]{3,2,1,0:T(8,128)S(1)}, u32[]{:S(2)}, u32[]{:S(2)}) %all-to-all-start) | async-done | bytes 786464 | tf_op jit(solution)/shard_map/all_to_all | solution.py:772
  50.5 0.8 copy-done.3
  51.4 1.5 %shard_map.161 = f32[32,6,8,128]{3,2,1,0:T(8,128)S(1)} custom-call(f32[32,6,8,128]{3,2,1,0:T(8,128)S(1)} %all-to-all-done.a_0_, f32[6,32,8,128]{3,2,1,0:T(8,128)S(1)} %subtract_multiply_fusion.a_1_, f32[3,32,8,128]{3,2,1,0:T(8,128)S(1)} %pad.4.a_2_, f32[8,128]{1,0:T(8,128)S(1)} %and_select_fusion.a_3_, f32[2,32,128]{2,1,0:T(8,128)S(1)} %copy-done.3, ...), custom_call_target="tpu_custom_call" | custom-call | tf_op jit(solution)/shard_map/pallas_call | solution.py:708
  52.9 24.0 %all_to_all.10.a_0_ = f32[32,6,8,128]{3,2,1,0:T(8,128)S(1)} all-to-all(f32[32,6,8,128]{3,2,1,0:T(8,128)S(1)} %shard_map.161), channel_id=1, replica_groups=mesh['gx'=4,'gy'=2,'gz'=4] {'gz','gx','gy'}, dimensions={0} | all-to-all | bytes 1572864 | tf_op jit(solution)/shard_map/all_to_all | solution.py:782
  76.9 0.8 shard_map.162
  77.7 1.6 %collective-permute-start.8 = (f32[16,1536]{1,0:T(8,128)S(1)}, f32[16,1536]{1,0:T(8,128)S(1)}, u32[]{:S(2)}, u32[]{:S(2)}) collective-permute-start(f32[16,1536]{1,0:T(8,128)S(1)} %get-tuple-element.37), channel_id=1, source_target_pairs={{0,4},{4,0},{8,12},{12,8},{16,20},{20,16},{24,28},{28,24},{1,5},{5... | collective-permute-start | bytes 294920 | tf_op jit(solution)/shard_map/ppermute | solution.py:725
  79.3 0.7 collective-permute-start.10
  79.9 1.5 %collective-permute-start.11 = (f32[16,1536]{1,0:T(8,128)S(1)}, f32[16,1536]{1,0:T(8,128)S(1)}, u32[]{:S(2)}, u32[]{:S(2)}) collective-permute-start(f32[16,1536]{1,0:T(8,128)S(1)} %get-tuple-element.40), channel_id=1, source_target_pairs={{0,16},{4,20},{8,24},{12,28},{16,0},{20,4},{24,8},{28,12},{1,17},{... | collective-permute-start | bytes 294920 | tf_op jit(solution)/shard_map/ppermute | solution.py:725
  81.5 1.4 %collective-permute-start.12 = (f32[16,1536]{1,0:T(8,128)S(1)}, f32[16,1536]{1,0:T(8,128)S(1)}, u32[]{:S(2)}, u32[]{:S(2)}) collective-permute-start(f32[16,1536]{1,0:T(8,128)S(1)} %get-tuple-element.41), channel_id=1, source_target_pairs={{0,20},{4,16},{8,28},{12,24},{16,4},{20,0},{24,12},{28,8},{1,21},{... | collective-permute-start | bytes 294920 | tf_op jit(solution)/shard_map/ppermute | solution.py:725
  82.9 0.6 collective-permute-done.8.a_1_
  83.5 0.2 collective-permute-start.13
  83.6 2.2 %collective-permute-start.14 = (f32[16,1536]{1,0:T(8,128)S(1)}, f32[16,1536]{1,0:T(8,128)S(1)}, u32[]{:S(2)}, u32[]{:S(2)}) collective-permute-start(f32[16,1536]{1,0:T(8,128)S(1)} %get-tuple-element.43), channel_id=1, source_target_pairs={{0,28},{4,24},{8,20},{12,16},{16,12},{20,8},{24,4},{28,0},{1,29},{... | collective-permute-start | bytes 294920 | tf_op jit(solution)/shard_map/ppermute | solution.py:725
  85.8 2.5 %collective-permute-done.12.a_5_ = f32[16,1536]{1,0:T(8,128)S(1)} collective-permute-done((f32[16,1536]{1,0:T(8,128)S(1)}, f32[16,1536]{1,0:T(8,128)S(1)}, u32[]{:S(2)}, u32[]{:S(2)}) %collective-permute-start.12) | collective-permute-done | bytes 98336 | tf_op jit(solution)/shard_map/ppermute | solution.py:725
  88.3 0.3 collective-permute-done.13.a_6_
  88.6 2.7 %collective-permute-done.14.a_7_ = f32[16,1536]{1,0:T(8,128)S(1)} collective-permute-done((f32[16,1536]{1,0:T(8,128)S(1)}, f32[16,1536]{1,0:T(8,128)S(1)}, u32[]{:S(2)}, u32[]{:S(2)}) %collective-permute-start.14) | collective-permute-done | bytes 98336 | tf_op jit(solution)/shard_map/ppermute | solution.py:725
  91.3 2.0 %shard_map.163 = (f32[3,4,128,128]{3,2,1,0:T(8,128)}, f32[3,4,128,128]{3,2,1,0:T(8,128)}) custom-call(f32[16,1536]{1,0:T(8,128)S(1)} %get-tuple-element.36.a_0_, f32[16,1536]{1,0:T(8,128)S(1)} %collective-permute-done.8.a_1_, f32[16,1536]{1,0:T(8,128)S(1)} %collective-permute-done.9.a_2_, f32[16,1536]{1,0:T(8,128)S(1)} %collective-permute-done.10.a_3_, ...), custom_call_target="tpu_custom_call" | custom-call | tf_op jit(solution)/shard_map/pallas_call | solution.py:708
  (55 shorter events, 0.8 us)
Async XLA Ops:
  0.6 13.1 %copy-start.6 = (bf16[2,256,768]{2,1,0:T(8,128)(2,1)S(1)}, bf16[2,256,768]{2,1,0:T(8,128)(2,1)}, u32[]{:S(2)}) copy-start(bf16[2,256,768]{2,1,0:T(8,128)(2,1)} %constant.91.clone) | copy-start | bytes 2359300
  0.6 14.4 %copy-start.9 = (s32[9]{0:T(128)S(1)}, s32[9]{0:T(128)}, u32[]{:S(2)}) copy-start(s32[9]{0:T(128)} %constant.106) | copy-start | bytes 112
  2.2 12.9 %collective-permute-start = (f32[16,1536]{1,0:T(8,128)S(1)}, f32[16,1536]{1,0:T(8,128)S(1)}, u32[]{:S(2)}, u32[]{:S(2)}) collective-permute-start(f32[16,1536]{1,0:T(8,128)S(1)} %get-tuple-element.26), channel_id=1, source_target_pairs={{0,4},{4,0},{8,12},{12,8},{16,20},{20,16},{24,28},{28,24},{1,5},{5... | collective-permute-start | bytes 294920 | tf_op jit(solution)/shard_map/ppermute | solution.py:725
  5.2 10.4 %collective-permute-start.1 = (f32[16,1536]{1,0:T(8,128)S(1)}, f32[16,1536]{1,0:T(8,128)S(1)}, u32[]{:S(2)}, u32[]{:S(2)}) collective-permute-start(f32[16,1536]{1,0:T(8,128)S(1)} %get-tuple-element.27), channel_id=1, source_target_pairs={{0,8},{4,12},{8,0},{12,4},{16,24},{20,28},{24,16},{28,20},{1,9},{5... | collective-permute-start | bytes 294920 | tf_op jit(solution)/shard_map/ppermute | solution.py:725
  5.2 11.2 %collective-permute-start.2 = (f32[16,1536]{1,0:T(8,128)S(1)}, f32[16,1536]{1,0:T(8,128)S(1)}, u32[]{:S(2)}, u32[]{:S(2)}) collective-permute-start(f32[16,1536]{1,0:T(8,128)S(1)} %get-tuple-element.28), channel_id=1, source_target_pairs={{0,12},{4,8},{8,4},{12,0},{16,28},{20,24},{24,20},{28,16},{1,13},{... | collective-permute-start | bytes 294920 | tf_op jit(solution)/shard_map/ppermute | solution.py:725
  5.4 12.9 %collective-permute-start.3 = (f32[16,1536]{1,0:T(8,128)S(1)}, f32[16,1536]{1,0:T(8,128)S(1)}, u32[]{:S(2)}, u32[]{:S(2)}) collective-permute-start(f32[16,1536]{1,0:T(8,128)S(1)} %get-tuple-element.29), channel_id=1, source_target_pairs={{0,16},{4,20},{8,24},{12,28},{16,0},{20,4},{24,8},{28,12},{1,17},{... | collective-permute-start | bytes 294920 | tf_op jit(solution)/shard_map/ppermute | solution.py:725
  7.3 11.0 %collective-permute-start.4 = (f32[16,1536]{1,0:T(8,128)S(1)}, f32[16,1536]{1,0:T(8,128)S(1)}, u32[]{:S(2)}, u32[]{:S(2)}) collective-permute-start(f32[16,1536]{1,0:T(8,128)S(1)} %get-tuple-element.30), channel_id=1, source_target_pairs={{0,20},{4,16},{8,28},{12,24},{16,4},{20,0},{24,12},{28,8},{1,21},{... | collective-permute-start | bytes 294920 | tf_op jit(solution)/shard_map/ppermute | solution.py:725
  15.1 5.1 %collective-permute-start.5 = (f32[16,1536]{1,0:T(8,128)S(1)}, f32[16,1536]{1,0:T(8,128)S(1)}, u32[]{:S(2)}, u32[]{:S(2)}) collective-permute-start(f32[16,1536]{1,0:T(8,128)S(1)} %get-tuple-element.31), channel_id=1, source_target_pairs={{0,24},{4,28},{8,16},{12,20},{16,8},{20,12},{24,0},{28,4},{1,25},{... | collective-permute-start | bytes 294920 | tf_op jit(solution)/shard_map/ppermute | solution.py:725
  15.7 5.2 %collective-permute-start.6 = (f32[16,1536]{1,0:T(8,128)S(1)}, f32[16,1536]{1,0:T(8,128)S(1)}, u32[]{:S(2)}, u32[]{:S(2)}) collective-permute-start(f32[16,1536]{1,0:T(8,128)S(1)} %get-tuple-element.32), channel_id=1, source_target_pairs={{0,28},{4,24},{8,20},{12,16},{16,12},{20,8},{24,4},{28,0},{1,29},{... | collective-permute-start | bytes 294920 | tf_op jit(solution)/shard_map/ppermute | solution.py:725
  16.4 13.7 %collective-permute-start.7 = (f32[392,256]{1,0:T(8,128)S(1)}, f32[392,256]{1,0:T(8,128)S(1)}, u32[]{:S(2)}, u32[]{:S(2)}) collective-permute-start(f32[392,256]{1,0:T(8,128)S(1)} %get-tuple-element.35), channel_id=1, source_target_pairs={{0,4},{4,0},{1,5},{5,1},{2,6},{6,2},{3,7},{7,3},{8,12},{12,8},{9,1... | collective-permute-start | bytes 1204232 | tf_op jit(solution)/shard_map/ppermute | solution.py:656
  23.0 7.4 %copy-start.8 = (f32[6]{0:T(128)S(1)}, f32[6]{0:T(128)}, u32[]{:S(2)}) copy-start(f32[6]{0:T(128)} %constant.94.clone) | copy-start | bytes 76
  23.0 27.5 %all-to-all-start = ((f32[32,6,8,128]{3,2,1,0:T(8,128)}), f32[32,6,8,128]{3,2,1,0:T(8,128)S(1)}, u32[]{:S(2)}, u32[]{:S(2)}) async-start(f32[32,6,8,128]{3,2,1,0:T(8,128)} %shard_map.160), calls=%async_computation | async-start | bytes 1572864 | tf_op jit(solution)/shard_map/all_to_all | solution.py:772
  37.4 3.7 %copy-start.7 = (f32[2,32,128]{2,1,0:T(8,128)S(1)}, f32[2,32,128]{2,1,0:T(8,128)}, u32[]{:S(2)}) copy-start(f32[2,32,128]{2,1,0:T(8,128)} %constant.97.clone) | copy-start | bytes 98308
  41.7 35.2 %copy-start.1 = (bf16[2,768,256]{2,1,0:T(8,128)(2,1)S(1)}, bf16[2,768,256]{2,1,0:T(8,128)(2,1)}, u32[]{:S(2)}) copy-start(bf16[2,768,256]{2,1,0:T(8,128)(2,1)} %constant.101.clone.a_2_) | copy-start | bytes 2359300
  41.7 35.2 %copy-start.4 = (f32[2,8,128]{2,1,0:T(8,128)S(1)}, f32[2,8,128]{2,1,0:T(8,128)}, u32[]{:S(2)}) copy-start(f32[2,8,128]{2,1,0:T(8,128)} %constant.92.clone.a_3_) | copy-start | bytes 24580
  50.5 26.4 %copy-start.2 = (bf16[2,768,256]{2,1,0:T(8,128)(2,1)S(1)}, bf16[2,768,256]{2,1,0:T(8,128)(2,1)}, u32[]{:S(2)}) copy-start(bf16[2,768,256]{2,1,0:T(8,128)(2,1)} %constant.100.clone.a_1_) | copy-start | bytes 2359300
  50.5 0.8 copy-start.3
  51.4 39.9 %copy-start = (f32[3,16,32,128]{3,2,1,0:T(8,128)S(1)}, f32[3,16,32,128]{3,2,1,0:T(8,128)}, u32[]{:S(2)}) copy-start(f32[3,16,32,128]{3,2,1,0:T(8,128)} %param.15) | copy-start | bytes 2359300
  51.4 39.9 %copy-start.5 = (f32[3]{0:T(128)S(1)}, f32[3]{0:T(128)}, u32[]{:S(2)}) copy-start(f32[3]{0:T(128)} %a_9_.1) | copy-start | bytes 40
  77.7 5.7 %collective-permute-start.8 = (f32[16,1536]{1,0:T(8,128)S(1)}, f32[16,1536]{1,0:T(8,128)S(1)}, u32[]{:S(2)}, u32[]{:S(2)}) collective-permute-start(f32[16,1536]{1,0:T(8,128)S(1)} %get-tuple-element.37), channel_id=1, source_target_pairs={{0,4},{4,0},{8,12},{12,8},{16,20},{20,16},{24,28},{28,24},{1,5},{5... | collective-permute-start | bytes 294920 | tf_op jit(solution)/shard_map/ppermute | solution.py:725
  79.3 4.3 %collective-permute-start.9 = (f32[16,1536]{1,0:T(8,128)S(1)}, f32[16,1536]{1,0:T(8,128)S(1)}, u32[]{:S(2)}, u32[]{:S(2)}) collective-permute-start(f32[16,1536]{1,0:T(8,128)S(1)} %get-tuple-element.38), channel_id=1, source_target_pairs={{0,8},{4,12},{8,0},{12,4},{16,24},{20,28},{24,16},{28,20},{1,9},{5... | collective-permute-start | bytes 294920 | tf_op jit(solution)/shard_map/ppermute | solution.py:725
  79.3 6.5 %collective-permute-start.10 = (f32[16,1536]{1,0:T(8,128)S(1)}, f32[16,1536]{1,0:T(8,128)S(1)}, u32[]{:S(2)}, u32[]{:S(2)}) collective-permute-start(f32[16,1536]{1,0:T(8,128)S(1)} %get-tuple-element.39), channel_id=1, source_target_pairs={{0,12},{4,8},{8,4},{12,0},{16,28},{20,24},{24,20},{28,16},{1,13},{... | collective-permute-start | bytes 294920 | tf_op jit(solution)/shard_map/ppermute | solution.py:725
  79.9 5.9 %collective-permute-start.11 = (f32[16,1536]{1,0:T(8,128)S(1)}, f32[16,1536]{1,0:T(8,128)S(1)}, u32[]{:S(2)}, u32[]{:S(2)}) collective-permute-start(f32[16,1536]{1,0:T(8,128)S(1)} %get-tuple-element.40), channel_id=1, source_target_pairs={{0,16},{4,20},{8,24},{12,28},{16,0},{20,4},{24,8},{28,12},{1,17},{... | collective-permute-start | bytes 294920 | tf_op jit(solution)/shard_map/ppermute | solution.py:725
  81.5 6.8 %collective-permute-start.12 = (f32[16,1536]{1,0:T(8,128)S(1)}, f32[16,1536]{1,0:T(8,128)S(1)}, u32[]{:S(2)}, u32[]{:S(2)}) collective-permute-start(f32[16,1536]{1,0:T(8,128)S(1)} %get-tuple-element.41), channel_id=1, source_target_pairs={{0,20},{4,16},{8,28},{12,24},{16,4},{20,0},{24,12},{28,8},{1,21},{... | collective-permute-start | bytes 294920 | tf_op jit(solution)/shard_map/ppermute | solution.py:725
  83.5 5.1 %collective-permute-start.13 = (f32[16,1536]{1,0:T(8,128)S(1)}, f32[16,1536]{1,0:T(8,128)S(1)}, u32[]{:S(2)}, u32[]{:S(2)}) collective-permute-start(f32[16,1536]{1,0:T(8,128)S(1)} %get-tuple-element.42), channel_id=1, source_target_pairs={{0,24},{4,28},{8,16},{12,20},{16,8},{20,12},{24,0},{28,4},{1,25},{... | collective-permute-start | bytes 294920 | tf_op jit(solution)/shard_map/ppermute | solution.py:725
  83.6 7.6 %collective-permute-start.14 = (f32[16,1536]{1,0:T(8,128)S(1)}, f32[16,1536]{1,0:T(8,128)S(1)}, u32[]{:S(2)}, u32[]{:S(2)}) collective-permute-start(f32[16,1536]{1,0:T(8,128)S(1)} %get-tuple-element.43), channel_id=1, source_target_pairs={{0,28},{4,24},{8,20},{12,16},{16,12},{20,8},{24,4},{28,0},{1,29},{... | collective-permute-start | bytes 294920 | tf_op jit(solution)/shard_map/ppermute | solution.py:725

commit v3 on v2

--- a/solution.py
+++ b/solution.py
@@ -245,7 +245,16 @@
 def split_table(table, axis):
     high = table.astype(jnp.bfloat16)
     low = (table - high.astype(np.float32)).astype(jnp.bfloat16)
-    return np.concatenate([high, low, high], axis)
+    return np.concatenate([high, low], axis)
+
+
+def high_high_low(value):
+    return jnp.concatenate([value[:, 0:256], value[:, 0:256], value[:, 256:512]], 1)
+
+
+def high_low_high(table, axis):
+    high, low = (lax.slice_in_dim(table, at, at + 256, axis=axis) for at in (0, 256))
+    return jnp.concatenate([high, low, high], axis)
 
 
 def mm(a, b, dims):
@@ -329,23 +338,26 @@
     return fwd.astype(np.float32), back.astype(np.float32)
 
 
-def x_twiddles(plan):
-    xl = np.arange(LANES) // plan.ly
-    ph = 2 * math.pi * np.arange(SLOTS)[:, None] * xl[None, :] / plan.nx
-    return np.stack([np.cos(ph), np.sin(ph)]).astype(np.float32)
+def fill_twiddles(ref, rows, lane_index, length):
+    row = lax.broadcasted_iota(jnp.int32, (rows, LANES), 0)
+    angle = (row * lane_index).astype(jnp.float32) * (2 * math.pi / length)
+    ref[0] = jnp.cos(angle)
+    ref[1] = jnp.sin(angle)
+
+
+def fill_x_twiddles(plan, ref):
+    lane = lax.broadcasted_iota(jnp.int32, (SUBS, LANES), 1)
+    fill_twiddles(ref, SUBS, lane // plan.ly, plan.nx)
 
 
 def z_tables(plan):
-    zc, nz = plan.zc, plan.nz
-    lane = np.arange(LANES) % zc
-    ph = 2 * math.pi * np.arange(plan.devices)[:, None] * lane[None, :] / nz
-    twiddle = np.stack([np.cos(ph), np.sin(ph)]).astype(np.float32)
+    zc = plan.zc
     small = 2 * math.pi * np.arange(zc)[:, None] * np.arange(zc)[None, :] / zc
     c = np.kron(np.eye(SLOTS), np.cos(small))
     s = np.kron(np.eye(SLOTS), np.sin(small))
     fwd = np.block([[c, -s], [s, c]]).astype(np.float32)
     back = np.block([[c, s], [-s, c]]).astype(np.float32)
-    return twiddle, fwd, back
+    return fwd, back
 
 
 def fetch(source, target, sem):
@@ -379,8 +391,9 @@
 
 def xy_forward_kernel(plan, *refs):
     chunks, refs = refs[: plan.planes], refs[plan.planes :]
-    table_ref, edge_ref, tw_ref, out_ref, lines_ref, g_ref, e_ref = refs
+    table_ref, edge_ref, out_ref, lines_ref, g_ref, e_ref, tw_ref = refs
     me = plane_index()
+    fill_x_twiddles(plan, tw_ref)
     for o in range(plan.planes):
         lines_ref[me ^ o] = chunks[o][...]
     zc = plan.zc
@@ -419,12 +432,12 @@
                 keep(g_ref, (r, c), rows, (re * tc + im * ts, im * tc - re * ts))
             g_ref[r, c, 0:zc, :] = jnp.zeros((zc, 512), jnp.bfloat16)
 
-    def widen(value):
-        return jnp.concatenate([value[:, 0:256], value[:, 0:256], value[:, 256:512]], 1)
-
-    edges = [mm(edge_ref[r], widen(e_ref[r]), ((1,), (1,))) for r in range(2)]
+    edges = [mm(high_low_high(edge_ref[r], 1), high_high_low(e_ref[r]), ((1,), (1,))) for r in range(2)]
     for c in range(plan.comps):
-        outs = [mm(table_ref[r], widen(g_ref[r, c]), ((1,), (1,))) for r in range(2)]
+        outs = [
+            mm(high_low_high(table_ref[r], 1), high_high_low(g_ref[r, c]), ((1,), (1,)))
+            for r in range(2)
+        ]
         for k2h in range(2):
             for g in range(plan.groups):
                 f = (k2h * plan.groups + g) * SUBS
@@ -436,14 +449,15 @@
                     both.append(jnp.where(first_slot, edge, outs[r][f : f + SUBS]))
                 one, two = both
                 gx, gz = g // plan.cz, g % plan.cz
-                dest = gz * plan.planes + gx * plan.cy + k2h
+                dest = (gx * plan.cy + k2h) * plan.cz + gz
                 out_ref[dest, 2 * c] = jnp.where(low, one, two)
                 out_ref[dest, 2 * c + 1] = pltpu.roll(jnp.where(low, two, one), 4, 0)
 
 
-def xy_inverse_kernel(plan, spec_ref, table_ref, edge_ref, tw_ref, *refs):
-    outs, (h_ref, t_ref, u_ref, out_ref) = refs[: plan.planes], refs[plan.planes :]
+def xy_inverse_kernel(plan, spec_ref, table_ref, edge_ref, *refs):
+    outs, (h_ref, t_ref, u_ref, out_ref, tw_ref) = refs[: plan.planes], refs[plan.planes :]
     me = plane_index()
+    fill_x_twiddles(plan, tw_ref)
     zc = plan.zc
     per = plan.lx // plan.xl
     low = lax.broadcasted_iota(jnp.int32, (SUBS, LANES), 0) < 4
@@ -452,7 +466,7 @@
             for g in range(plan.groups):
                 f = (k2h * plan.groups + g) * SUBS
                 gx, gz = g // plan.cz, g % plan.cz
-                src = gz * plan.planes + gx * plan.cy + k2h
+                src = (gx * plan.cy + k2h) * plan.cz + gz
                 re = spec_ref[src, 2 * c]
                 im = pltpu.roll(spec_ref[src, 2 * c + 1], 4, 0)
                 h_ref[c, 0, f : f + SUBS, :] = jnp.where(low, re, im)
@@ -462,16 +476,13 @@
             t_ref[r, LANES * c : LANES * (c + 1), 0:256] = hi
             t_ref[r, LANES * c : LANES * (c + 1), 256:512] = lo
 
-    def widen(value):
-        return jnp.concatenate([value[:, 0:256], value[:, 0:256], value[:, 256:512]], 1)
-
     edges = []
     for r in range(2):
-        u_ref[r] = mm(widen(t_ref[r]), table_ref[r], ((1,), (0,)))
+        u_ref[r] = mm(high_high_low(t_ref[r]), high_low_high(table_ref[r], 0), ((1,), (0,)))
         rows = jnp.concatenate(
             [t_ref[r, LANES * c : LANES * c + zc, :] for c in range(plan.comps)], 0
         )
-        edges.append(mm(widen(rows), edge_ref[r], ((1,), (0,))))
+        edges.append(mm(high_high_low(rows), high_low_high(edge_ref[r], 0), ((1,), (0,))))
     for c in range(plan.comps):
         fields = []
         for r in range(2):
@@ -498,17 +509,20 @@
 
 
 def z_kernel(
-    plan, in_ref, k_ref, kx_ref, mask_ref, tw_ref, fwd_ref, back_ref, out_ref, s_ref, b_ref
+    plan, in_ref, k_ref, kx_ref, mask_ref, fwd_ref, back_ref, out_ref, s_ref, b_ref, tw_ref
 ):
     n = plan.devices
+    lane = lax.broadcasted_iota(jnp.int32, (n, LANES), 1)
+    fill_twiddles(tw_ref, n, lane % plan.zc, plan.nz)
     half = n // 2 + 1
     mask = mask_ref[...]
+    place = [(s % plan.planes) * plan.cz + s // plan.planes for s in range(n)]
     keep = 1.0 - mask
 
     def transform(at, count, table):
         hi, lo = split(s_ref[at, 0 : SUBS * count, :])
         wide = jnp.concatenate([hi, hi, lo], 1)
-        s_ref[at, 0 : SUBS * count, :] = mm(wide, table[...], ((1,), (0,)))
+        s_ref[at, 0 : SUBS * count, :] = mm(wide, high_low_high(table[...], 0), ((1,), (0,)))
 
     def to_spectrum(values, at):
         for k, (re, im) in enumerate(values):
@@ -530,13 +544,13 @@
         return values
 
     for c in range(plan.comps):
-        values = [(in_ref[s, 2 * c], in_ref[s, 2 * c + 1] * keep) for s in range(n)]
+        values = [(in_ref[place[s], 2 * c], in_ref[place[s], 2 * c + 1] * keep) for s in range(n)]
         to_spectrum(complex_fft(values, -1), c)
     extra = []
     for s in range(n):
-        e = in_ref[s, 1] * mask
-        e = e + pltpu.roll(in_ref[s, 3] * mask, 1, 0)
-        e = e + pltpu.roll(in_ref[s, 5] * mask, 2, 0)
+        e = in_ref[place[s], 1] * mask
+        e = e + pltpu.roll(in_ref[place[s], 3] * mask, 1, 0)
+        e = e + pltpu.roll(in_ref[place[s], 5] * mask, 2, 0)
         extra.append(e + pltpu.roll(e, 3, 0))
     extra = real_fft(extra)
     zero = jnp.zeros((SUBS, LANES), jnp.float32)
@@ -570,8 +584,8 @@
             e = b_ref[s]
             if c:
                 e = pltpu.roll(e, SUBS - c, 0)
-            out_ref[s, 2 * c] = values[s][0]
-            out_ref[s, 2 * c + 1] = values[s][1] * keep + e * mask
+            out_ref[place[s], 2 * c] = values[s][0]
+            out_ref[place[s], 2 * c + 1] = values[s][1] * keep + e * mask
 
 
 def finish_kernel(plan, *refs):
@@ -662,7 +676,8 @@
     edge = jnp.transpose(edge, (1, 3, 0, 2)).reshape(6, 32, plan.zc)
     kz = jnp.arange(plan.nz).reshape(plan.zc, 32).T
     table = np.array([[slot_kx(k2, s) for s in range(SLOTS)] for k2 in range(4)])
-    kx = jnp.asarray(table.reshape(2, 2, SLOTS), jnp.int32)[gy]
+    table = table.reshape(2, 2, SLOTS).astype(np.int32)
+    kx = jnp.where(gy == 0, table[0], table[1])
     kyq = (4 * group + 2 * jnp.arange(2)[None, :] + jnp.arange(2)[:, None])
     kx_full = jnp.broadcast_to(kx[None, :, None, :], (2, 2, 2, SLOTS))
     swap = (gy == 0) & (kyq > plan.ny // 2)
@@ -679,8 +694,8 @@
     tensor = scale * (exchange_coeff * diag * eig[None] - main)
     edge_eig = lattice_eigen(jnp.asarray(32), plan.nx) + lattice_eigen(4 * group, plan.ny) + ez
     edge = scale * (exchange_coeff * diag[:, :, :, 0] * edge_eig[None] - edge)
-    order = np.array([[0, 1, 2], [3, 5, 4], [4, 3, 5]])
-    edge = edge[order]
+    order = ((0, 1, 2), (3, 5, 4), (4, 3, 5))
+    edge = jnp.stack([jnp.stack([edge[i] for i in row]) for row in order])
     edge = jnp.transpose(edge, (0, 2, 1, 3))
     edge = jnp.pad(edge, ((0, 0), (0, 0), (0, 5), (0, LANES - plan.zc)))
     special = (gy == 0) & ((group == 0) | (group == plan.groups // 2))
@@ -727,7 +742,7 @@
 
 
 def on_chip(like, *tables):
-    there = like > -jnp.inf
+    there = like > -1e30
     return [jnp.where(there, t, jnp.zeros((), t.dtype)) for t in tables]
 
 
@@ -740,8 +755,7 @@
     fwd, back = xy_tables(plan)
     fwd = [split_table(t, 2) for t in (fwd[:, :, 0:256], fwd[:, :, 256:512])]
     back = [split_table(t, 1) for t in (back[:, :, 0:256], back[:, :, 256:512])]
-    tw = x_twiddles(plan)
-    ztw, zf, zb = z_tables(plan)
+    zf, zb = z_tables(plan)
     zf, zb = split_table(zf, 0), split_table(zb, 0)
     chunk = vmem((zc, width), f32)
     spectrum = (n, 6, SUBS, LANES)
@@ -752,45 +766,49 @@
         [chunk] * planes,
         [vmem((tiles, LANES, LANES), f32), vmem((plan.lz, width), f32), dma((3,))],
     )(m_tiles)
-    first, kernel = lax.optimization_barrier((packed[0], kernel))
+    late = lax.axis_index("gy").astype(f32)
+    first, kernel, late = lax.optimization_barrier((packed[0], kernel, late))
     packed = [first, *packed[1:]]
     own, other = tensor_pick(plan, kernel)
-    *fwd, x_tw = on_chip(own[0, 0], *fwd, tw)
+    fwd = on_chip(late, *fwd)
     tensor, edge, mask = field_tensor(plan, own, other)
-    ztw, zf, zb = on_chip(tensor[0, 0, 0, 0], ztw, zf, zb)
+    zf, zb = on_chip(tensor[0, 0, 0, 0], zf, zb)
     lines = plane_swap(plan, packed)
     spec = call(
         lambda *a: xy_forward_kernel(plan, *a),
-        "v" * planes + "vvv",
+        "v" * planes + "vv",
         vmem(spectrum, f32),
         [
             vmem((planes, zc, width), f32),
             vmem((2, 3, LANES, 512), bf16),
             vmem((2, LANES, 512), bf16),
+            vmem((2, SUBS, LANES), f32),
         ],
-    )(*lines, *fwd, x_tw)
-    spec = lax.all_to_all(spec, ("gz", "gx", "gy"), split_axis=0, concat_axis=0, tiled=True)
+    )(*lines, *fwd)
+    spec = lax.all_to_all(spec, ("gx", "gy", "gz"), split_axis=0, concat_axis=0, tiled=True)
     spec = call(
         lambda *a: z_kernel(plan, *a),
-        "vvvvvvv",
+        "vvvvvv",
         vmem(spectrum, f32),
         [
             vmem((4, n * SUBS, 256), f32),
             vmem((n, SUBS, LANES), f32),
+            vmem((2, n, LANES), f32),
         ],
-    )(spec, tensor, edge, mask, ztw, zf, zb)
-    spec = lax.all_to_all(spec, ("gz", "gx", "gy"), split_axis=0, concat_axis=0, tiled=True)
+    )(spec, tensor, edge, mask, zf, zb)
+    spec = lax.all_to_all(spec, ("gx", "gy", "gz"), split_axis=0, concat_axis=0, tiled=True)
     field = call(
         lambda *a: xy_inverse_kernel(plan, *a),
-        "vvvv",
+        "vvv",
         [chunk] * planes,
         [
             vmem((3, 2, 256, LANES), f32),
             vmem((2, 3 * LANES, 512), bf16),
             vmem((2, 3 * LANES, 256), f32),
             vmem((planes, zc, width), f32),
+            vmem((2, SUBS, LANES), f32),
         ],
-    )(spec, *back, tw)
+    )(spec, *back)
     field = plane_swap(plan, field)
     cells = (3, tiles // 3, LANES, LANES)
     pred, torque = call(

time: 93.7 us -> 98.1 us (1.047)
  waiting for transfers between devices: 16.2 us -> 22.7 us
  other arithmetic: 4.56 us -> 6.12 us
  starting transfers between devices: 24.4 us -> 23.2 us
    ppermute x14, waiting for transfers between devices: 8.57 us -> 15.7 us  [plane_swap(): lax.ppermute(chunks[o], ('gx', 'gy'), [(k, k ^ o) for k in members])]
    select_n x4 -> x2, other arithmetic: 3.81 us -> 2.19 us  [on_chip(): return [jnp.where(there, t, jnp.zeros((), t.dtype)) for t in tables]]
    all_to_all x1, starting transfers between devices: 6.95 us -> 5.66 us  [fast_shards(): lax.all_to_all(spec, ('gx', 'gy', 'gz'), split_axis=0, concat_axis=0, til...]
    select_n x1, other arithmetic: 0.05 us -> 1.2 us  [field_tensor(): jnp.where(gy == 0, jnp.concatenate([own, other]), jnp.concatenate([other,...]
    ppermute x1, starting transfers between devices: 1.95 us -> 3.06 us  [field_tensor(): other = lax.ppermute(other, 'gy', [(0, 1), (1, 0)])]
    ppermute x14, starting transfers between devices: 15.5 us -> 14.5 us  [plane_swap(): lax.ppermute(chunks[o], ('gx', 'gy'), [(k, k ^ o) for k in members])]
    pad x1, local copies, waits for them, and re-layouts: 0.04 us -> 1.05 us  [field_tensor(): edge = jnp.pad(edge, ((0, 0), (0, 0), (0, 5), (0, LANES - plan.zc)))]
  transfers between devices with their start and end apart: 16 -> 16, of which waited for: 8 -> 8; matrix products, arithmetic and copies ran while one was open for 17% -> 18% of each run, Pallas kernels for 4% -> 2%
where the time goes in v3:
time: 98.1 us; the launch traced here: 97.6 us
  starting transfers between devices  23.2 us (24%)
  blocking collectives  23.2 us (24%)
  waiting for transfers between devices  22.7 us (23%)
  local copies, waits for them, and re-layouts  11.6 us (12%)
  Pallas kernels  9.36 us (10%)
  other arithmetic  6.12 us (6%)
  between operations  1.53 us (2%)
    all_to_all x1, blocking collectives, fast_shards(): lax.all_to_all(spec, ('gx', 'gy', 'gz'), split_axis=0, concat_axis=0, til...  23.2 us
    ppermute x14, waiting for transfers between devices, plane_swap(): lax.ppermute(chunks[o], ('gx', 'gy'), [(k, k ^ o) for k in members])  15.7 us
    ppermute x14, starting transfers between devices, plane_swap(): lax.ppermute(chunks[o], ('gx', 'gy'), [(k, k ^ o) for k in members])  14.5 us
    pallas_call x6, Pallas kernels, run(): step(*(x if p == 's' else pltpu.with_memory_space_constraint(x, spaces[p]...  9.36 us
    all_to_all x1, waiting for transfers between devices, fast_shards(): lax.all_to_all(spec, ('gx', 'gy', 'gz'), split_axis=0, concat_axis=0, til...  7.01 us
    reshape x2, local copies, waits for them, and re-layouts, field_tensor(): main = got[:, :6 * 4 * 2 * 8].reshape(2, 6, 2, 2, 2, 8, kzs // 32, 32)  6.21 us
    all_to_all x1, starting transfers between devices, fast_shards(): lax.all_to_all(spec, ('gx', 'gy', 'gz'), split_axis=0, concat_axis=0, til...  5.66 us
    ppermute x1, starting transfers between devices, field_tensor(): other = lax.ppermute(other, 'gy', [(0, 1), (1, 0)])  3.06 us
  transfers between devices with their start and end apart: 16, of which 8 were waited for; matrix products, arithmetic and copies ran while one was open for 18% of the time, Pallas kernels for 2%

profile of v3, /device:TPU:0, one launch (start us, length us, event | category | flops | bytes accessed | tf_op | source)
XLA Modules:
  0.0 97.6 jit_solution(2070180515618547305)
XLA Ops:
  0.6 1.5 %shard_map.131 = (f32[16,1536]{1,0:T(8,128)S(1)}, f32[16,1536]{1,0:T(8,128)S(1)}, f32[16,1536]{1,0:T(8,128)S(1)}, f32[16,1536]{1,0:T(8,128)S(1)}, f32[16,1536]{1...) custom-call(f32[12,128,128]{2,1,0:T(8,128)} %bitcast.28), custom_call_target="tpu_custom_call" | custom-call | tf_op jit(solution)/shard_map/pallas_call | solution.py:723
  2.2 1.4 %shard_map.133 = (f32[392,256]{1,0:T(8,128)S(1)}, f32[392,256]{1,0:T(8,128)S(1)}) custom-call(f32[6,4,64,256]{3,2,1,0:T(8,128)} %bitcast.32), custom_call_target="tpu_custom_call" | custom-call | tf_op jit(solution)/shard_map/pallas_call | solution.py:723
  3.6 3.1 %collective-permute-start.7 = (f32[392,256]{1,0:T(8,128)S(1)}, f32[392,256]{1,0:T(8,128)}, u32[]{:S(2)}, u32[]{:S(2)}) collective-permute-start(f32[392,256]{1,0:T(8,128)S(1)} %get-tuple-element.37), channel_id=1, source_target_pairs={{0,4},{4,0},{1,5},{5,1},{2,6},{6,2},{3,7},{7,3},{8,12},{12,8},{9,1... | collective-permute-start | bytes 1204232 | tf_op jit(solution)/shard_map/ppermute | solution.py:670
  6.6 0.1 collective-permute-start
  6.7 2.1 %collective-permute-start.2 = (f32[16,1536]{1,0:T(8,128)S(1)}, f32[16,1536]{1,0:T(8,128)S(1)}, u32[]{:S(2)}, u32[]{:S(2)}) collective-permute-start(f32[16,1536]{1,0:T(8,128)S(1)} %get-tuple-element.29), channel_id=1, source_target_pairs={{0,12},{4,8},{8,4},{12,0},{16,28},{20,24},{24,20},{28,16},{1,13},{... | collective-permute-start | bytes 294920 | tf_op jit(solution)/shard_map/ppermute | solution.py:740
  8.8 1.5 %collective-permute-start.3 = (f32[16,1536]{1,0:T(8,128)S(1)}, f32[16,1536]{1,0:T(8,128)S(1)}, u32[]{:S(2)}, u32[]{:S(2)}) collective-permute-start(f32[16,1536]{1,0:T(8,128)S(1)} %get-tuple-element.30), channel_id=1, source_target_pairs={{0,16},{4,20},{8,24},{12,28},{16,0},{20,4},{24,8},{28,12},{1,17},{... | collective-permute-start | bytes 294920 | tf_op jit(solution)/shard_map/ppermute | solution.py:740
  10.4 0.1 and.84
  10.5 0.1 add.126
  10.7 0.7 broadcast_select_fusion.4
  11.4 0.1 add_add_fusion
  11.5 0.1 add.129
  11.6 0.1 add.130
  11.8 0.7 broadcast_add_fusion
  12.5 1.1 %broadcast_select_fusion = (bf16[2,256,512]{2,1,0:T(8,128)(2,1)S(1)}, bf16[2,256,512]{2,1,0:T(8,128)(2,1)S(1)}) fusion(bf16[2,256,512]{2,1,0:T(8,128)(2,1)} %constant.81.clone, pred[]{:T(512)S(6)} %gt.16, bf16[2,256,512]{2,1,0:T(8,128)(2,1)S(1)} %copy-done.4), kind=kLoop, calls=%fused_computation.2 | loop fusion | flops 524288 | bytes 2097153 | tf_op jit(solution)/shard_map/jit(_where)/select_n | solution.py:746
  13.6 5.3 %collective-permute-done.a_1_ = f32[16,1536]{1,0:T(8,128)S(1)} collective-permute-done((f32[16,1536]{1,0:T(8,128)S(1)}, f32[16,1536]{1,0:T(8,128)S(1)}, u32[]{:S(2)}, u32[]{:S(2)}) %collective-permute-start) | collective-permute-done | bytes 98336 | tf_op jit(solution)/shard_map/ppermute | solution.py:740
  18.9 2.9 %collective-permute-start.4 = (f32[16,1536]{1,0:T(8,128)S(1)}, f32[16,1536]{1,0:T(8,128)S(1)}, u32[]{:S(2)}, u32[]{:S(2)}) collective-permute-start(f32[16,1536]{1,0:T(8,128)S(1)} %get-tuple-element.31), channel_id=1, source_target_pairs={{0,20},{4,16},{8,28},{12,24},{16,4},{20,0},{24,12},{28,8},{1,21},{... | collective-permute-start | bytes 294920 | tf_op jit(solution)/shard_map/ppermute | solution.py:740
  21.8 1.7 %collective-permute-start.6 = (f32[16,1536]{1,0:T(8,128)S(1)}, f32[16,1536]{1,0:T(8,128)S(1)}, u32[]{:S(2)}, u32[]{:S(2)}) collective-permute-start(f32[16,1536]{1,0:T(8,128)S(1)} %get-tuple-element.33), channel_id=1, source_target_pairs={{0,28},{4,24},{8,20},{12,16},{16,12},{20,8},{24,4},{28,0},{1,29},{... | collective-permute-start | bytes 294920 | tf_op jit(solution)/shard_map/ppermute | solution.py:740
  23.5 0.7 and_select_fusion.a_3_
  24.3 0.7 collective-permute-done.4.a_5_
  24.9 2.1 %collective-permute-done.5.a_6_ = f32[16,1536]{1,0:T(8,128)S(1)} collective-permute-done((f32[16,1536]{1,0:T(8,128)S(1)}, f32[16,1536]{1,0:T(8,128)S(1)}, u32[]{:S(2)}, u32[]{:S(2)}) %collective-permute-start.5) | collective-permute-done | bytes 98336 | tf_op jit(solution)/shard_map/ppermute | solution.py:740
  27.0 1.6 %collective-permute-done.6.a_7_ = f32[16,1536]{1,0:T(8,128)S(1)} collective-permute-done((f32[16,1536]{1,0:T(8,128)S(1)}, f32[16,1536]{1,0:T(8,128)S(1)}, u32[]{:S(2)}, u32[]{:S(2)}) %collective-permute-start.6) | collective-permute-done | bytes 98336 | tf_op jit(solution)/shard_map/ppermute | solution.py:740
  28.6 2.1 %shard_map.132 = f32[32,6,8,128]{3,2,1,0:T(8,128)} custom-call(f32[16,1536]{1,0:T(8,128)S(1)} %get-tuple-element.26.a_0_, f32[16,1536]{1,0:T(8,128)S(1)} %collective-permute-done.a_1_, f32[16,1536]{1,0:T(8,128)S(1)} %collective-permute-done.1.a_2_, f32[16,1536]{1,0:T(8,128)S(1)} %collective-permute-done.2.a_3_, f32[16,1536]{1,0:T(8,128)S(1)} %collective-permute-done.3.a_4_, ...), custom_call_target="tpu_custom_call" | custom-call | tf_op jit(solution)/shard_map/pallas_call | solution.py:723
  30.7 5.7 %all-to-all-start = ((f32[32,6,8,128]{3,2,1,0:T(8,128)}), f32[32,6,8,128]{3,2,1,0:T(8,128)S(1)}, u32[]{:S(2)}, u32[]{:S(2)}) async-start(f32[32,6,8,128]{3,2,1,0:T(8,128)} %shard_map.132), calls=%async_computation | async-start | bytes 1572864 | tf_op jit(solution)/shard_map/all_to_all | solution.py:788
  36.5 1.2 %maximum_select_fusion = f32[2,392,256]{2,1,0:T(8,128)S(1)} fusion(f32[1,392,256]{2,1,0:T(8,128)} %bitcast.5, f32[1,392,256]{2,1,0:T(8,128)S(1)} %bitcast.30, pred[]{:T(512)S(6)} %eq.37), kind=kLoop, calls=%fused_computation | loop fusion | flops 602112 | bytes 1605633 | tf_op jit(solution)/shard_map/jit(_where)/select_n | solution.py:672
  37.7 0.1 reshape.218
  37.8 0.1 fusion
  38.0 0.8 copy.26
  38.8 2.4 %reshape.216 = f32[2,6,2,2,2,8,8,32]{7,6,5,4,3,2,1,0:T(8,128)} reshape(f32[2,384,256]{2,1,0:T(8,128)S(1)} %slice.34) | data formatting | bytes 1572864 | tf_op jit(solution)/shard_map/reshape | solution.py:673
  41.1 3.9 %copy.23 = f32[2,6,2,2,2,8,8,32]{7,6,0,5,2,4,3,1:T(8,128)} copy(f32[2,6,2,2,2,8,8,32]{7,6,5,4,3,2,1,0:T(8,128)} %reshape.216) | data formatting | bytes 1572864 | tf_op jit(solution)/shard_map/reshape | solution.py:673
  45.0 2.4 %copy.24 = f32[6,32,8,128]{3,2,1,0:T(8,128)S(1)} copy(f32[6,32,8,128]{1,3,2,0:T(8,128)} %bitcast.31) | data formatting | bytes 1572864 | tf_op jit(solution)/shard_map/reshape | solution.py:674
  47.4 0.1 subtract_multiply_fusion.a_1_
  47.5 0.5 slice.40
  48.1 1.0 %pad.4.a_2_ = f32[3,32,8,128]{3,2,1,0:T(8,128)S(1)} pad(f32[3,32,3,16]{3,2,1,0:T(4,128)} %bitcast.33, f32[]{:T(128)} %constant.28.clone.1), padding=0_0x0_0x0_5x0_112 | pad | bytes 411652 | tf_op jit(solution)/shard_map/jit(_pad)/pad | solution.py:700
  49.7 1.1 %broadcast_select_fusion.2 = (bf16[512,256]{1,0:T(8,128)(2,1)S(1)}, bf16[512,256]{1,0:T(8,128)(2,1)S(1)}) fusion(bf16[512,256]{1,0:T(8,128)(2,1)} %constant.86.clone, pred[]{:T(512)} %bitcast.14, bf16[512,256]{1,0:T(8,128)(2,1)} %constant.85.clone), kind=kLoop, calls=%fused_computation.4 | loop fusion | flops 262144 | bytes 1048577 | tf_op jit(solution)/shard_map/jit(_where)/select_n | solution.py:746
  50.8 7.0 %all-to-all-done.a_0_ = f32[32,6,8,128]{3,2,1,0:T(8,128)S(1)} async-done(((f32[32,6,8,128]{3,2,1,0:T(8,128)}), f32[32,6,8,128]{3,2,1,0:T(8,128)S(1)}, u32[]{:S(2)}, u32[]{:S(2)}) %all-to-all-start) | async-done | bytes 786464 | tf_op jit(solution)/shard_map/all_to_all | solution.py:788
  57.8 1.6 %shard_map.134 = f32[32,6,8,128]{3,2,1,0:T(8,128)S(1)} custom-call(f32[32,6,8,128]{3,2,1,0:T(8,128)S(1)} %all-to-all-done.a_0_, f32[6,32,8,128]{3,2,1,0:T(8,128)S(1)} %subtract_multiply_fusion.a_1_, f32[3,32,8,128]{3,2,1,0:T(8,128)S(1)} %pad.4.a_2_, f32[8,128]{1,0:T(8,128)S(1)} %and_select_fusion.a_3_, bf16[512,256]{1,0:T(8,128)(2,1)S(1)} %get-tuple-element.57.a_4_, ...), custom_call_target="tpu_custom_call" | custom-call | tf_op jit(solution)/shard_map/pallas_call | solution.py:723
  59.3 23.2 %all_to_all.10.a_0_ = f32[32,6,8,128]{3,2,1,0:T(8,128)S(1)} all-to-all(f32[32,6,8,128]{3,2,1,0:T(8,128)S(1)} %shard_map.134), channel_id=1, replica_groups=mesh['gx'=4,'gy'=2,'gz'=4] {'gx','gy','gz'}, dimensions={0} | all-to-all | bytes 1572864 | tf_op jit(solution)/shard_map/all_to_all | solution.py:799
  82.5 0.8 shard_map.135
  83.3 0.8 collective-permute-start.10
  84.1 0.7 collective-permute-start.11
  84.8 1.6 %collective-permute-start.12 = (f32[16,1536]{1,0:T(8,128)S(1)}, f32[16,1536]{1,0:T(8,128)S(1)}, u32[]{:S(2)}, u32[]{:S(2)}) collective-permute-start(f32[16,1536]{1,0:T(8,128)S(1)} %get-tuple-element.43), channel_id=1, source_target_pairs={{0,20},{4,16},{8,28},{12,24},{16,4},{20,0},{24,12},{28,8},{1,21},{... | collective-permute-start | bytes 294920 | tf_op jit(solution)/shard_map/ppermute | solution.py:740
  86.4 1.0 %collective-permute-start.13 = (f32[16,1536]{1,0:T(8,128)S(1)}, f32[16,1536]{1,0:T(8,128)S(1)}, u32[]{:S(2)}, u32[]{:S(2)}) collective-permute-start(f32[16,1536]{1,0:T(8,128)S(1)} %get-tuple-element.44), channel_id=1, source_target_pairs={{0,24},{4,28},{8,16},{12,20},{16,8},{20,12},{24,0},{28,4},{1,25},{... | collective-permute-start | bytes 294920 | tf_op jit(solution)/shard_map/ppermute | solution.py:740
  87.4 1.4 %collective-permute-start.14 = (f32[16,1536]{1,0:T(8,128)S(1)}, f32[16,1536]{1,0:T(8,128)S(1)}, u32[]{:S(2)}, u32[]{:S(2)}) collective-permute-start(f32[16,1536]{1,0:T(8,128)S(1)} %get-tuple-element.45), channel_id=1, source_target_pairs={{0,28},{4,24},{8,20},{12,16},{16,12},{20,8},{24,4},{28,0},{1,29},{... | collective-permute-start | bytes 294920 | tf_op jit(solution)/shard_map/ppermute | solution.py:740
  88.8 0.8 collective-permute-start.8
  89.6 2.5 %collective-permute-done.12.a_5_ = f32[16,1536]{1,0:T(8,128)S(1)} collective-permute-done((f32[16,1536]{1,0:T(8,128)S(1)}, f32[16,1536]{1,0:T(8,128)S(1)}, u32[]{:S(2)}, u32[]{:S(2)}) %collective-permute-start.12) | collective-permute-done | bytes 98336 | tf_op jit(solution)/shard_map/ppermute | solution.py:740
  92.1 0.7 collective-permute-done.13.a_6_
  92.8 2.8 %collective-permute-done.14.a_7_ = f32[16,1536]{1,0:T(8,128)S(1)} collective-permute-done((f32[16,1536]{1,0:T(8,128)S(1)}, f32[16,1536]{1,0:T(8,128)S(1)}, u32[]{:S(2)}, u32[]{:S(2)}) %collective-permute-start.14) | collective-permute-done | bytes 98336 | tf_op jit(solution)/shard_map/ppermute | solution.py:740
  95.6 2.0 %shard_map.136 = (f32[3,4,128,128]{3,2,1,0:T(8,128)}, f32[3,4,128,128]{3,2,1,0:T(8,128)}) custom-call(f32[16,1536]{1,0:T(8,128)S(1)} %get-tuple-element.38.a_0_, f32[16,1536]{1,0:T(8,128)S(1)} %collective-permute-done.8.a_1_, f32[16,1536]{1,0:T(8,128)S(1)} %collective-permute-done.9.a_2_, f32[16,1536]{1,0:T(8,128)S(1)} %collective-permute-done.10.a_3_, ...), custom_call_target="tpu_custom_call" | custom-call | tf_op jit(solution)/shard_map/pallas_call | solution.py:723
  (49 shorter events, 0.5 us)
Async XLA Ops:
  0.6 11.8 %copy-start.4 = (bf16[2,256,512]{2,1,0:T(8,128)(2,1)S(1)}, bf16[2,256,512]{2,1,0:T(8,128)(2,1)}, u32[]{:S(2)}) copy-start(bf16[2,256,512]{2,1,0:T(8,128)(2,1)} %constant.80.clone) | copy-start | bytes 1572868
  3.6 32.9 %collective-permute-start.7 = (f32[392,256]{1,0:T(8,128)S(1)}, f32[392,256]{1,0:T(8,128)}, u32[]{:S(2)}, u32[]{:S(2)}) collective-permute-start(f32[392,256]{1,0:T(8,128)S(1)} %get-tuple-element.37), channel_id=1, source_target_pairs={{0,4},{4,0},{1,5},{5,1},{2,6},{6,2},{3,7},{7,3},{8,12},{12,8},{9,1... | collective-permute-start | bytes 1204232 | tf_op jit(solution)/shard_map/ppermute | solution.py:670
  6.6 12.2 %collective-permute-start = (f32[16,1536]{1,0:T(8,128)S(1)}, f32[16,1536]{1,0:T(8,128)S(1)}, u32[]{:S(2)}, u32[]{:S(2)}) collective-permute-start(f32[16,1536]{1,0:T(8,128)S(1)} %get-tuple-element.27), channel_id=1, source_target_pairs={{0,4},{4,0},{8,12},{12,8},{16,20},{20,16},{24,28},{28,24},{1,5},{5... | collective-permute-start | bytes 294920 | tf_op jit(solution)/shard_map/ppermute | solution.py:740
  6.7 15.1 %collective-permute-start.1 = (f32[16,1536]{1,0:T(8,128)S(1)}, f32[16,1536]{1,0:T(8,128)S(1)}, u32[]{:S(2)}, u32[]{:S(2)}) collective-permute-start(f32[16,1536]{1,0:T(8,128)S(1)} %get-tuple-element.28), channel_id=1, source_target_pairs={{0,8},{4,12},{8,0},{12,4},{16,24},{20,28},{24,16},{28,20},{1,9},{5... | collective-permute-start | bytes 294920 | tf_op jit(solution)/shard_map/ppermute | solution.py:740
  6.7 15.1 %collective-permute-start.2 = (f32[16,1536]{1,0:T(8,128)S(1)}, f32[16,1536]{1,0:T(8,128)S(1)}, u32[]{:S(2)}, u32[]{:S(2)}) collective-permute-start(f32[16,1536]{1,0:T(8,128)S(1)} %get-tuple-element.29), channel_id=1, source_target_pairs={{0,12},{4,8},{8,4},{12,0},{16,28},{20,24},{24,20},{28,16},{1,13},{... | collective-permute-start | bytes 294920 | tf_op jit(solution)/shard_map/ppermute | solution.py:740
  8.8 15.5 %collective-permute-start.3 = (f32[16,1536]{1,0:T(8,128)S(1)}, f32[16,1536]{1,0:T(8,128)S(1)}, u32[]{:S(2)}, u32[]{:S(2)}) collective-permute-start(f32[16,1536]{1,0:T(8,128)S(1)} %get-tuple-element.30), channel_id=1, source_target_pairs={{0,16},{4,20},{8,24},{12,28},{16,0},{20,4},{24,8},{28,12},{1,17},{... | collective-permute-start | bytes 294920 | tf_op jit(solution)/shard_map/ppermute | solution.py:740
  10.3 1.3 %copy-start.7 = (pred[8]{0:T(512)(128)(4,1)}, pred[8]{0:T(512)(128)(4,1)S(1)}, u32[]{:S(2)}) copy-start(pred[8]{0:T(512)(128)(4,1)S(1)} %iota_compare_fusion.1) | copy-start | bytes 28
  18.9 6.1 %collective-permute-start.4 = (f32[16,1536]{1,0:T(8,128)S(1)}, f32[16,1536]{1,0:T(8,128)S(1)}, u32[]{:S(2)}, u32[]{:S(2)}) collective-permute-start(f32[16,1536]{1,0:T(8,128)S(1)} %get-tuple-element.31), channel_id=1, source_target_pairs={{0,20},{4,16},{8,28},{12,24},{16,4},{20,0},{24,12},{28,8},{1,21},{... | collective-permute-start | bytes 294920 | tf_op jit(solution)/shard_map/ppermute | solution.py:740
  21.8 5.3 %collective-permute-start.5 = (f32[16,1536]{1,0:T(8,128)S(1)}, f32[16,1536]{1,0:T(8,128)S(1)}, u32[]{:S(2)}, u32[]{:S(2)}) collective-permute-start(f32[16,1536]{1,0:T(8,128)S(1)} %get-tuple-element.32), channel_id=1, source_target_pairs={{0,24},{4,28},{8,16},{12,20},{16,8},{20,12},{24,0},{28,4},{1,25},{... | collective-permute-start | bytes 294920 | tf_op jit(solution)/shard_map/ppermute | solution.py:740
  21.8 6.8 %collective-permute-start.6 = (f32[16,1536]{1,0:T(8,128)S(1)}, f32[16,1536]{1,0:T(8,128)S(1)}, u32[]{:S(2)}, u32[]{:S(2)}) collective-permute-start(f32[16,1536]{1,0:T(8,128)S(1)} %get-tuple-element.33), channel_id=1, source_target_pairs={{0,28},{4,24},{8,20},{12,16},{16,12},{20,8},{24,4},{28,0},{1,29},{... | collective-permute-start | bytes 294920 | tf_op jit(solution)/shard_map/ppermute | solution.py:740
  28.6 9.2 %copy-start.6 = (f32[6]{0:T(128)S(1)}, f32[6]{0:T(128)}, u32[]{:S(2)}) copy-start(f32[6]{0:T(128)} %constant.84.clone) | copy-start | bytes 76
  30.7 27.0 %all-to-all-start = ((f32[32,6,8,128]{3,2,1,0:T(8,128)}), f32[32,6,8,128]{3,2,1,0:T(8,128)S(1)}, u32[]{:S(2)}, u32[]{:S(2)}) async-start(f32[32,6,8,128]{3,2,1,0:T(8,128)} %shard_map.132), calls=%async_computation | async-start | bytes 1572864 | tf_op jit(solution)/shard_map/all_to_all | solution.py:788
  45.0 2.4 %copy-start.5 = (f32[32,8,128]{2,1,0:T(8,128)S(1)}, f32[32,8,128]{2,1,0:T(8,128)}, u32[]{:S(2)}) copy-start(f32[32,8,128]{2,1,0:T(8,128)} %broadcast_add_fusion) | copy-start | bytes 393220
  48.0 34.5 %copy-start.1 = (bf16[2,512,256]{2,1,0:T(8,128)(2,1)S(1)}, bf16[2,512,256]{2,1,0:T(8,128)(2,1)}, u32[]{:S(2)}) copy-start(bf16[2,512,256]{2,1,0:T(8,128)(2,1)} %constant.87.clone.a_1_) | copy-start | bytes 1572868
  48.0 34.5 %copy-start.2 = (bf16[2,512,256]{2,1,0:T(8,128)(2,1)S(1)}, bf16[2,512,256]{2,1,0:T(8,128)(2,1)}, u32[]{:S(2)}) copy-start(bf16[2,512,256]{2,1,0:T(8,128)(2,1)} %constant.88.clone.a_2_) | copy-start | bytes 1572868
  57.8 37.9 %copy-start = (f32[3,16,32,128]{3,2,1,0:T(8,128)S(1)}, f32[3,16,32,128]{3,2,1,0:T(8,128)}, u32[]{:S(2)}) copy-start(f32[3,16,32,128]{3,2,1,0:T(8,128)} %param.12) | copy-start | bytes 2359300
  57.8 37.9 %copy-start.3 = (f32[3]{0:T(128)S(1)}, f32[3]{0:T(128)}, u32[]{:S(2)}) copy-start(f32[3]{0:T(128)} %a_9_.1) | copy-start | bytes 40
  83.3 5.5 %collective-permute-start.10 = (f32[16,1536]{1,0:T(8,128)S(1)}, f32[16,1536]{1,0:T(8,128)S(1)}, u32[]{:S(2)}, u32[]{:S(2)}) collective-permute-start(f32[16,1536]{1,0:T(8,128)S(1)} %get-tuple-element.41), channel_id=1, source_target_pairs={{0,12},{4,8},{8,4},{12,0},{16,28},{20,24},{24,20},{28,16},{1,13},{... | collective-permute-start | bytes 294920 | tf_op jit(solution)/shard_map/ppermute | solution.py:740
  84.1 5.5 %collective-permute-start.11 = (f32[16,1536]{1,0:T(8,128)S(1)}, f32[16,1536]{1,0:T(8,128)S(1)}, u32[]{:S(2)}, u32[]{:S(2)}) collective-permute-start(f32[16,1536]{1,0:T(8,128)S(1)} %get-tuple-element.42), channel_id=1, source_target_pairs={{0,16},{4,20},{8,24},{12,28},{16,0},{20,4},{24,8},{28,12},{1,17},{... | collective-permute-start | bytes 294920 | tf_op jit(solution)/shard_map/ppermute | solution.py:740
  84.8 7.3 %collective-permute-start.12 = (f32[16,1536]{1,0:T(8,128)S(1)}, f32[16,1536]{1,0:T(8,128)S(1)}, u32[]{:S(2)}, u32[]{:S(2)}) collective-permute-start(f32[16,1536]{1,0:T(8,128)S(1)} %get-tuple-element.43), channel_id=1, source_target_pairs={{0,20},{4,16},{8,28},{12,24},{16,4},{20,0},{24,12},{28,8},{1,21},{... | collective-permute-start | bytes 294920 | tf_op jit(solution)/shard_map/ppermute | solution.py:740
  86.4 6.5 %collective-permute-start.13 = (f32[16,1536]{1,0:T(8,128)S(1)}, f32[16,1536]{1,0:T(8,128)S(1)}, u32[]{:S(2)}, u32[]{:S(2)}) collective-permute-start(f32[16,1536]{1,0:T(8,128)S(1)} %get-tuple-element.44), channel_id=1, source_target_pairs={{0,24},{4,28},{8,16},{12,20},{16,8},{20,12},{24,0},{28,4},{1,25},{... | collective-permute-start | bytes 294920 | tf_op jit(solution)/shard_map/ppermute | solution.py:740
  87.4 8.2 %collective-permute-start.14 = (f32[16,1536]{1,0:T(8,128)S(1)}, f32[16,1536]{1,0:T(8,128)S(1)}, u32[]{:S(2)}, u32[]{:S(2)}) collective-permute-start(f32[16,1536]{1,0:T(8,128)S(1)} %get-tuple-element.45), channel_id=1, source_target_pairs={{0,28},{4,24},{8,20},{12,16},{16,12},{20,8},{24,4},{28,0},{1,29},{... | collective-permute-start | bytes 294920 | tf_op jit(solution)/shard_map/ppermute | solution.py:740
  88.8 6.8 %collective-permute-start.8 = (f32[16,1536]{1,0:T(8,128)S(1)}, f32[16,1536]{1,0:T(8,128)S(1)}, u32[]{:S(2)}, u32[]{:S(2)}) collective-permute-start(f32[16,1536]{1,0:T(8,128)S(1)} %get-tuple-element.39), channel_id=1, source_target_pairs={{0,4},{4,0},{8,12},{12,8},{16,20},{20,16},{24,28},{28,24},{1,5},{5... | collective-permute-start | bytes 294920 | tf_op jit(solution)/shard_map/ppermute | solution.py:740
  89.6 6.0 %collective-permute-start.9 = (f32[16,1536]{1,0:T(8,128)S(1)}, f32[16,1536]{1,0:T(8,128)S(1)}, u32[]{:S(2)}, u32[]{:S(2)}) collective-permute-start(f32[16,1536]{1,0:T(8,128)S(1)} %get-tuple-element.40), channel_id=1, source_target_pairs={{0,8},{4,12},{8,0},{12,4},{16,24},{20,28},{24,16},{28,20},{1,9},{5... | collective-permute-start | bytes 294920 | tf_op jit(solution)/shard_map/ppermute | solution.py:740

commit v4 on v3

--- a/solution.py
+++ b/solution.py
@@ -391,7 +391,8 @@
 
 def xy_forward_kernel(plan, *refs):
     chunks, refs = refs[: plan.planes], refs[plan.planes :]
-    table_ref, edge_ref, out_ref, lines_ref, g_ref, e_ref, tw_ref = refs
+    table_ref, edge_ref, out_hbm, lines_ref, g_ref, e_ref, tw_ref, out_ref, sem = refs
+    stores = []
     me = plane_index()
     fill_x_twiddles(plan, tw_ref)
     for o in range(plan.planes):
@@ -452,6 +453,10 @@
                 dest = (gx * plan.cy + k2h) * plan.cz + gz
                 out_ref[dest, 2 * c] = jnp.where(low, one, two)
                 out_ref[dest, 2 * c + 1] = pltpu.roll(jnp.where(low, two, one), 4, 0)
+        pair = pl.ds(2 * c, 2)
+        stores.append(fetch(out_ref.at[:, pair], out_hbm.at[:, pair], sem.at[c]))
+    for store in stores:
+        store.wait()
 
 
 def xy_inverse_kernel(plan, spec_ref, table_ref, edge_ref, *refs):
@@ -730,7 +735,7 @@
     return run
 
 
-SEND_ORDER = (7, 4, 1, 5, 6, 3, 2)
+SEND_ORDER = (4, 1, 5, 7, 6, 3, 2)
 
 
 def plane_swap(plan, chunks):
@@ -777,12 +782,14 @@
     spec = call(
         lambda *a: xy_forward_kernel(plan, *a),
         "v" * planes + "vv",
-        vmem(spectrum, f32),
+        sds(spectrum, f32),
         [
             vmem((planes, zc, width), f32),
             vmem((2, 3, LANES, 512), bf16),
             vmem((2, LANES, 512), bf16),
             vmem((2, SUBS, LANES), f32),
+            vmem(spectrum, f32),
+            dma((3,)),
         ],
     )(*lines, *fwd)
     spec = lax.all_to_all(spec, ("gx", "gy", "gz"), split_axis=0, concat_axis=0, tiled=True)

time: 98.1 us -> 98 us (level)
  no operation moved by 1% of the time
where the time goes in v4:
time: 98 us; the launch traced here: 97.5 us
  starting transfers between devices  23.2 us (24%)
  blocking collectives  23.2 us (24%)
  waiting for transfers between devices  22.7 us (23%)
  local copies, waits for them, and re-layouts  11.6 us (12%)
  Pallas kernels  9.22 us (9%)
  other arithmetic  6.12 us (6%)
  between operations  1.54 us (2%)
    all_to_all x1, blocking collectives, fast_shards(): lax.all_to_all(spec, ('gx', 'gy', 'gz'), split_axis=0, concat_axis=0, til...  23.2 us
    ppermute x14, waiting for transfers between devices, plane_swap(): lax.ppermute(chunks[o], ('gx', 'gy'), [(k, k ^ o) for k in members])  15.7 us
    ppermute x14, starting transfers between devices, plane_swap(): lax.ppermute(chunks[o], ('gx', 'gy'), [(k, k ^ o) for k in members])  14.5 us
    pallas_call x6, Pallas kernels, run(): step(*(x if p == 's' else pltpu.with_memory_space_constraint(x, spaces[p]...  9.22 us
    all_to_all x1, waiting for transfers between devices, fast_shards(): lax.all_to_all(spec, ('gx', 'gy', 'gz'), split_axis=0, concat_axis=0, til...  7.01 us
    reshape x2, local copies, waits for them, and re-layouts, field_tensor(): main = got[:, :6 * 4 * 2 * 8].reshape(2, 6, 2, 2, 2, 8, kzs // 32, 32)  6.21 us
    all_to_all x1, starting transfers between devices, fast_shards(): lax.all_to_all(spec, ('gx', 'gy', 'gz'), split_axis=0, concat_axis=0, til...  5.67 us
    ppermute x1, starting transfers between devices, field_tensor(): other = lax.ppermute(other, 'gy', [(0, 1), (1, 0)])  3.06 us
  transfers between devices with their start and end apart: 16, of which 8 were waited for; matrix products, arithmetic and copies ran while one was open for 18% of the time, Pallas kernels for 2%

profile of v4, /device:TPU:0, one launch (start us, length us, event | category | flops | bytes accessed | tf_op | source)
XLA Modules:
  0.0 97.5 jit_solution(17625299945338090813)
XLA Ops:
  0.6 1.5 %shard_map.131 = (f32[16,1536]{1,0:T(8,128)S(1)}, f32[16,1536]{1,0:T(8,128)S(1)}, f32[16,1536]{1,0:T(8,128)S(1)}, f32[16,1536]{1,0:T(8,128)S(1)}, f32[16,1536]{1...) custom-call(f32[12,128,128]{2,1,0:T(8,128)} %bitcast.28), custom_call_target="tpu_custom_call" | custom-call | tf_op jit(solution)/shard_map/pallas_call | solution.py:728
  2.2 1.4 %shard_map.133 = (f32[392,256]{1,0:T(8,128)S(1)}, f32[392,256]{1,0:T(8,128)S(1)}) custom-call(f32[6,4,64,256]{3,2,1,0:T(8,128)} %bitcast.32), custom_call_target="tpu_custom_call" | custom-call | tf_op jit(solution)/shard_map/pallas_call | solution.py:728
  3.6 3.1 %collective-permute-start.7 = (f32[392,256]{1,0:T(8,128)S(1)}, f32[392,256]{1,0:T(8,128)}, u32[]{:S(2)}, u32[]{:S(2)}) collective-permute-start(f32[392,256]{1,0:T(8,128)S(1)} %get-tuple-element.37), channel_id=1, source_target_pairs={{0,4},{4,0},{1,5},{5,1},{2,6},{6,2},{3,7},{7,3},{8,12},{12,8},{9,1... | collective-permute-start | bytes 1204232 | tf_op jit(solution)/shard_map/ppermute | solution.py:675
  6.6 0.1 collective-permute-start
  6.7 2.1 %collective-permute-start.2 = (f32[16,1536]{1,0:T(8,128)S(1)}, f32[16,1536]{1,0:T(8,128)S(1)}, u32[]{:S(2)}, u32[]{:S(2)}) collective-permute-start(f32[16,1536]{1,0:T(8,128)S(1)} %get-tuple-element.29), channel_id=1, source_target_pairs={{0,12},{4,8},{8,4},{12,0},{16,28},{20,24},{24,20},{28,16},{1,13},{... | collective-permute-start | bytes 294920 | tf_op jit(solution)/shard_map/ppermute | solution.py:745
  8.8 1.5 %collective-permute-start.3 = (f32[16,1536]{1,0:T(8,128)S(1)}, f32[16,1536]{1,0:T(8,128)S(1)}, u32[]{:S(2)}, u32[]{:S(2)}) collective-permute-start(f32[16,1536]{1,0:T(8,128)S(1)} %get-tuple-element.30), channel_id=1, source_target_pairs={{0,16},{4,20},{8,24},{12,28},{16,0},{20,4},{24,8},{28,12},{1,17},{... | collective-permute-start | bytes 294920 | tf_op jit(solution)/shard_map/ppermute | solution.py:745
  10.4 0.1 and.84
  10.5 0.1 add.126
  10.7 0.7 broadcast_select_fusion.4
  11.4 0.1 add_add_fusion
  11.5 0.1 add.129
  11.6 0.1 add.130
  11.8 0.7 broadcast_add_fusion
  12.5 1.1 %broadcast_select_fusion = (bf16[2,256,512]{2,1,0:T(8,128)(2,1)S(1)}, bf16[2,256,512]{2,1,0:T(8,128)(2,1)S(1)}) fusion(bf16[2,256,512]{2,1,0:T(8,128)(2,1)} %constant.81.clone, pred[]{:T(512)S(6)} %gt.16, bf16[2,256,512]{2,1,0:T(8,128)(2,1)S(1)} %copy-done.4), kind=kLoop, calls=%fused_computation.2 | loop fusion | flops 524288 | bytes 2097153 | tf_op jit(solution)/shard_map/jit(_where)/select_n | solution.py:751
  13.6 5.3 %collective-permute-done.a_1_ = f32[16,1536]{1,0:T(8,128)S(1)} collective-permute-done((f32[16,1536]{1,0:T(8,128)S(1)}, f32[16,1536]{1,0:T(8,128)S(1)}, u32[]{:S(2)}, u32[]{:S(2)}) %collective-permute-start) | collective-permute-done | bytes 98336 | tf_op jit(solution)/shard_map/ppermute | solution.py:745
  18.9 2.9 %collective-permute-start.4 = (f32[16,1536]{1,0:T(8,128)S(1)}, f32[16,1536]{1,0:T(8,128)S(1)}, u32[]{:S(2)}, u32[]{:S(2)}) collective-permute-start(f32[16,1536]{1,0:T(8,128)S(1)} %get-tuple-element.31), channel_id=1, source_target_pairs={{0,20},{4,16},{8,28},{12,24},{16,4},{20,0},{24,12},{28,8},{1,21},{... | collective-permute-start | bytes 294920 | tf_op jit(solution)/shard_map/ppermute | solution.py:745
  21.8 1.7 %collective-permute-start.6 = (f32[16,1536]{1,0:T(8,128)S(1)}, f32[16,1536]{1,0:T(8,128)S(1)}, u32[]{:S(2)}, u32[]{:S(2)}) collective-permute-start(f32[16,1536]{1,0:T(8,128)S(1)} %get-tuple-element.33), channel_id=1, source_target_pairs={{0,28},{4,24},{8,20},{12,16},{16,12},{20,8},{24,4},{28,0},{1,29},{... | collective-permute-start | bytes 294920 | tf_op jit(solution)/shard_map/ppermute | solution.py:745
  23.5 0.7 and_select_fusion.a_3_
  24.3 0.7 collective-permute-done.4.a_5_
  24.9 2.1 %collective-permute-done.5.a_6_ = f32[16,1536]{1,0:T(8,128)S(1)} collective-permute-done((f32[16,1536]{1,0:T(8,128)S(1)}, f32[16,1536]{1,0:T(8,128)S(1)}, u32[]{:S(2)}, u32[]{:S(2)}) %collective-permute-start.5) | collective-permute-done | bytes 98336 | tf_op jit(solution)/shard_map/ppermute | solution.py:745
  27.0 1.6 %collective-permute-done.6.a_7_ = f32[16,1536]{1,0:T(8,128)S(1)} collective-permute-done((f32[16,1536]{1,0:T(8,128)S(1)}, f32[16,1536]{1,0:T(8,128)S(1)}, u32[]{:S(2)}, u32[]{:S(2)}) %collective-permute-start.6) | collective-permute-done | bytes 98336 | tf_op jit(solution)/shard_map/ppermute | solution.py:745
  28.6 2.0 %shard_map.132 = f32[32,6,8,128]{3,2,1,0:T(8,128)} custom-call(f32[16,1536]{1,0:T(8,128)S(1)} %get-tuple-element.26.a_0_, f32[16,1536]{1,0:T(8,128)S(1)} %collective-permute-done.a_1_, f32[16,1536]{1,0:T(8,128)S(1)} %collective-permute-done.1.a_2_, f32[16,1536]{1,0:T(8,128)S(1)} %collective-permute-done.2.a_3_, f32[16,1536]{1,0:T(8,128)S(1)} %collective-permute-done.3.a_4_, ...), custom_call_target="tpu_custom_call" | custom-call | tf_op jit(solution)/shard_map/pallas_call | solution.py:728
  30.6 5.7 %all-to-all-start = ((f32[32,6,8,128]{3,2,1,0:T(8,128)}), f32[32,6,8,128]{3,2,1,0:T(8,128)S(1)}, u32[]{:S(2)}, u32[]{:S(2)}) async-start(f32[32,6,8,128]{3,2,1,0:T(8,128)} %shard_map.132), calls=%async_computation | async-start | bytes 1572864 | tf_op jit(solution)/shard_map/all_to_all | solution.py:795
  36.3 1.2 %maximum_select_fusion = f32[2,392,256]{2,1,0:T(8,128)S(1)} fusion(f32[1,392,256]{2,1,0:T(8,128)} %bitcast.5, f32[1,392,256]{2,1,0:T(8,128)S(1)} %bitcast.30, pred[]{:T(512)S(6)} %eq.37), kind=kLoop, calls=%fused_computation | loop fusion | flops 602112 | bytes 1605633 | tf_op jit(solution)/shard_map/jit(_where)/select_n | solution.py:677
  37.6 0.1 reshape.218
  37.7 0.1 fusion
  37.8 0.8 copy.26
  38.6 2.4 %reshape.216 = f32[2,6,2,2,2,8,8,32]{7,6,5,4,3,2,1,0:T(8,128)} reshape(f32[2,384,256]{2,1,0:T(8,128)S(1)} %slice.34) | data formatting | bytes 1572864 | tf_op jit(solution)/shard_map/reshape | solution.py:678
  41.0 3.9 %copy.23 = f32[2,6,2,2,2,8,8,32]{7,6,0,5,2,4,3,1:T(8,128)} copy(f32[2,6,2,2,2,8,8,32]{7,6,5,4,3,2,1,0:T(8,128)} %reshape.216) | data formatting | bytes 1572864 | tf_op jit(solution)/shard_map/reshape | solution.py:678
  44.8 2.4 %copy.24 = f32[6,32,8,128]{3,2,1,0:T(8,128)S(1)} copy(f32[6,32,8,128]{1,3,2,0:T(8,128)} %bitcast.31) | data formatting | bytes 1572864 | tf_op jit(solution)/shard_map/reshape | solution.py:679
  47.3 0.1 subtract_multiply_fusion.a_1_
  47.4 0.5 slice.40
  47.9 1.0 %pad.4.a_2_ = f32[3,32,8,128]{3,2,1,0:T(8,128)S(1)} pad(f32[3,32,3,16]{3,2,1,0:T(4,128)} %bitcast.33, f32[]{:T(128)} %constant.28.clone.1), padding=0_0x0_0x0_5x0_112 | pad | bytes 411652 | tf_op jit(solution)/shard_map/jit(_pad)/pad | solution.py:705
  49.5 1.1 %broadcast_select_fusion.2 = (bf16[512,256]{1,0:T(8,128)(2,1)S(1)}, bf16[512,256]{1,0:T(8,128)(2,1)S(1)}) fusion(bf16[512,256]{1,0:T(8,128)(2,1)} %constant.86.clone, pred[]{:T(512)} %bitcast.14, bf16[512,256]{1,0:T(8,128)(2,1)} %constant.85.clone), kind=kLoop, calls=%fused_computation.4 | loop fusion | flops 262144 | bytes 1048577 | tf_op jit(solution)/shard_map/jit(_where)/select_n | solution.py:751
  50.6 7.0 %all-to-all-done.a_0_ = f32[32,6,8,128]{3,2,1,0:T(8,128)S(1)} async-done(((f32[32,6,8,128]{3,2,1,0:T(8,128)}), f32[32,6,8,128]{3,2,1,0:T(8,128)S(1)}, u32[]{:S(2)}, u32[]{:S(2)}) %all-to-all-start) | async-done | bytes 786464 | tf_op jit(solution)/shard_map/all_to_all | solution.py:795
  57.6 1.6 %shard_map.134 = f32[32,6,8,128]{3,2,1,0:T(8,128)S(1)} custom-call(f32[32,6,8,128]{3,2,1,0:T(8,128)S(1)} %all-to-all-done.a_0_, f32[6,32,8,128]{3,2,1,0:T(8,128)S(1)} %subtract_multiply_fusion.a_1_, f32[3,32,8,128]{3,2,1,0:T(8,128)S(1)} %pad.4.a_2_, f32[8,128]{1,0:T(8,128)S(1)} %and_select_fusion.a_3_, bf16[512,256]{1,0:T(8,128)(2,1)S(1)} %get-tuple-element.57.a_4_, ...), custom_call_target="tpu_custom_call" | custom-call | tf_op jit(solution)/shard_map/pallas_call | solution.py:728
  59.2 23.2 %all_to_all.10.a_0_ = f32[32,6,8,128]{3,2,1,0:T(8,128)S(1)} all-to-all(f32[32,6,8,128]{3,2,1,0:T(8,128)S(1)} %shard_map.134), channel_id=1, replica_groups=mesh['gx'=4,'gy'=2,'gz'=4] {'gx','gy','gz'}, dimensions={0} | all-to-all | bytes 1572864 | tf_op jit(solution)/shard_map/all_to_all | solution.py:806
  82.4 0.8 shard_map.135
  83.2 0.8 collective-permute-start.10
  84.0 0.7 collective-permute-start.11
  84.7 1.6 %collective-permute-start.12 = (f32[16,1536]{1,0:T(8,128)S(1)}, f32[16,1536]{1,0:T(8,128)S(1)}, u32[]{:S(2)}, u32[]{:S(2)}) collective-permute-start(f32[16,1536]{1,0:T(8,128)S(1)} %get-tuple-element.43), channel_id=1, source_target_pairs={{0,20},{4,16},{8,28},{12,24},{16,4},{20,0},{24,12},{28,8},{1,21},{... | collective-permute-start | bytes 294920 | tf_op jit(solution)/shard_map/ppermute | solution.py:745
  86.2 1.0 %collective-permute-start.13 = (f32[16,1536]{1,0:T(8,128)S(1)}, f32[16,1536]{1,0:T(8,128)S(1)}, u32[]{:S(2)}, u32[]{:S(2)}) collective-permute-start(f32[16,1536]{1,0:T(8,128)S(1)} %get-tuple-element.44), channel_id=1, source_target_pairs={{0,24},{4,28},{8,16},{12,20},{16,8},{20,12},{24,0},{28,4},{1,25},{... | collective-permute-start | bytes 294920 | tf_op jit(solution)/shard_map/ppermute | solution.py:745
  87.2 1.4 %collective-permute-start.14 = (f32[16,1536]{1,0:T(8,128)S(1)}, f32[16,1536]{1,0:T(8,128)S(1)}, u32[]{:S(2)}, u32[]{:S(2)}) collective-permute-start(f32[16,1536]{1,0:T(8,128)S(1)} %get-tuple-element.45), channel_id=1, source_target_pairs={{0,28},{4,24},{8,20},{12,16},{16,12},{20,8},{24,4},{28,0},{1,29},{... | collective-permute-start | bytes 294920 | tf_op jit(solution)/shard_map/ppermute | solution.py:745
  88.7 0.8 collective-permute-start.8
  89.5 2.5 %collective-permute-done.12.a_5_ = f32[16,1536]{1,0:T(8,128)S(1)} collective-permute-done((f32[16,1536]{1,0:T(8,128)S(1)}, f32[16,1536]{1,0:T(8,128)S(1)}, u32[]{:S(2)}, u32[]{:S(2)}) %collective-permute-start.12) | collective-permute-done | bytes 98336 | tf_op jit(solution)/shard_map/ppermute | solution.py:745
  92.0 0.7 collective-permute-done.13.a_6_
  92.7 2.8 %collective-permute-done.14.a_7_ = f32[16,1536]{1,0:T(8,128)S(1)} collective-permute-done((f32[16,1536]{1,0:T(8,128)S(1)}, f32[16,1536]{1,0:T(8,128)S(1)}, u32[]{:S(2)}, u32[]{:S(2)}) %collective-permute-start.14) | collective-permute-done | bytes 98336 | tf_op jit(solution)/shard_map/ppermute | solution.py:745
  95.5 2.0 %shard_map.136 = (f32[3,4,128,128]{3,2,1,0:T(8,128)}, f32[3,4,128,128]{3,2,1,0:T(8,128)}) custom-call(f32[16,1536]{1,0:T(8,128)S(1)} %get-tuple-element.38.a_0_, f32[16,1536]{1,0:T(8,128)S(1)} %collective-permute-done.8.a_1_, f32[16,1536]{1,0:T(8,128)S(1)} %collective-permute-done.9.a_2_, f32[16,1536]{1,0:T(8,128)S(1)} %collective-permute-done.10.a_3_, ...), custom_call_target="tpu_custom_call" | custom-call | tf_op jit(solution)/shard_map/pallas_call | solution.py:728
  (49 shorter events, 0.5 us)
Async XLA Ops:
  0.6 11.8 %copy-start.4 = (bf16[2,256,512]{2,1,0:T(8,128)(2,1)S(1)}, bf16[2,256,512]{2,1,0:T(8,128)(2,1)}, u32[]{:S(2)}) copy-start(bf16[2,256,512]{2,1,0:T(8,128)(2,1)} %constant.80.clone) | copy-start | bytes 1572868
  3.6 32.7 %collective-permute-start.7 = (f32[392,256]{1,0:T(8,128)S(1)}, f32[392,256]{1,0:T(8,128)}, u32[]{:S(2)}, u32[]{:S(2)}) collective-permute-start(f32[392,256]{1,0:T(8,128)S(1)} %get-tuple-element.37), channel_id=1, source_target_pairs={{0,4},{4,0},{1,5},{5,1},{2,6},{6,2},{3,7},{7,3},{8,12},{12,8},{9,1... | collective-permute-start | bytes 1204232 | tf_op jit(solution)/shard_map/ppermute | solution.py:675
  6.6 12.2 %collective-permute-start = (f32[16,1536]{1,0:T(8,128)S(1)}, f32[16,1536]{1,0:T(8,128)S(1)}, u32[]{:S(2)}, u32[]{:S(2)}) collective-permute-start(f32[16,1536]{1,0:T(8,128)S(1)} %get-tuple-element.27), channel_id=1, source_target_pairs={{0,4},{4,0},{8,12},{12,8},{16,20},{20,16},{24,28},{28,24},{1,5},{5... | collective-permute-start | bytes 294920 | tf_op jit(solution)/shard_map/ppermute | solution.py:745
  6.7 15.1 %collective-permute-start.1 = (f32[16,1536]{1,0:T(8,128)S(1)}, f32[16,1536]{1,0:T(8,128)S(1)}, u32[]{:S(2)}, u32[]{:S(2)}) collective-permute-start(f32[16,1536]{1,0:T(8,128)S(1)} %get-tuple-element.28), channel_id=1, source_target_pairs={{0,8},{4,12},{8,0},{12,4},{16,24},{20,28},{24,16},{28,20},{1,9},{5... | collective-permute-start | bytes 294920 | tf_op jit(solution)/shard_map/ppermute | solution.py:745
  6.7 15.1 %collective-permute-start.2 = (f32[16,1536]{1,0:T(8,128)S(1)}, f32[16,1536]{1,0:T(8,128)S(1)}, u32[]{:S(2)}, u32[]{:S(2)}) collective-permute-start(f32[16,1536]{1,0:T(8,128)S(1)} %get-tuple-element.29), channel_id=1, source_target_pairs={{0,12},{4,8},{8,4},{12,0},{16,28},{20,24},{24,20},{28,16},{1,13},{... | collective-permute-start | bytes 294920 | tf_op jit(solution)/shard_map/ppermute | solution.py:745
  8.8 15.5 %collective-permute-start.3 = (f32[16,1536]{1,0:T(8,128)S(1)}, f32[16,1536]{1,0:T(8,128)S(1)}, u32[]{:S(2)}, u32[]{:S(2)}) collective-permute-start(f32[16,1536]{1,0:T(8,128)S(1)} %get-tuple-element.30), channel_id=1, source_target_pairs={{0,16},{4,20},{8,24},{12,28},{16,0},{20,4},{24,8},{28,12},{1,17},{... | collective-permute-start | bytes 294920 | tf_op jit(solution)/shard_map/ppermute | solution.py:745
  10.3 1.3 %copy-start.7 = (pred[8]{0:T(512)(128)(4,1)}, pred[8]{0:T(512)(128)(4,1)S(1)}, u32[]{:S(2)}) copy-start(pred[8]{0:T(512)(128)(4,1)S(1)} %iota_compare_fusion.1) | copy-start | bytes 28
  18.9 6.1 %collective-permute-start.4 = (f32[16,1536]{1,0:T(8,128)S(1)}, f32[16,1536]{1,0:T(8,128)S(1)}, u32[]{:S(2)}, u32[]{:S(2)}) collective-permute-start(f32[16,1536]{1,0:T(8,128)S(1)} %get-tuple-element.31), channel_id=1, source_target_pairs={{0,20},{4,16},{8,28},{12,24},{16,4},{20,0},{24,12},{28,8},{1,21},{... | collective-permute-start | bytes 294920 | tf_op jit(solution)/shard_map/ppermute | solution.py:745
  21.8 5.3 %collective-permute-start.5 = (f32[16,1536]{1,0:T(8,128)S(1)}, f32[16,1536]{1,0:T(8,128)S(1)}, u32[]{:S(2)}, u32[]{:S(2)}) collective-permute-start(f32[16,1536]{1,0:T(8,128)S(1)} %get-tuple-element.32), channel_id=1, source_target_pairs={{0,24},{4,28},{8,16},{12,20},{16,8},{20,12},{24,0},{28,4},{1,25},{... | collective-permute-start | bytes 294920 | tf_op jit(solution)/shard_map/ppermute | solution.py:745
  21.8 6.8 %collective-permute-start.6 = (f32[16,1536]{1,0:T(8,128)S(1)}, f32[16,1536]{1,0:T(8,128)S(1)}, u32[]{:S(2)}, u32[]{:S(2)}) collective-permute-start(f32[16,1536]{1,0:T(8,128)S(1)} %get-tuple-element.33), channel_id=1, source_target_pairs={{0,28},{4,24},{8,20},{12,16},{16,12},{20,8},{24,4},{28,0},{1,29},{... | collective-permute-start | bytes 294920 | tf_op jit(solution)/shard_map/ppermute | solution.py:745
  28.6 9.1 %copy-start.6 = (f32[6]{0:T(128)S(1)}, f32[6]{0:T(128)}, u32[]{:S(2)}) copy-start(f32[6]{0:T(128)} %constant.84.clone) | copy-start | bytes 76
  30.6 27.0 %all-to-all-start = ((f32[32,6,8,128]{3,2,1,0:T(8,128)}), f32[32,6,8,128]{3,2,1,0:T(8,128)S(1)}, u32[]{:S(2)}, u32[]{:S(2)}) async-start(f32[32,6,8,128]{3,2,1,0:T(8,128)} %shard_map.132), calls=%async_computation | async-start | bytes 1572864 | tf_op jit(solution)/shard_map/all_to_all | solution.py:795
  44.8 2.4 %copy-start.5 = (f32[32,8,128]{2,1,0:T(8,128)S(1)}, f32[32,8,128]{2,1,0:T(8,128)}, u32[]{:S(2)}) copy-start(f32[32,8,128]{2,1,0:T(8,128)} %broadcast_add_fusion) | copy-start | bytes 393220
  47.9 34.5 %copy-start.1 = (bf16[2,512,256]{2,1,0:T(8,128)(2,1)S(1)}, bf16[2,512,256]{2,1,0:T(8,128)(2,1)}, u32[]{:S(2)}) copy-start(bf16[2,512,256]{2,1,0:T(8,128)(2,1)} %constant.87.clone.a_1_) | copy-start | bytes 1572868
  47.9 34.5 %copy-start.2 = (bf16[2,512,256]{2,1,0:T(8,128)(2,1)S(1)}, bf16[2,512,256]{2,1,0:T(8,128)(2,1)}, u32[]{:S(2)}) copy-start(bf16[2,512,256]{2,1,0:T(8,128)(2,1)} %constant.88.clone.a_2_) | copy-start | bytes 1572868
  57.6 37.9 %copy-start = (f32[3,16,32,128]{3,2,1,0:T(8,128)S(1)}, f32[3,16,32,128]{3,2,1,0:T(8,128)}, u32[]{:S(2)}) copy-start(f32[3,16,32,128]{3,2,1,0:T(8,128)} %param.12) | copy-start | bytes 2359300
  57.6 37.9 %copy-start.3 = (f32[3]{0:T(128)S(1)}, f32[3]{0:T(128)}, u32[]{:S(2)}) copy-start(f32[3]{0:T(128)} %a_9_.1) | copy-start | bytes 40
  83.2 5.5 %collective-permute-start.10 = (f32[16,1536]{1,0:T(8,128)S(1)}, f32[16,1536]{1,0:T(8,128)S(1)}, u32[]{:S(2)}, u32[]{:S(2)}) collective-permute-start(f32[16,1536]{1,0:T(8,128)S(1)} %get-tuple-element.41), channel_id=1, source_target_pairs={{0,12},{4,8},{8,4},{12,0},{16,28},{20,24},{24,20},{28,16},{1,13},{... | collective-permute-start | bytes 294920 | tf_op jit(solution)/shard_map/ppermute | solution.py:745
  84.0 5.5 %collective-permute-start.11 = (f32[16,1536]{1,0:T(8,128)S(1)}, f32[16,1536]{1,0:T(8,128)S(1)}, u32[]{:S(2)}, u32[]{:S(2)}) collective-permute-start(f32[16,1536]{1,0:T(8,128)S(1)} %get-tuple-element.42), channel_id=1, source_target_pairs={{0,16},{4,20},{8,24},{12,28},{16,0},{20,4},{24,8},{28,12},{1,17},{... | collective-permute-start | bytes 294920 | tf_op jit(solution)/shard_map/ppermute | solution.py:745
  84.7 7.3 %collective-permute-start.12 = (f32[16,1536]{1,0:T(8,128)S(1)}, f32[16,1536]{1,0:T(8,128)S(1)}, u32[]{:S(2)}, u32[]{:S(2)}) collective-permute-start(f32[16,1536]{1,0:T(8,128)S(1)} %get-tuple-element.43), channel_id=1, source_target_pairs={{0,20},{4,16},{8,28},{12,24},{16,4},{20,0},{24,12},{28,8},{1,21},{... | collective-permute-start | bytes 294920 | tf_op jit(solution)/shard_map/ppermute | solution.py:745
  86.2 6.4 %collective-permute-start.13 = (f32[16,1536]{1,0:T(8,128)S(1)}, f32[16,1536]{1,0:T(8,128)S(1)}, u32[]{:S(2)}, u32[]{:S(2)}) collective-permute-start(f32[16,1536]{1,0:T(8,128)S(1)} %get-tuple-element.44), channel_id=1, source_target_pairs={{0,24},{4,28},{8,16},{12,20},{16,8},{20,12},{24,0},{28,4},{1,25},{... | collective-permute-start | bytes 294920 | tf_op jit(solution)/shard_map/ppermute | solution.py:745
  87.2 8.2 %collective-permute-start.14 = (f32[16,1536]{1,0:T(8,128)S(1)}, f32[16,1536]{1,0:T(8,128)S(1)}, u32[]{:S(2)}, u32[]{:S(2)}) collective-permute-start(f32[16,1536]{1,0:T(8,128)S(1)} %get-tuple-element.45), channel_id=1, source_target_pairs={{0,28},{4,24},{8,20},{12,16},{16,12},{20,8},{24,4},{28,0},{1,29},{... | collective-permute-start | bytes 294920 | tf_op jit(solution)/shard_map/ppermute | solution.py:745
  88.7 6.8 %collective-permute-start.8 = (f32[16,1536]{1,0:T(8,128)S(1)}, f32[16,1536]{1,0:T(8,128)S(1)}, u32[]{:S(2)}, u32[]{:S(2)}) collective-permute-start(f32[16,1536]{1,0:T(8,128)S(1)} %get-tuple-element.39), channel_id=1, source_target_pairs={{0,4},{4,0},{8,12},{12,8},{16,20},{20,16},{24,28},{28,24},{1,5},{5... | collective-permute-start | bytes 294920 | tf_op jit(solution)/shard_map/ppermute | solution.py:745
  89.5 6.0 %collective-permute-start.9 = (f32[16,1536]{1,0:T(8,128)S(1)}, f32[16,1536]{1,0:T(8,128)S(1)}, u32[]{:S(2)}, u32[]{:S(2)}) collective-permute-start(f32[16,1536]{1,0:T(8,128)S(1)} %get-tuple-element.40), channel_id=1, source_target_pairs={{0,8},{4,12},{8,0},{12,4},{16,24},{20,28},{24,16},{28,20},{1,9},{5... | collective-permute-start | bytes 294920 | tf_op jit(solution)/shard_map/ppermute | solution.py:745

commit v5 on v4

--- a/solution.py
+++ b/solution.py
@@ -735,13 +735,13 @@
     return run
 
 
-SEND_ORDER = (4, 1, 5, 7, 6, 3, 2)
-
-
-def plane_swap(plan, chunks):
+SEND_ORDER = {"gather": (4, 1, 5, 7, 6, 3, 2), "scatter": (4, 1, 5, 6, 3, 2, 7)}
+
+
+def plane_swap(plan, chunks, name):
     members = range(plan.planes)
     out = list(chunks)
-    for o in SEND_ORDER:
+    for o in SEND_ORDER[name]:
         out[o] = lax.ppermute(chunks[o], ("gx", "gy"), [(k, k ^ o) for k in members])
     return out
 
@@ -778,7 +778,7 @@
     fwd = on_chip(late, *fwd)
     tensor, edge, mask = field_tensor(plan, own, other)
     zf, zb = on_chip(tensor[0, 0, 0, 0], zf, zb)
-    lines = plane_swap(plan, packed)
+    lines = plane_swap(plan, packed, "gather")
     spec = call(
         lambda *a: xy_forward_kernel(plan, *a),
         "v" * planes + "vv",
@@ -816,7 +816,7 @@
             vmem((2, SUBS, LANES), f32),
         ],
     )(spec, *back)
-    field = plane_swap(plan, field)
+    field = plane_swap(plan, field, "scatter")
     cells = (3, tiles // 3, LANES, LANES)
     pred, torque = call(
         lambda *a: finish_kernel(plan, *a),

time: 98 us -> 98 us (level)
  no operation moved by 1% of the time
where the time goes in v5:
time: 98 us; the launch traced here: 97.5 us
  starting transfers between devices  23.2 us (24%)
  blocking collectives  23.2 us (24%)
  waiting for transfers between devices  22.7 us (23%)
  local copies, waits for them, and re-layouts  11.6 us (12%)
  Pallas kernels  9.22 us (9%)
  other arithmetic  6.12 us (6%)
  between operations  1.54 us (2%)
    all_to_all x1, blocking collectives, fast_shards(): lax.all_to_all(spec, ('gx', 'gy', 'gz'), split_axis=0, concat_axis=0, til...  23.2 us
    ppermute x14, waiting for transfers between devices, plane_swap(): lax.ppermute(chunks[o], ('gx', 'gy'), [(k, k ^ o) for k in members])  15.7 us
    ppermute x14, starting transfers between devices, plane_swap(): lax.ppermute(chunks[o], ('gx', 'gy'), [(k, k ^ o) for k in members])  14.5 us
    pallas_call x6, Pallas kernels, run(): step(*(x if p == 's' else pltpu.with_memory_space_constraint(x, spaces[p]...  9.22 us
    all_to_all x1, waiting for transfers between devices, fast_shards(): lax.all_to_all(spec, ('gx', 'gy', 'gz'), split_axis=0, concat_axis=0, til...  7.01 us
    reshape x2, local copies, waits for them, and re-layouts, field_tensor(): main = got[:, :6 * 4 * 2 * 8].reshape(2, 6, 2, 2, 2, 8, kzs // 32, 32)  6.21 us
    all_to_all x1, starting transfers between devices, fast_shards(): lax.all_to_all(spec, ('gx', 'gy', 'gz'), split_axis=0, concat_axis=0, til...  5.67 us
    ppermute x1, starting transfers between devices, field_tensor(): other = lax.ppermute(other, 'gy', [(0, 1), (1, 0)])  3.06 us
  transfers between devices with their start and end apart: 16, of which 8 were waited for; matrix products, arithmetic and copies ran while one was open for 18% of the time, Pallas kernels for 2%

profile of v5, /device:TPU:0, one launch (start us, length us, event | category | flops | bytes accessed | tf_op | source)
XLA Modules:
  0.0 97.5 jit_solution(17625299945338090813)
XLA Ops:
  0.6 1.5 %shard_map.131 = (f32[16,1536]{1,0:T(8,128)S(1)}, f32[16,1536]{1,0:T(8,128)S(1)}, f32[16,1536]{1,0:T(8,128)S(1)}, f32[16,1536]{1,0:T(8,128)S(1)}, f32[16,1536]{1...) custom-call(f32[12,128,128]{2,1,0:T(8,128)} %bitcast.28), custom_call_target="tpu_custom_call" | custom-call | tf_op jit(solution)/shard_map/pallas_call | solution.py:728
  2.2 1.4 %shard_map.133 = (f32[392,256]{1,0:T(8,128)S(1)}, f32[392,256]{1,0:T(8,128)S(1)}) custom-call(f32[6,4,64,256]{3,2,1,0:T(8,128)} %bitcast.32), custom_call_target="tpu_custom_call" | custom-call | tf_op jit(solution)/shard_map/pallas_call | solution.py:728
  3.6 3.1 %collective-permute-start.7 = (f32[392,256]{1,0:T(8,128)S(1)}, f32[392,256]{1,0:T(8,128)}, u32[]{:S(2)}, u32[]{:S(2)}) collective-permute-start(f32[392,256]{1,0:T(8,128)S(1)} %get-tuple-element.37), channel_id=1, source_target_pairs={{0,4},{4,0},{1,5},{5,1},{2,6},{6,2},{3,7},{7,3},{8,12},{12,8},{9,1... | collective-permute-start | bytes 1204232 | tf_op jit(solution)/shard_map/ppermute | solution.py:675
  6.6 0.1 collective-permute-start
  6.7 2.1 %collective-permute-start.2 = (f32[16,1536]{1,0:T(8,128)S(1)}, f32[16,1536]{1,0:T(8,128)S(1)}, u32[]{:S(2)}, u32[]{:S(2)}) collective-permute-start(f32[16,1536]{1,0:T(8,128)S(1)} %get-tuple-element.29), channel_id=1, source_target_pairs={{0,12},{4,8},{8,4},{12,0},{16,28},{20,24},{24,20},{28,16},{1,13},{... | collective-permute-start | bytes 294920 | tf_op jit(solution)/shard_map/ppermute | solution.py:745
  8.8 1.5 %collective-permute-start.3 = (f32[16,1536]{1,0:T(8,128)S(1)}, f32[16,1536]{1,0:T(8,128)S(1)}, u32[]{:S(2)}, u32[]{:S(2)}) collective-permute-start(f32[16,1536]{1,0:T(8,128)S(1)} %get-tuple-element.30), channel_id=1, source_target_pairs={{0,16},{4,20},{8,24},{12,28},{16,0},{20,4},{24,8},{28,12},{1,17},{... | collective-permute-start | bytes 294920 | tf_op jit(solution)/shard_map/ppermute | solution.py:745
  10.4 0.1 and.84
  10.5 0.1 add.126
  10.7 0.7 broadcast_select_fusion.4
  11.4 0.1 add_add_fusion
  11.5 0.1 add.129
  11.6 0.1 add.130
  11.8 0.7 broadcast_add_fusion
  12.5 1.1 %broadcast_select_fusion = (bf16[2,256,512]{2,1,0:T(8,128)(2,1)S(1)}, bf16[2,256,512]{2,1,0:T(8,128)(2,1)S(1)}) fusion(bf16[2,256,512]{2,1,0:T(8,128)(2,1)} %constant.81.clone, pred[]{:T(512)S(6)} %gt.16, bf16[2,256,512]{2,1,0:T(8,128)(2,1)S(1)} %copy-done.4), kind=kLoop, calls=%fused_computation.2 | loop fusion | flops 524288 | bytes 2097153 | tf_op jit(solution)/shard_map/jit(_where)/select_n | solution.py:751
  13.6 5.3 %collective-permute-done.a_1_ = f32[16,1536]{1,0:T(8,128)S(1)} collective-permute-done((f32[16,1536]{1,0:T(8,128)S(1)}, f32[16,1536]{1,0:T(8,128)S(1)}, u32[]{:S(2)}, u32[]{:S(2)}) %collective-permute-start) | collective-permute-done | bytes 98336 | tf_op jit(solution)/shard_map/ppermute | solution.py:745
  18.9 2.9 %collective-permute-start.4 = (f32[16,1536]{1,0:T(8,128)S(1)}, f32[16,1536]{1,0:T(8,128)S(1)}, u32[]{:S(2)}, u32[]{:S(2)}) collective-permute-start(f32[16,1536]{1,0:T(8,128)S(1)} %get-tuple-element.31), channel_id=1, source_target_pairs={{0,20},{4,16},{8,28},{12,24},{16,4},{20,0},{24,12},{28,8},{1,21},{... | collective-permute-start | bytes 294920 | tf_op jit(solution)/shard_map/ppermute | solution.py:745
  21.8 1.7 %collective-permute-start.6 = (f32[16,1536]{1,0:T(8,128)S(1)}, f32[16,1536]{1,0:T(8,128)S(1)}, u32[]{:S(2)}, u32[]{:S(2)}) collective-permute-start(f32[16,1536]{1,0:T(8,128)S(1)} %get-tuple-element.33), channel_id=1, source_target_pairs={{0,28},{4,24},{8,20},{12,16},{16,12},{20,8},{24,4},{28,0},{1,29},{... | collective-permute-start | bytes 294920 | tf_op jit(solution)/shard_map/ppermute | solution.py:745
  23.5 0.7 and_select_fusion.a_3_
  24.3 0.7 collective-permute-done.4.a_5_
  24.9 2.1 %collective-permute-done.5.a_6_ = f32[16,1536]{1,0:T(8,128)S(1)} collective-permute-done((f32[16,1536]{1,0:T(8,128)S(1)}, f32[16,1536]{1,0:T(8,128)S(1)}, u32[]{:S(2)}, u32[]{:S(2)}) %collective-permute-start.5) | collective-permute-done | bytes 98336 | tf_op jit(solution)/shard_map/ppermute | solution.py:745
  27.0 1.6 %collective-permute-done.6.a_7_ = f32[16,1536]{1,0:T(8,128)S(1)} collective-permute-done((f32[16,1536]{1,0:T(8,128)S(1)}, f32[16,1536]{1,0:T(8,128)S(1)}, u32[]{:S(2)}, u32[]{:S(2)}) %collective-permute-start.6) | collective-permute-done | bytes 98336 | tf_op jit(solution)/shard_map/ppermute | solution.py:745
  28.6 2.0 %shard_map.132 = f32[32,6,8,128]{3,2,1,0:T(8,128)} custom-call(f32[16,1536]{1,0:T(8,128)S(1)} %get-tuple-element.26.a_0_, f32[16,1536]{1,0:T(8,128)S(1)} %collective-permute-done.a_1_, f32[16,1536]{1,0:T(8,128)S(1)} %collective-permute-done.1.a_2_, f32[16,1536]{1,0:T(8,128)S(1)} %collective-permute-done.2.a_3_, f32[16,1536]{1,0:T(8,128)S(1)} %collective-permute-done.3.a_4_, ...), custom_call_target="tpu_custom_call" | custom-call | tf_op jit(solution)/shard_map/pallas_call | solution.py:728
  30.6 5.7 %all-to-all-start = ((f32[32,6,8,128]{3,2,1,0:T(8,128)}), f32[32,6,8,128]{3,2,1,0:T(8,128)S(1)}, u32[]{:S(2)}, u32[]{:S(2)}) async-start(f32[32,6,8,128]{3,2,1,0:T(8,128)} %shard_map.132), calls=%async_computation | async-start | bytes 1572864 | tf_op jit(solution)/shard_map/all_to_all | solution.py:795
  36.3 1.2 %maximum_select_fusion = f32[2,392,256]{2,1,0:T(8,128)S(1)} fusion(f32[1,392,256]{2,1,0:T(8,128)} %bitcast.5, f32[1,392,256]{2,1,0:T(8,128)S(1)} %bitcast.30, pred[]{:T(512)S(6)} %eq.37), kind=kLoop, calls=%fused_computation | loop fusion | flops 602112 | bytes 1605633 | tf_op jit(solution)/shard_map/jit(_where)/select_n | solution.py:677
  37.6 0.1 reshape.218
  37.7 0.1 fusion
  37.8 0.8 copy.26
  38.6 2.4 %reshape.216 = f32[2,6,2,2,2,8,8,32]{7,6,5,4,3,2,1,0:T(8,128)} reshape(f32[2,384,256]{2,1,0:T(8,128)S(1)} %slice.34) | data formatting | bytes 1572864 | tf_op jit(solution)/shard_map/reshape | solution.py:678
  41.0 3.9 %copy.23 = f32[2,6,2,2,2,8,8,32]{7,6,0,5,2,4,3,1:T(8,128)} copy(f32[2,6,2,2,2,8,8,32]{7,6,5,4,3,2,1,0:T(8,128)} %reshape.216) | data formatting | bytes 1572864 | tf_op jit(solution)/shard_map/reshape | solution.py:678
  44.8 2.4 %copy.24 = f32[6,32,8,128]{3,2,1,0:T(8,128)S(1)} copy(f32[6,32,8,128]{1,3,2,0:T(8,128)} %bitcast.31) | data formatting | bytes 1572864 | tf_op jit(solution)/shard_map/reshape | solution.py:679
  47.3 0.1 subtract_multiply_fusion.a_1_
  47.4 0.5 slice.40
  47.9 1.0 %pad.4.a_2_ = f32[3,32,8,128]{3,2,1,0:T(8,128)S(1)} pad(f32[3,32,3,16]{3,2,1,0:T(4,128)} %bitcast.33, f32[]{:T(128)} %constant.28.clone.1), padding=0_0x0_0x0_5x0_112 | pad | bytes 411652 | tf_op jit(solution)/shard_map/jit(_pad)/pad | solution.py:705
  49.5 1.1 %broadcast_select_fusion.2 = (bf16[512,256]{1,0:T(8,128)(2,1)S(1)}, bf16[512,256]{1,0:T(8,128)(2,1)S(1)}) fusion(bf16[512,256]{1,0:T(8,128)(2,1)} %constant.86.clone, pred[]{:T(512)} %bitcast.14, bf16[512,256]{1,0:T(8,128)(2,1)} %constant.85.clone), kind=kLoop, calls=%fused_computation.4 | loop fusion | flops 262144 | bytes 1048577 | tf_op jit(solution)/shard_map/jit(_where)/select_n | solution.py:751
  50.6 7.0 %all-to-all-done.a_0_ = f32[32,6,8,128]{3,2,1,0:T(8,128)S(1)} async-done(((f32[32,6,8,128]{3,2,1,0:T(8,128)}), f32[32,6,8,128]{3,2,1,0:T(8,128)S(1)}, u32[]{:S(2)}, u32[]{:S(2)}) %all-to-all-start) | async-done | bytes 786464 | tf_op jit(solution)/shard_map/all_to_all | solution.py:795
  57.6 1.6 %shard_map.134 = f32[32,6,8,128]{3,2,1,0:T(8,128)S(1)} custom-call(f32[32,6,8,128]{3,2,1,0:T(8,128)S(1)} %all-to-all-done.a_0_, f32[6,32,8,128]{3,2,1,0:T(8,128)S(1)} %subtract_multiply_fusion.a_1_, f32[3,32,8,128]{3,2,1,0:T(8,128)S(1)} %pad.4.a_2_, f32[8,128]{1,0:T(8,128)S(1)} %and_select_fusion.a_3_, bf16[512,256]{1,0:T(8,128)(2,1)S(1)} %get-tuple-element.57.a_4_, ...), custom_call_target="tpu_custom_call" | custom-call | tf_op jit(solution)/shard_map/pallas_call | solution.py:728
  59.2 23.2 %all_to_all.10.a_0_ = f32[32,6,8,128]{3,2,1,0:T(8,128)S(1)} all-to-all(f32[32,6,8,128]{3,2,1,0:T(8,128)S(1)} %shard_map.134), channel_id=1, replica_groups=mesh['gx'=4,'gy'=2,'gz'=4] {'gx','gy','gz'}, dimensions={0} | all-to-all | bytes 1572864 | tf_op jit(solution)/shard_map/all_to_all | solution.py:806
  82.4 0.8 shard_map.135
  83.2 0.8 collective-permute-start.10
  84.0 0.7 collective-permute-start.11
  84.7 1.6 %collective-permute-start.12 = (f32[16,1536]{1,0:T(8,128)S(1)}, f32[16,1536]{1,0:T(8,128)S(1)}, u32[]{:S(2)}, u32[]{:S(2)}) collective-permute-start(f32[16,1536]{1,0:T(8,128)S(1)} %get-tuple-element.43), channel_id=1, source_target_pairs={{0,20},{4,16},{8,28},{12,24},{16,4},{20,0},{24,12},{28,8},{1,21},{... | collective-permute-start | bytes 294920 | tf_op jit(solution)/shard_map/ppermute | solution.py:745
  86.2 1.0 %collective-permute-start.13 = (f32[16,1536]{1,0:T(8,128)S(1)}, f32[16,1536]{1,0:T(8,128)S(1)}, u32[]{:S(2)}, u32[]{:S(2)}) collective-permute-start(f32[16,1536]{1,0:T(8,128)S(1)} %get-tuple-element.44), channel_id=1, source_target_pairs={{0,24},{4,28},{8,16},{12,20},{16,8},{20,12},{24,0},{28,4},{1,25},{... | collective-permute-start | bytes 294920 | tf_op jit(solution)/shard_map/ppermute | solution.py:745
  87.2 1.4 %collective-permute-start.14 = (f32[16,1536]{1,0:T(8,128)S(1)}, f32[16,1536]{1,0:T(8,128)S(1)}, u32[]{:S(2)}, u32[]{:S(2)}) collective-permute-start(f32[16,1536]{1,0:T(8,128)S(1)} %get-tuple-element.45), channel_id=1, source_target_pairs={{0,28},{4,24},{8,20},{12,16},{16,12},{20,8},{24,4},{28,0},{1,29},{... | collective-permute-start | bytes 294920 | tf_op jit(solution)/shard_map/ppermute | solution.py:745
  88.7 0.8 collective-permute-start.8
  89.5 2.5 %collective-permute-done.12.a_5_ = f32[16,1536]{1,0:T(8,128)S(1)} collective-permute-done((f32[16,1536]{1,0:T(8,128)S(1)}, f32[16,1536]{1,0:T(8,128)S(1)}, u32[]{:S(2)}, u32[]{:S(2)}) %collective-permute-start.12) | collective-permute-done | bytes 98336 | tf_op jit(solution)/shard_map/ppermute | solution.py:745
  92.0 0.7 collective-permute-done.13.a_6_
  92.7 2.8 %collective-permute-done.14.a_7_ = f32[16,1536]{1,0:T(8,128)S(1)} collective-permute-done((f32[16,1536]{1,0:T(8,128)S(1)}, f32[16,1536]{1,0:T(8,128)S(1)}, u32[]{:S(2)}, u32[]{:S(2)}) %collective-permute-start.14) | collective-permute-done | bytes 98336 | tf_op jit(solution)/shard_map/ppermute | solution.py:745
  95.5 2.0 %shard_map.136 = (f32[3,4,128,128]{3,2,1,0:T(8,128)}, f32[3,4,128,128]{3,2,1,0:T(8,128)}) custom-call(f32[16,1536]{1,0:T(8,128)S(1)} %get-tuple-element.38.a_0_, f32[16,1536]{1,0:T(8,128)S(1)} %collective-permute-done.8.a_1_, f32[16,1536]{1,0:T(8,128)S(1)} %collective-permute-done.9.a_2_, f32[16,1536]{1,0:T(8,128)S(1)} %collective-permute-done.10.a_3_, ...), custom_call_target="tpu_custom_call" | custom-call | tf_op jit(solution)/shard_map/pallas_call | solution.py:728
  (49 shorter events, 0.5 us)
Async XLA Ops:
  0.6 11.8 %copy-start.4 = (bf16[2,256,512]{2,1,0:T(8,128)(2,1)S(1)}, bf16[2,256,512]{2,1,0:T(8,128)(2,1)}, u32[]{:S(2)}) copy-start(bf16[2,256,512]{2,1,0:T(8,128)(2,1)} %constant.80.clone) | copy-start | bytes 1572868
  3.6 32.7 %collective-permute-start.7 = (f32[392,256]{1,0:T(8,128)S(1)}, f32[392,256]{1,0:T(8,128)}, u32[]{:S(2)}, u32[]{:S(2)}) collective-permute-start(f32[392,256]{1,0:T(8,128)S(1)} %get-tuple-element.37), channel_id=1, source_target_pairs={{0,4},{4,0},{1,5},{5,1},{2,6},{6,2},{3,7},{7,3},{8,12},{12,8},{9,1... | collective-permute-start | bytes 1204232 | tf_op jit(solution)/shard_map/ppermute | solution.py:675
  6.6 12.2 %collective-permute-start = (f32[16,1536]{1,0:T(8,128)S(1)}, f32[16,1536]{1,0:T(8,128)S(1)}, u32[]{:S(2)}, u32[]{:S(2)}) collective-permute-start(f32[16,1536]{1,0:T(8,128)S(1)} %get-tuple-element.27), channel_id=1, source_target_pairs={{0,4},{4,0},{8,12},{12,8},{16,20},{20,16},{24,28},{28,24},{1,5},{5... | collective-permute-start | bytes 294920 | tf_op jit(solution)/shard_map/ppermute | solution.py:745
  6.7 15.1 %collective-permute-start.1 = (f32[16,1536]{1,0:T(8,128)S(1)}, f32[16,1536]{1,0:T(8,128)S(1)}, u32[]{:S(2)}, u32[]{:S(2)}) collective-permute-start(f32[16,1536]{1,0:T(8,128)S(1)} %get-tuple-element.28), channel_id=1, source_target_pairs={{0,8},{4,12},{8,0},{12,4},{16,24},{20,28},{24,16},{28,20},{1,9},{5... | collective-permute-start | bytes 294920 | tf_op jit(solution)/shard_map/ppermute | solution.py:745
  6.7 15.1 %collective-permute-start.2 = (f32[16,1536]{1,0:T(8,128)S(1)}, f32[16,1536]{1,0:T(8,128)S(1)}, u32[]{:S(2)}, u32[]{:S(2)}) collective-permute-start(f32[16,1536]{1,0:T(8,128)S(1)} %get-tuple-element.29), channel_id=1, source_target_pairs={{0,12},{4,8},{8,4},{12,0},{16,28},{20,24},{24,20},{28,16},{1,13},{... | collective-permute-start | bytes 294920 | tf_op jit(solution)/shard_map/ppermute | solution.py:745
  8.8 15.5 %collective-permute-start.3 = (f32[16,1536]{1,0:T(8,128)S(1)}, f32[16,1536]{1,0:T(8,128)S(1)}, u32[]{:S(2)}, u32[]{:S(2)}) collective-permute-start(f32[16,1536]{1,0:T(8,128)S(1)} %get-tuple-element.30), channel_id=1, source_target_pairs={{0,16},{4,20},{8,24},{12,28},{16,0},{20,4},{24,8},{28,12},{1,17},{... | collective-permute-start | bytes 294920 | tf_op jit(solution)/shard_map/ppermute | solution.py:745
  10.3 1.3 %copy-start.7 = (pred[8]{0:T(512)(128)(4,1)}, pred[8]{0:T(512)(128)(4,1)S(1)}, u32[]{:S(2)}) copy-start(pred[8]{0:T(512)(128)(4,1)S(1)} %iota_compare_fusion.1) | copy-start | bytes 28
  18.9 6.1 %collective-permute-start.4 = (f32[16,1536]{1,0:T(8,128)S(1)}, f32[16,1536]{1,0:T(8,128)S(1)}, u32[]{:S(2)}, u32[]{:S(2)}) collective-permute-start(f32[16,1536]{1,0:T(8,128)S(1)} %get-tuple-element.31), channel_id=1, source_target_pairs={{0,20},{4,16},{8,28},{12,24},{16,4},{20,0},{24,12},{28,8},{1,21},{... | collective-permute-start | bytes 294920 | tf_op jit(solution)/shard_map/ppermute | solution.py:745
  21.8 5.3 %collective-permute-start.5 = (f32[16,1536]{1,0:T(8,128)S(1)}, f32[16,1536]{1,0:T(8,128)S(1)}, u32[]{:S(2)}, u32[]{:S(2)}) collective-permute-start(f32[16,1536]{1,0:T(8,128)S(1)} %get-tuple-element.32), channel_id=1, source_target_pairs={{0,24},{4,28},{8,16},{12,20},{16,8},{20,12},{24,0},{28,4},{1,25},{... | collective-permute-start | bytes 294920 | tf_op jit(solution)/shard_map/ppermute | solution.py:745
  21.8 6.8 %collective-permute-start.6 = (f32[16,1536]{1,0:T(8,128)S(1)}, f32[16,1536]{1,0:T(8,128)S(1)}, u32[]{:S(2)}, u32[]{:S(2)}) collective-permute-start(f32[16,1536]{1,0:T(8,128)S(1)} %get-tuple-element.33), channel_id=1, source_target_pairs={{0,28},{4,24},{8,20},{12,16},{16,12},{20,8},{24,4},{28,0},{1,29},{... | collective-permute-start | bytes 294920 | tf_op jit(solution)/shard_map/ppermute | solution.py:745
  28.6 9.1 %copy-start.6 = (f32[6]{0:T(128)S(1)}, f32[6]{0:T(128)}, u32[]{:S(2)}) copy-start(f32[6]{0:T(128)} %constant.84.clone) | copy-start | bytes 76
  30.6 27.0 %all-to-all-start = ((f32[32,6,8,128]{3,2,1,0:T(8,128)}), f32[32,6,8,128]{3,2,1,0:T(8,128)S(1)}, u32[]{:S(2)}, u32[]{:S(2)}) async-start(f32[32,6,8,128]{3,2,1,0:T(8,128)} %shard_map.132), calls=%async_computation | async-start | bytes 1572864 | tf_op jit(solution)/shard_map/all_to_all | solution.py:795
  44.8 2.4 %copy-start.5 = (f32[32,8,128]{2,1,0:T(8,128)S(1)}, f32[32,8,128]{2,1,0:T(8,128)}, u32[]{:S(2)}) copy-start(f32[32,8,128]{2,1,0:T(8,128)} %broadcast_add_fusion) | copy-start | bytes 393220
  47.9 34.5 %copy-start.1 = (bf16[2,512,256]{2,1,0:T(8,128)(2,1)S(1)}, bf16[2,512,256]{2,1,0:T(8,128)(2,1)}, u32[]{:S(2)}) copy-start(bf16[2,512,256]{2,1,0:T(8,128)(2,1)} %constant.87.clone.a_1_) | copy-start | bytes 1572868
  47.9 34.5 %copy-start.2 = (bf16[2,512,256]{2,1,0:T(8,128)(2,1)S(1)}, bf16[2,512,256]{2,1,0:T(8,128)(2,1)}, u32[]{:S(2)}) copy-start(bf16[2,512,256]{2,1,0:T(8,128)(2,1)} %constant.88.clone.a_2_) | copy-start | bytes 1572868
  57.6 37.9 %copy-start = (f32[3,16,32,128]{3,2,1,0:T(8,128)S(1)}, f32[3,16,32,128]{3,2,1,0:T(8,128)}, u32[]{:S(2)}) copy-start(f32[3,16,32,128]{3,2,1,0:T(8,128)} %param.12) | copy-start | bytes 2359300
  57.6 37.9 %copy-start.3 = (f32[3]{0:T(128)S(1)}, f32[3]{0:T(128)}, u32[]{:S(2)}) copy-start(f32[3]{0:T(128)} %a_9_.1) | copy-start | bytes 40
  83.2 5.5 %collective-permute-start.10 = (f32[16,1536]{1,0:T(8,128)S(1)}, f32[16,1536]{1,0:T(8,128)S(1)}, u32[]{:S(2)}, u32[]{:S(2)}) collective-permute-start(f32[16,1536]{1,0:T(8,128)S(1)} %get-tuple-element.41), channel_id=1, source_target_pairs={{0,12},{4,8},{8,4},{12,0},{16,28},{20,24},{24,20},{28,16},{1,13},{... | collective-permute-start | bytes 294920 | tf_op jit(solution)/shard_map/ppermute | solution.py:745
  84.0 5.5 %collective-permute-start.11 = (f32[16,1536]{1,0:T(8,128)S(1)}, f32[16,1536]{1,0:T(8,128)S(1)}, u32[]{:S(2)}, u32[]{:S(2)}) collective-permute-start(f32[16,1536]{1,0:T(8,128)S(1)} %get-tuple-element.42), channel_id=1, source_target_pairs={{0,16},{4,20},{8,24},{12,28},{16,0},{20,4},{24,8},{28,12},{1,17},{... | collective-permute-start | bytes 294920 | tf_op jit(solution)/shard_map/ppermute | solution.py:745
  84.7 7.3 %collective-permute-start.12 = (f32[16,1536]{1,0:T(8,128)S(1)}, f32[16,1536]{1,0:T(8,128)S(1)}, u32[]{:S(2)}, u32[]{:S(2)}) collective-permute-start(f32[16,1536]{1,0:T(8,128)S(1)} %get-tuple-element.43), channel_id=1, source_target_pairs={{0,20},{4,16},{8,28},{12,24},{16,4},{20,0},{24,12},{28,8},{1,21},{... | collective-permute-start | bytes 294920 | tf_op jit(solution)/shard_map/ppermute | solution.py:745
  86.2 6.4 %collective-permute-start.13 = (f32[16,1536]{1,0:T(8,128)S(1)}, f32[16,1536]{1,0:T(8,128)S(1)}, u32[]{:S(2)}, u32[]{:S(2)}) collective-permute-start(f32[16,1536]{1,0:T(8,128)S(1)} %get-tuple-element.44), channel_id=1, source_target_pairs={{0,24},{4,28},{8,16},{12,20},{16,8},{20,12},{24,0},{28,4},{1,25},{... | collective-permute-start | bytes 294920 | tf_op jit(solution)/shard_map/ppermute | solution.py:745
  87.2 8.2 %collective-permute-start.14 = (f32[16,1536]{1,0:T(8,128)S(1)}, f32[16,1536]{1,0:T(8,128)S(1)}, u32[]{:S(2)}, u32[]{:S(2)}) collective-permute-start(f32[16,1536]{1,0:T(8,128)S(1)} %get-tuple-element.45), channel_id=1, source_target_pairs={{0,28},{4,24},{8,20},{12,16},{16,12},{20,8},{24,4},{28,0},{1,29},{... | collective-permute-start | bytes 294920 | tf_op jit(solution)/shard_map/ppermute | solution.py:745
  88.7 6.8 %collective-permute-start.8 = (f32[16,1536]{1,0:T(8,128)S(1)}, f32[16,1536]{1,0:T(8,128)S(1)}, u32[]{:S(2)}, u32[]{:S(2)}) collective-permute-start(f32[16,1536]{1,0:T(8,128)S(1)} %get-tuple-element.39), channel_id=1, source_target_pairs={{0,4},{4,0},{8,12},{12,8},{16,20},{20,16},{24,28},{28,24},{1,5},{5... | collective-permute-start | bytes 294920 | tf_op jit(solution)/shard_map/ppermute | solution.py:745
  89.5 6.0 %collective-permute-start.9 = (f32[16,1536]{1,0:T(8,128)S(1)}, f32[16,1536]{1,0:T(8,128)S(1)}, u32[]{:S(2)}, u32[]{:S(2)}) collective-permute-start(f32[16,1536]{1,0:T(8,128)S(1)} %get-tuple-element.40), channel_id=1, source_target_pairs={{0,8},{4,12},{8,0},{12,4},{16,24},{20,28},{24,16},{28,20},{1,9},{5... | collective-permute-start | bytes 294920 | tf_op jit(solution)/shard_map/ppermute | solution.py:745
